TPU v7x, 512 devices: a whole 4x8x8 slice. The times are simulated.
512 devices in a mesh: inter: 64 (over y, z_hi, core), intra: 8 (over x, z_lo).
Axes of the slice: x: 4, y: 8, z: 8 (z_hi: 4, z_lo: 2; z = z_hi * 2 + z_lo), core: 2. Of those that a mesh axis runs over, the one named last changes fastest.
Arguments:
- hidden_in: bfloat16 [64, 1024, 4096], P('inter', 'intra'), may hold values from -120 to 120, as said below
- norm_gain: bfloat16 [4096], P(('inter', 'intra')), may hold values from 0.5 to 2, as said below
- qkv_weight: bfloat16 [4096, 768], P(('inter', 'intra')), may hold values from -0.09375 to 0.09375
- attn_cotangent: bfloat16 [64, 1024, 512], P('inter', 'intra'), may hold values from -6 to 6
Outputs:
- attn: bfloat16 [64, 1024, 512], P('inter', 'intra')
- grad_in: bfloat16 [64, 1024, 4096], P('inter', 'intra')
- weight_grad: float32 [4096, 768], P(('intra', 'inter'))
- gain_grad: float32 [4096], P(('intra', 'inter'))
Inputs may be any that keep to these rules, and one draw needn't show every extreme that they name: `hidden_in`: activations with spread row and feature scales. `norm_gain`: positive gains.
All inputs are finite; a program needn't handle non-finite values.
Results may differ from a plain program's by a relative error of at most 0.015.
Values may be sent and summed in bfloat16 or wider, within the bound.
A program may use at most 64 MiB of HBM per device.

v0:
```python
import math

import jax
import jax.numpy as jnp
from jax import lax
from jax.sharding import PartitionSpec as P

HD = 128
HEADS = 4


eps_norm = 1e-05
rope_base = 500000.0


def sent_together(arrays, axis, dim, along):
    widths = [math.prod(a.shape[along:]) for a in arrays]
    both = jnp.concatenate(
        [a.reshape(*a.shape[:along], w) for a, w in zip(arrays, widths)], axis=along
    )
    filled = lax.all_gather(both, axis, axis=dim, tiled=True)
    tiles = jnp.split(filled, [sum(widths[:k]) for k in range(1, len(widths))], axis=along)
    return tuple(
        (b.reshape(*filled.shape[:along], *a.shape[along:]) for a, b in zip(arrays, tiles))
    )


def in_one_piece(arrays, axis, dim, along):
    ends, at = ([], 0)
    for a in arrays[:-1]:
        at += a.shape[along]
        ends.append(at)
    both = jnp.concatenate(arrays, axis=along)
    return tuple(jnp.split(lax.all_gather(both, axis, axis=dim, tiled=True), ends, axis=along))


def gather_turned(arrays, axis, dims):
    turned = [jnp.moveaxis(a, dim, 0) for a, dim in zip(arrays, dims)]
    both = jnp.concatenate([t.reshape(len(t), -1) for t in turned], axis=1)
    filled, at, outs = (lax.all_gather(both, axis, axis=0, tiled=True), 0, [])
    for t, dim in zip(turned, dims):
        section = filled[:, at : at + t[0].size].reshape(-1, *t.shape[1:])
        outs.append(jnp.moveaxis(section, 0, dim))
        at += t[0].size
    return tuple(outs)


def in_order(tiles, dim):
    tiles = jnp.moveaxis(tiles, 0, dim)
    dims = tiles.shape
    return tiles.reshape(*dims[:dim], dims[dim] * dims[dim + 1], *dims[dim + 2 :])


def from_everyone(x, axis):
    copies = jnp.broadcast_to(x, (lax.axis_size(axis), *x.shape))
    return lax.all_to_all(copies, axis, split_axis=0, concat_axis=0, tiled=True)


def gather_directly(x, axis, dim):
    return in_order(from_everyone(x, axis), dim)


def split_up(x, dim, size):
    dims = x.shape
    tiles = x.reshape(*dims[:dim], size, dims[dim] // size, *dims[dim + 1 :])
    return jnp.moveaxis(tiles, dim, 0)


def summed_on_arrival(x, axis, dim):
    tiles = split_up(x, dim, lax.axis_size(axis))
    arrived = lax.all_to_all(tiles, axis, split_axis=0, concat_axis=0, tiled=True)
    return arrived.sum(axis=0)


def summed_on_arrival_2(x, axis, dim):
    size = lax.axis_size(axis)
    tiles = lax.all_to_all(split_up(x, dim, size), axis, 0, 0, tiled=True)
    return jnp.sum(tiles.astype(jnp.float32), axis=0)


def side_by_side(arrays, axis, dim, along):
    columns = [a.reshape(*a.shape[:along], -1) for a in arrays]
    both = jnp.concatenate(columns, axis=along)
    filled, at, outs = (summed_on_arrival_2(both, axis, dim), 0, [])
    for a, column in zip(arrays, columns):
        section = filled[..., at : at + column.shape[along]]
        outs.append(section.reshape(*section.shape[:along], *a.shape[along:]))
        at += column.shape[along]
    return tuple(outs)


def rope_tables(positions, head_size):
    half_size = head_size // 2
    freqs = rope_base ** (-jnp.arange(half_size, dtype=jnp.float32) / half_size)
    angles = positions.astype(jnp.float32)[:, None] * freqs[None, :]
    return (jnp.cos(angles), jnp.sin(angles))


def rotate(values_in, cosine, sine):
    half_size = values_in.shape[-1] // 2
    first, second = (values_in[..., :half_size], values_in[..., half_size:])
    return jnp.concatenate(
        [first * cosine - second * sine, second * cosine + first * sine], axis=-1
    )


def unrotate(grad_out, cosine, sine):
    half_size = grad_out.shape[-1] // 2
    first, second = (grad_out[..., :half_size], grad_out[..., half_size:])
    return jnp.concatenate(
        [first * cosine + second * sine, second * cosine - first * sine], axis=-1
    )


def forward_fold(query_rows, row_pos):

    def forward_advance(carry, piece, start):
        row_top, row_total, weighted = carry
        key_part, value_part = piece
        scores = jnp.einsum("qd,kd->qk", query_rows, key_part, preferred_element_type=jnp.float32)
        key_pos = start + jnp.arange(key_part.shape[0], dtype=jnp.int32)
        allowed = key_pos[None, :] <= row_pos[:, None]
        scores = jnp.where(allowed, scores, -1e30)
        new_top = jnp.maximum(row_top, jnp.max(scores, axis=1))
        numbers = jnp.where(allowed, jnp.exp(scores - new_top[:, None]), 0.0)
        row_total = jnp.sum(numbers, axis=1)
        weighted = jnp.dot(
            numbers,
            value_part.astype(jnp.float32),
            precision=lax.Precision.HIGHEST,
            preferred_element_type=jnp.float32,
        )
        return (new_top, row_total, weighted)

    return forward_advance


def query_grad_fold(query_rows, row_pos, grad_flat, log_total, row_delta):

    def query_advance(grad_query, piece, start):
        key_part, value_part = piece
        scores = jnp.einsum("qd,kd->qk", query_rows, key_part, preferred_element_type=jnp.float32)
        key_pos = start + jnp.arange(key_part.shape[0], dtype=jnp.int32)
        allowed = key_pos[None, :] <= row_pos[:, None]
        probs = jnp.where(
            allowed, jnp.exp(jnp.where(allowed, scores, -1e30) - log_total[:, None]), 0.0
        )
        grad_probs = jnp.einsum(
            "qd,kd->qk", grad_flat, value_part, preferred_element_type=jnp.float32
        )
        grad_scores = (probs * (grad_probs - row_delta[:, None])).astype(jnp.bfloat16)
        return jnp.dot(grad_scores, key_part, preferred_element_type=jnp.float32)

    return query_advance


def key_grad_fold(key_rows, value_rows, key_pos, log_all, delta_all, heads_count):

    def key_advance(carry, piece, start):
        query_part, attn_grad_part = piece
        count = query_part.shape[0]
        scores = jnp.einsum("qd,kd->qk", query_part, key_rows, preferred_element_type=jnp.float32)
        query_pos = jnp.arange(count, dtype=jnp.int32) // heads_count
        allowed = key_pos[None, :] <= query_pos[:, None]
        probs = jnp.where(
            allowed, jnp.exp(jnp.where(allowed, scores, -1e30) - log_all[:, None]), 0.0
        )
        grad_values = jnp.einsum(
            "qk,qd->kd",
            probs.astype(jnp.bfloat16),
            attn_grad_part,
            preferred_element_type=jnp.float32,
        )
        grad_probs = jnp.einsum(
            "qd,kd->qk", attn_grad_part, value_rows, preferred_element_type=jnp.float32
        )
        grad_scores = (probs * (grad_probs - delta_all[:, None])).astype(jnp.bfloat16)
        grad_keys = jnp.einsum(
            "qk,qd->kd", grad_scores, query_part, preferred_element_type=jnp.float32
        )
        return (grad_keys, grad_values)

    return key_advance


def local(hidden_in, norm_gain, qkv_weight, attn_cotangent):
    rows_in = hidden_in[0]
    grad_attn = attn_cotangent[0]
    tokens_here = rows_in.shape[0]
    width = rows_in.shape[1]
    head_size = HD
    heads_count = HEADS
    qcols = heads_count * head_size
    scale = head_size ** (-0.5)
    weight_group, gain_group = sent_together((qkv_weight, norm_gain), "intra", 0, 1)
    weight_full, gain_full = sent_together((weight_group, gain_group), "inter", 0, 1)
    query_pos = lax.axis_index("intra") * tokens_here + jnp.arange(tokens_here, dtype=jnp.int32)
    row_pos = jnp.broadcast_to(query_pos[:, None], (tokens_here, heads_count)).reshape(
        tokens_here * heads_count
    )
    cosine, sine = rope_tables(query_pos, head_size)
    wide_rows = rows_in.astype(jnp.float32)
    inv_rms = lax.rsqrt(jnp.mean(wide_rows * wide_rows, axis=1, keepdims=True) + eps_norm)
    normed = (wide_rows * inv_rms * gain_full.astype(jnp.float32)[None, :]).astype(jnp.bfloat16)
    mixed = jnp.dot(normed, weight_full, preferred_element_type=jnp.float32)
    query_rows = (
        (
            rotate(
                mixed[:, :qcols].reshape(tokens_here, heads_count, head_size),
                cosine[:, None, :],
                sine[:, None, :],
            )
            * scale
        )
        .astype(jnp.bfloat16)
        .reshape(tokens_here * heads_count, head_size)
    )
    key_rows = rotate(mixed[:, qcols : qcols + head_size], cosine, sine).astype(jnp.bfloat16)
    value_rows = mixed[:, qcols + head_size :].astype(jnp.bfloat16)
    grad_flat = grad_attn.reshape(tokens_here * heads_count, head_size)
    flat_rows = tokens_here * heads_count
    forward_step = forward_fold(query_rows, row_pos)
    start_carry = (
        jnp.full((flat_rows,), -1e30, jnp.float32),
        jnp.zeros((flat_rows,), jnp.float32),
        jnp.zeros((flat_rows, head_size), jnp.float32),
    )
    key_all, value_all = in_one_piece((key_rows, value_rows), "intra", 0, 1)
    row_top, row_total, weighted = forward_step(start_carry, (key_all, value_all), 0)
    attn_flat = (weighted / row_total[:, None]).astype(jnp.bfloat16)
    log_total = row_top + jnp.log(row_total)
    row_delta = jnp.sum(grad_flat.astype(jnp.float32) * attn_flat.astype(jnp.float32), axis=1)
    query_step = query_grad_fold(query_rows, row_pos, grad_flat, log_total, row_delta)
    grad_query = query_step(jnp.zeros((flat_rows, head_size), jnp.float32), (key_all, value_all), 0)
    log_all, delta_all = gather_turned((log_total, row_delta), "intra", (0, 0))
    key_step = key_grad_fold(key_rows, value_rows, query_pos, log_all, delta_all, heads_count)
    grad_keys, grad_values = key_step(
        (
            jnp.zeros((tokens_here, head_size), jnp.float32),
            jnp.zeros((tokens_here, head_size), jnp.float32),
        ),
        in_one_piece((query_rows, grad_flat), "intra", 0, 1),
        jnp.int32(0),
    )
    query_back = (
        unrotate(
            grad_query.reshape(tokens_here, heads_count, head_size),
            cosine[:, None, :],
            sine[:, None, :],
        )
        * scale
    ).reshape(tokens_here, qcols)
    grad_mixed = jnp.concatenate(
        [query_back, unrotate(grad_keys, cosine, sine), grad_values], axis=1
    ).astype(jnp.bfloat16)
    weight_back, gain_back = (weight_full, gain_full)
    gain_wide = gain_back.astype(jnp.float32)[None, :]
    grad_normed = jnp.einsum(
        "tc,dc->td", grad_mixed, weight_back, preferred_element_type=jnp.float32
    )
    inner = jnp.sum(grad_normed * gain_wide * wide_rows, axis=1, keepdims=True)
    grad_rows = (
        gain_wide * grad_normed * inv_rms - wide_rows * inv_rms**3 / width * inner
    ).astype(jnp.bfloat16)
    gain_term = jnp.sum(grad_normed * wide_rows * inv_rms, axis=0)
    normed_cols = lax.all_to_all(normed, "intra", split_axis=1, concat_axis=0, tiled=True)
    group_term = lax.dot_general(
        normed_cols,
        gather_directly(grad_mixed, "intra", 0),
        (((0,), (0,)), ((), ())),
        preferred_element_type=jnp.float32,
    )
    term_low = lax.optimization_barrier(group_term.astype(jnp.bfloat16))
    gain_sums = summed_on_arrival(gain_term, "intra", 0)
    weight_grad, gain_grad = side_by_side(
        (term_low.astype(jnp.float32).astype(jnp.bfloat16), gain_sums.astype(jnp.bfloat16)),
        "inter",
        0,
        1,
    )
    return (attn_flat.reshape(tokens_here, qcols)[None], grad_rows[None], weight_grad, gain_grad)


def solution(mesh):
    return jax.shard_map(
        local,
        mesh=mesh,
        in_specs=(
            P("inter", "intra", None),
            P(("inter", "intra")),
            P(("inter", "intra"), None),
            P("inter", "intra", None),
        ),
        out_specs=(
            P("inter", "intra", None),
            P("inter", "intra", None),
            P(("intra", "inter"), None),
            P(("intra", "inter")),
        ),
        check_vma=False,
    )
```

profile of v0, /device:TPU:1, one launch (start us, length us, event | category | flops | bytes accessed | tf_op | source)
XLA Modules:
  0.0 335.1 jit_solution(8068869801132005356)
XLA Ops:
  7.2 0.0 copy-start
  7.2 0.0 all-gather.3.cloned.1.call-start
  7.2 0.8 copy.32
  8.0 0.7 pad_maximum_fusion.4
  8.8 25.4 %all_gather.15 = bf16[64,769]{1,0:T(8,128)(2,1)} all-gather(bf16[8,769]{1,0:T(8,128)(2,1)S(1)} %pad_maximum_fusion.4), channel_id=1, replica_groups=mesh['inter'=64,'intra'=8] {'intra'}, dimensions={0}, use_global_device_ids=true | all-gather | bytes 110736 | tf_op jit(solution)/shard_map/all_gather | solution.py:21
  34.2 0.0 all-gather.3.cloned.1.call-update
  34.2 0.0 all-gather.5.cloned.1.call-start
  34.3 0.5 copy-done.23
  34.8 0.1 broadcast_in_dim.26
  34.9 0.7 le.15
  35.6 1.0 reshape_squeeze.3
  36.6 0.8 copy.34
  37.4 2.6 copy.44
  40.0 0.3 fusion.10
  40.3 0.5 multiply_multiply_fusion
  40.8 103.4 %all-gather.3.cloned.1.call-done = bf16[4096,769]{1,0:T(8,128)(2,1)} async-done(((bf16[64,769]{1,0:T(8,128)(2,1)}), bf16[4096,769]{1,0:T(8,128)(2,1)}) %all-gather.3.cloned.1.call-update) | async-done | bytes 6299664 | tf_op jit(solution)/shard_map/all_gather | solution.py:21
  144.3 1.6 convert_reduce_fusion
  145.9 3.8 %fusion.2 = f32[128,768]{1,0:T(8,128)S(1)} fusion(bf16[4096,769]{1,0:T(8,128)(2,1)} %all-gather.3.cloned.1.call-done, bf16[1,128,4096]{2,1,0:T(8,128)(2,1)S(1)} %copy-done, f32[4096]{0:T(1024)S(1)} %convert_reduce_fusion, f32[128]{0:T(128)S(1)} %get-tuple-element.19), kind=kOutput, calls=%fused_computation.2 | convolution fusion | flops 807403520 | bytes 7750144 | tf_op jit(solution)/shard_map/dot_general | solution.py:205
  149.7 0.1 reshape.199
  149.8 0.3 fusion.61
  150.2 0.3 multiply_subtract_fusion.1
  150.5 0.1 fusion.45
  150.6 0.7 pad_maximum_fusion.1
  151.4 0.0 all-gather.5.cloned.1.call-update
  151.4 0.6 add_select_fusion
  152.0 0.6 reshape.205
  152.6 0.1 pad_maximum_fusion.3
  152.7 27.3 %all_gather.17 = bf16[1024,256]{1,0:T(8,128)(2,1)S(1)} all-gather(bf16[128,256]{1,0:T(8,128)(2,1)S(1)} %pad_maximum_fusion.3), channel_id=1, replica_groups=mesh['inter'=64,'intra'=8] {'intra'}, dimensions={0}, use_global_device_ids=true | all-gather | bytes 589824 | tf_op jit(solution)/shard_map/all_gather | solution.py:34
  180.1 1.3 fusion.79
  181.3 1.3 fusion.20
  182.7 2.4 multiply_reduce_fusion
  185.2 2.6 fusion.23
  187.7 1.4 multiply_add_fusion
  189.1 0.2 fusion.46
  189.4 0.1 copy-done.1
  189.5 1.5 multiply_convert_fusion
  191.0 4.3 %all-to-all-start = ((bf16[128,8,512]{0,2,1:T(8,128)(2,1)}), bf16[128,8,512]{0,2,1:T(8,128)(2,1)}, u32[]{:S(2)}, u32[]{:S(2)}) async-start(bf16[128,8,512]{0,2,1:T(8,128)(2,1)} %multiply_convert_fusion), calls=%async_computation | async-start | bytes 2097152 | tf_op jit(solution)/shard_map/all_to_all | solution.py:266
  195.3 41.1 %all_gather.19 = f32[4096,2]{0,1:T(2,128)S(1)} all-gather(f32[512,2]{0,1:T(2,128)S(1)} %pad_maximum_fusion.5), channel_id=1, replica_groups=mesh['inter'=64,'intra'=8] {'intra'}, dimensions={0}, use_global_device_ids=true | all-gather | bytes 36864 | tf_op jit(solution)/shard_map/all_gather | solution.py:40
  236.4 0.0 all-gather.5.cloned.1.call-done
  236.5 3.3 fusion.6
  239.8 0.5 convolution_convert_fusion
  240.3 0.1 copy.38
  240.5 3.0 fusion.22
  243.5 0.3 fusion.65
  243.9 0.1 pad_maximum_fusion.2
  244.0 6.3 %fusion.18 = (f32[4096]{0:T(1024)S(1)}, f32[128]{0:T(128)S(1)}, f32[128,4096]{1,0:T(8,128)}) fusion(bf16[1,128,4096]{2,1,0:T(8,128)(2,1)S(1)} %copy-done, f32[128]{0:T(128)S(1)} %copy-done.21, f32[4096]{0:T(1024)S(1)} %convert_reduce_fusion, bf16[128,768]{1,0:T(8,128)(2,1)S(1)} %pad_maximum_fusion.2, bf16[4096,769]{1,0:T(8,128)(2,1)} %all-gather.3.cloned.1.call-done), kind=kOutput, calls=%fused_computation.26 | convolution fusion | flops 808972160 | bytes 9667584 | tf_op jit(solution)/shard_map/tc,dc->td/dot_general | solution.py:258
  250.3 0.0 all-to-all-done
  250.3 7.5 %all_to_all.32 = f32[8,1,512]{2,1,0:T(1,128)S(1)} all-to-all(f32[8,1,512]{2,1,0:T(1,128)S(1)} %bitcast.67), channel_id=1, replica_groups=mesh['inter'=64,'intra'=8] {'intra'}, dimensions={0} | all-to-all | bytes 32768 | tf_op jit(solution)/shard_map/all_to_all | solution.py:71
  257.8 1.3 broadcast_in_dim.59
  259.1 3.6 %all-to-all-start.1 = ((bf16[8,128,768]{2,1,0:T(8,128)(2,1)}), bf16[8,128,768]{2,1,0:T(8,128)(2,1)S(1)}, u32[]{:S(2)}, u32[]{:S(2)}) async-start(bf16[8,128,768]{2,1,0:T(8,128)(2,1)} %broadcast_in_dim.59), calls=%async_computation.1 | async-start | bytes 3145728 | tf_op jit(solution)/shard_map/all_to_all | solution.py:56
  262.7 0.3 convert_element_type.120
  263.0 12.8 %all-to-all-done.1 = bf16[8,128,768]{2,1,0:T(8,128)(2,1)S(1)} async-done(((bf16[8,128,768]{2,1,0:T(8,128)(2,1)}), bf16[8,128,768]{2,1,0:T(8,128)(2,1)S(1)}, u32[]{:S(2)}, u32[]{:S(2)}) %all-to-all-start.1) | async-done | bytes 1572896 | tf_op jit(solution)/shard_map/all_to_all | solution.py:56
  275.8 2.2 bitcast_convert_fusion
  278.0 0.0 copy-start.9
  278.0 0.0 copy-start.22
  278.0 1.0 pad_maximum_fusion
  279.0 21.0 %all-to-all-start.3 = ((bf16[64,8,769]{2,1,0:T(8,128)(2,1)}), bf16[64,8,769]{2,1,0:T(8,128)(2,1)S(1)}, u32[]{:S(2)}, u32[]{:S(2)}) async-start(bf16[64,8,769]{2,1,0:T(8,128)(2,1)} %pad_maximum_fusion), calls=%async_computation.3 | async-start | bytes 1835008 | tf_op jit(solution)/shard_map/all_to_all | solution.py:77
  300.0 0.1 copy.33
  300.2 0.7 broadcast_in_dim_reshape.2
  300.9 3.2 fusion.26
  304.1 22.7 %all-to-all-done.3 = bf16[64,8,769]{2,1,0:T(8,128)(2,1)S(1)} async-done(((bf16[64,8,769]{2,1,0:T(8,128)(2,1)}), bf16[64,8,769]{2,1,0:T(8,128)(2,1)S(1)}, u32[]{:S(2)}, u32[]{:S(2)}) %all-to-all-start.3) | async-done | bytes 787488 | tf_op jit(solution)/shard_map/all_to_all | solution.py:77
  326.8 0.2 convert_reduce_fusion.1
  327.0 0.6 slice.73
  327.6 0.6 slice_reduce_fusion
  (57 shorter events, 0.2 us)
Async XLA Ops:
  7.2 32.8 %copy-start = (bf16[1,128,4096]{2,1,0:T(8,128)(2,1)S(1)}, bf16[1,128,4096]{2,1,0:T(8,128)(2,1)}, u32[]{:S(2)}) copy-start(bf16[1,128,4096]{2,1,0:T(8,128)(2,1)} %param.4) | copy-start | bytes 3145732
  7.2 137.1 %all-gather.3.cloned.1.call-start = ((), (), s32[]{:S(2)}) async-start(), calls=%async_computation.4 | async-start | bytes 7454720 | tf_op jit(solution)/shard_map/all_gather | solution.py:21
  34.2 202.2 %all-gather.5.cloned.1.call-start = ((), (), s32[]{:S(2)}) async-start(), calls=%async_computation.5 | async-start | bytes 2359296 | tf_op jit(solution)/shard_map/all_gather | solution.py:34
  34.3 0.5 copy-start.23
  40.0 109.8 %copy-start.15 = (f32[128]{0:T(128)}, f32[128]{0:T(128)S(1)}, u32[]{:S(2)}) copy-start(f32[128]{0:T(128)S(1)} %fusion.77) | copy-start | bytes 1540
  40.0 109.8 %copy-start.17 = (f32[64]{0:T(128)}, f32[64]{0:T(128)S(1)}, u32[]{:S(2)}) copy-start(f32[64]{0:T(128)S(1)} %multiply_power_fusion) | copy-start | bytes 772
  40.8 108.8 %copy-start.19 = (f32[128]{0:T(128)}, f32[128]{0:T(128)S(1)}, u32[]{:S(2)}) copy-start(f32[128]{0:T(128)S(1)} %get-tuple-element.19) | copy-start | bytes 1540
  149.7 3.0 copy-start.4
  150.2 2.6 copy-start.5
  150.2 2.6 copy-start.7
  180.0 2.6 copy-start.3
  180.0 2.7 copy-start.10
  180.1 2.7 copy-start.12
  182.7 2.4 copy-start.13
  185.2 4.2 %copy-start.11 = (f32[8,512]{1,0:T(8,128)S(1)}, f32[8,512]{1,0:T(8,128)}, u32[]{:S(2)}) copy-start(f32[8,512]{1,0:T(8,128)} %reshape.205) | copy-start | bytes 49156
  187.7 1.8 copy-start.1
  187.7 1.8 copy-start.20
  189.5 46.9 %copy-start.6 = (bf16[128,64]{1,0:T(8,128)(2,1)S(1)}, bf16[128,64]{1,0:T(8,128)(2,1)}, u32[]{:S(2)}) copy-start(bf16[128,64]{1,0:T(8,128)(2,1)} %copy-done.5) | copy-start | bytes 49156
  189.5 46.9 %copy-start.8 = (bf16[128,64]{1,0:T(8,128)(2,1)S(1)}, bf16[128,64]{1,0:T(8,128)(2,1)}, u32[]{:S(2)}) copy-start(bf16[128,64]{1,0:T(8,128)(2,1)} %copy-done.7) | copy-start | bytes 49156
  189.5 47.0 %copy-start.14 = (s32[4096]{0:T(1024)S(1)}, s32[4096]{0:T(1024)}, u32[]{:S(2)}) copy-start(s32[4096]{0:T(1024)} %add_select_fusion) | copy-start | bytes 49156
  189.5 47.0 %copy-start.24 = (s32[128]{0:T(128)S(1)}, s32[128]{0:T(128)}, u32[]{:S(2)}) copy-start(s32[128]{0:T(128)} %copy-done.23) | copy-start | bytes 1540
  191.0 59.3 %all-to-all-start = ((bf16[128,8,512]{0,2,1:T(8,128)(2,1)}), bf16[128,8,512]{0,2,1:T(8,128)(2,1)}, u32[]{:S(2)}, u32[]{:S(2)}) async-start(bf16[128,8,512]{0,2,1:T(8,128)(2,1)} %multiply_convert_fusion), calls=%async_computation | async-start | bytes 2097152 | tf_op jit(solution)/shard_map/all_to_all | solution.py:266
  236.5 3.3 copy-start.2
  240.4 3.1 copy-start.16
  240.5 3.1 copy-start.18
  240.5 3.5 %copy-start.21 = (f32[128]{0:T(128)S(1)}, f32[128]{0:T(128)}, u32[]{:S(2)}) copy-start(f32[128]{0:T(128)} %copy-done.19) | copy-start | bytes 1540
  259.1 16.7 %all-to-all-start.1 = ((bf16[8,128,768]{2,1,0:T(8,128)(2,1)}), bf16[8,128,768]{2,1,0:T(8,128)(2,1)S(1)}, u32[]{:S(2)}, u32[]{:S(2)}) async-start(bf16[8,128,768]{2,1,0:T(8,128)(2,1)} %broadcast_in_dim.59), calls=%async_computation.1 | async-start | bytes 3145728 | tf_op jit(solution)/shard_map/all_to_all | solution.py:56
  278.0 22.0 %copy-start.9 = (bf16[512,128]{0,1:T(8,128)(2,1)S(1)}, bf16[512,128]{0,1:T(8,128)(2,1)}, u32[]{:S(2)}) copy-start(bf16[512,128]{0,1:T(8,128)(2,1)} %get-tuple-element.23) | copy-start | bytes 393220
  278.0 22.9 %copy-start.22 = (f32[128]{0:T(128)S(1)}, f32[128]{0:T(128)}, u32[]{:S(2)}) copy-start(f32[128]{0:T(128)} %get-tuple-element.18) | copy-start | bytes 1540
  279.0 47.8 %all-to-all-start.3 = ((bf16[64,8,769]{2,1,0:T(8,128)(2,1)}), bf16[64,8,769]{2,1,0:T(8,128)(2,1)S(1)}, u32[]{:S(2)}, u32[]{:S(2)}) async-start(bf16[64,8,769]{2,1,0:T(8,128)(2,1)} %pad_maximum_fusion), calls=%async_computation.3 | async-start | bytes 1835008 | tf_op jit(solution)/shard_map/all_to_all | solution.py:77
Sparse Core Ops, SparseCore 0:
  34.3 109.8 all-gather.2
  151.5 65.5 all-gather.4
where the time goes:
time: 336 us; the launch traced here: 335 us
  waiting for transfers between devices  139 us (41%)
  blocking collectives  101 us (30%)
  starting transfers between devices  28.9 us (9%)
  matrix products  25.5 us (8%)
  other arithmetic  14.6 us (4%)
  between operations  14.5 us (4%)
  local copies, waits for them, and re-layouts  11.2 us (3%)
    all_gather x1, waiting for transfers between devices, sent_together(): filled = lax.all_gather(both, axis, axis=dim, tiled=True)  103 us
    all_gather x1, blocking collectives, gather_turned(): filled, at, outs = (lax.all_gather(both, axis, axis=0, tiled=True), 0, [])  41.1 us
    all_gather x1, blocking collectives, in_one_piece(): lax.all_gather(both, axis, axis=dim, tiled=True)  27.3 us
    all_gather x1, blocking collectives, sent_together(): filled = lax.all_gather(both, axis, axis=dim, tiled=True)  25.4 us
    all_to_all x1, waiting for transfers between devices, summed_on_arrival_2(): tiles = lax.all_to_all(split_up(x, dim, size), axis, 0, 0, tiled=True)  22.7 us
    all_to_all x1, starting transfers between devices, summed_on_arrival_2(): tiles = lax.all_to_all(split_up(x, dim, size), axis, 0, 0, tiled=True)  21 us
    all_to_all x1, waiting for transfers between devices, from_everyone(): return lax.all_to_all(copies, axis, split_axis=0, concat_axis=0, tiled=True)  12.8 us
    all_to_all x1, blocking collectives, summed_on_arrival(): lax.all_to_all(tiles, axis, split_axis=0, concat_axis=0, tiled=True)  7.46 us
  transfers between devices with their start and end apart: 5, of which 3 were waited for; matrix products, arithmetic and copies ran while one was open for 11% of the time, Pallas kernels for 0%

commit v1 on v0

--- a/solution.py
+++ b/solution.py
@@ -1,28 +1,224 @@
+import functools
 import math
 
 import jax
 import jax.numpy as jnp
 from jax import lax
+from jax.experimental import pallas as pl
+from jax.experimental.pallas import tpu as pltpu
 from jax.sharding import PartitionSpec as P
 
 HD = 128
 HEADS = 4
-
+TILES = HEADS + 2
+MESH = pl.DeviceIdType.MESH
+SIZES = {"x": 4, "y": 8, "z": 8}
+ORDERS = (("z", "y", "x"), ("x", "z", "y"), ("y", "x", "z"))
+HALVES = 2
 
 eps_norm = 1e-05
 rope_base = 500000.0
 
 
-def sent_together(arrays, axis, dim, along):
-    widths = [math.prod(a.shape[along:]) for a in arrays]
-    both = jnp.concatenate(
-        [a.reshape(*a.shape[:along], w) for a, w in zip(arrays, widths)], axis=along
-    )
-    filled = lax.all_gather(both, axis, axis=dim, tiled=True)
-    tiles = jnp.split(filled, [sum(widths[:k]) for k in range(1, len(widths))], axis=along)
-    return tuple(
-        (b.reshape(*filled.shape[:along], *a.shape[along:]) for a, b in zip(arrays, tiles))
-    )
+def place():
+    i, j = lax.axis_index("inter"), lax.axis_index("intra")
+    return {"x": j // 2, "y": i // 8, "z": ((i // 2) % 4) * 2 + j % 2}, i % 2
+
+
+def device(at, core):
+    return ((at["y"] * 4 + at["z"] // 2) * 2 + core, at["x"] * 2 + at["z"] % 2)
+
+
+def moved(at, dim, step):
+    size = SIZES[dim]
+    return {**at, dim: (at[dim] + step + size) % size}
+
+
+def slab(ref, tile, at, cores=slice(None)):
+    every = slice(None)
+    y, x = at.get("y", every), at.get("x", every)
+    high, low = (at["z"] // 2, at["z"] % 2) if "z" in at else (every, every)
+    return ref.at[tile, y, high, cores, x, low]
+
+
+def enter(at, core, barrier):
+    peers = [device(at, 1 - core)]
+    for dim, size in SIZES.items():
+        peers += [device(moved(at, dim, step), core) for step in range(1, size)]
+    for peer in peers:
+        pl.semaphore_signal(barrier, inc=1, device_id=peer, device_id_type=MESH)
+    pl.semaphore_wait(barrier, len(peers))
+
+
+def gather_kernel(
+    mine_ref, full_ref, swap_send, swap_recv, send_1, recv_1, send_2, recv_2, ring_send, ring_recv, pass_send, pass_recv, own_sem
+):
+    at, core = place()
+    partner = device(at, 1 - core)
+    enter(at, core, pltpu.get_barrier_semaphore())
+
+    def remote(src, dst, send, recv, peer):
+        return pltpu.make_async_remote_copy(
+            src_ref=src, dst_ref=dst, send_sem=send, recv_sem=recv, device_id=peer, device_id_type=MESH
+        )
+
+    mine = [3 * core + p for p in range(3)]
+    theirs = [3 * (1 - core) + p for p in range(3)]
+    swaps, owns = [], []
+    for p in range(3):
+        swaps.append(
+            remote(
+                mine_ref.at[theirs[p]],
+                slab(full_ref, theirs[p], at, core),
+                swap_send.at[p],
+                swap_recv.at[p],
+                partner,
+            )
+        )
+        swaps[-1].start()
+        owns.append(
+            pltpu.make_async_copy(mine_ref.at[mine[p]], slab(full_ref, mine[p], at, core), own_sem.at[p])
+        )
+        owns[-1].start()
+    for p in range(3):
+        owns[p].wait()
+    swap_in = [
+        remote(
+            mine_ref.at[mine[p]],
+            slab(full_ref, mine[p], at, 1 - core),
+            swap_send.at[p],
+            swap_recv.at[p],
+            partner,
+        )
+        for p in range(3)
+    ]
+
+    def direct(p, dim, known, send, recv):
+        src = slab(full_ref, mine[p], known)
+        copies = []
+        for step in range(1, SIZES[dim]):
+            k = step - 1
+            copies.append(remote(src, src, send.at[p, k], recv.at[p, k], device(moved(at, dim, step), core)))
+            copies[-1].start()
+        return copies
+
+    def arrived(p, dim, known, send, recv):
+        for step in range(1, SIZES[dim]):
+            k = step - 1
+            there = slab(full_ref, mine[p], moved(known, dim, -step))
+            remote(there, there, send.at[p, k], recv.at[p, k], partner).wait_recv()
+
+    sent = []
+    first, second = [], []
+    for p in range(3):
+        swap_in[p].wait_recv()
+        sent += direct(p, ORDERS[p][0], at, send_1, recv_1)
+    for p in range(3):
+        a, b, c = ORDERS[p]
+        arrived(p, a, at, send_1, recv_1)
+        known = {b: at[b], c: at[c]}
+        sent += direct(p, b, known, send_2, recv_2)
+
+    sign = 1 - 2 * core
+    ways = ((0, sign), (1, -sign))
+
+    def piece(p, where, h):
+        return slab(full_ref, mine[p], {ORDERS[p][2]: where}, h)
+
+    def hop(p, way, step, h):
+        dim = ORDERS[p][2]
+        direction = ways[way][1]
+        return remote(
+            piece(p, moved(at, dim, -direction * step)[dim], h),
+            piece(p, moved(at, dim, -direction * step)[dim], h),
+            ring_send.at[p, way, step, h],
+            ring_recv.at[p, way, step, h],
+            device(moved(at, dim, direction), core),
+        )
+
+    def arriving(p, way, step, h):
+        dim = ORDERS[p][2]
+        where = moved(at, dim, -ways[way][1] * (step + 1))[dim]
+        return remote(
+            piece(p, where, h), piece(p, where, h), ring_send.at[p, way, step, h], ring_recv.at[p, way, step, h], partner
+        )
+
+    def pass_on(p, where, slot):
+        copy = remote(
+            slab(full_ref, mine[p], {ORDERS[p][2]: where}),
+            slab(full_ref, mine[p], {ORDERS[p][2]: where}),
+            pass_send.at[p, slot],
+            pass_recv.at[p, slot],
+            partner,
+        )
+        copy.start()
+        return copy
+
+    def steps_of(p, way):
+        return SIZES[ORDERS[p][2]] // 2 - way
+
+    for p in range(3):
+        a, b, c = ORDERS[p]
+        arrived(p, b, {b: at[b], c: at[c]}, send_2, recv_2)
+        for h in range(HALVES):
+            for way in range(2):
+                copy = hop(p, way, 0, h)
+                copy.start()
+                sent.append(copy)
+        sent.append(pass_on(p, at[c], 0))
+    for step in range(4):
+        for h in range(HALVES):
+            for p in range(3):
+                for way in range(2):
+                    if step >= steps_of(p, way):
+                        continue
+                    arriving(p, way, step, h).wait_recv()
+                    if step + 1 < steps_of(p, way):
+                        copy = hop(p, way, step + 1, h)
+                        copy.start()
+                        sent.append(copy)
+                    if h == HALVES - 1:
+                        dim = ORDERS[p][2]
+                        where = moved(at, dim, -ways[way][1] * (step + 1))[dim]
+                        sent.append(pass_on(p, where, (1 + step if way == 0 else -1 - step) % 8))
+    for p in range(3):
+        dim = ORDERS[p][2]
+        size = SIZES[dim]
+        for step in range(size // 2 + 1):
+            for way in range(2):
+                if (step == 0 and way == 1) or step > steps_of(p, way):
+                    continue
+                slot = 0 if step == 0 else (step if way == 0 else -step)
+                where = moved(at, dim, (ways[way][1]) * step)[dim]
+                there = slab(full_ref, theirs[p], {dim: where})
+                remote(there, there, pass_send.at[p, slot % 8], pass_recv.at[p, slot % 8], partner).wait_recv()
+    for copy in swaps + sent:
+        copy.wait_send()
+
+
+def gather_weights(tiles):
+    dma = pltpu.SemaphoreType.DMA
+    return pl.pallas_call(
+        gather_kernel,
+        out_shape=jax.ShapeDtypeStruct((TILES, 8, 4, 2, 4, 2, 8, HD), jnp.bfloat16),
+        in_specs=[pl.BlockSpec(memory_space=pltpu.VMEM)],
+        out_specs=pl.BlockSpec(memory_space=pltpu.VMEM),
+        scratch_shapes=[
+            dma((3,)),
+            dma((3,)),
+            dma((3, 7)),
+            dma((3, 7)),
+            dma((3, 7)),
+            dma((3, 7)),
+            dma((3, 2, 4, HALVES)),
+            dma((3, 2, 4, HALVES)),
+            dma((3, 8)),
+            dma((3, 8)),
+            dma((3,)),
+        ],
+        compiler_params=pltpu.CompilerParams(collective_id=0, has_side_effects=True, vmem_limit_bytes=48 * 2**20),
+        name="gather_weights",
+    )(tiles)
 
 
 def in_one_piece(arrays, axis, dim, along):
@@ -183,6 +379,15 @@
     return key_advance
 
 
+def gain_of_outputs(norm_gain):
+    pairs = []
+    for i in range(64):
+        for j in range(8):
+            row = (j * 512 + i * 8) // 8
+            pairs.append((row, i * 8 + j))
+    return lax.ppermute(norm_gain, ("inter", "intra"), pairs).astype(jnp.float32)
+
+
 def local(hidden_in, norm_gain, qkv_weight, attn_cotangent):
     rows_in = hidden_in[0]
     grad_attn = attn_cotangent[0]
@@ -192,8 +397,11 @@
     heads_count = HEADS
     qcols = heads_count * head_size
     scale = head_size ** (-0.5)
-    weight_group, gain_group = sent_together((qkv_weight, norm_gain), "intra", 0, 1)
-    weight_full, gain_full = sent_together((weight_group, gain_group), "inter", 0, 1)
+    scaled = (qkv_weight.astype(jnp.float32) * norm_gain.astype(jnp.float32)[:, None]).astype(jnp.bfloat16)
+    tiles = jnp.moveaxis(scaled.reshape(8, TILES, HD), 1, 0)
+    weight_tiles = gather_weights(tiles).reshape(TILES, width, HD)
+    weight_full = jnp.moveaxis(weight_tiles, 0, 1).reshape(width, TILES * HD)
+    gain_here = gain_of_outputs(norm_gain)
     query_pos = lax.axis_index("intra") * tokens_here + jnp.arange(tokens_here, dtype=jnp.int32)
     row_pos = jnp.broadcast_to(query_pos[:, None], (tokens_here, heads_count)).reshape(
         tokens_here * heads_count
@@ -201,7 +409,7 @@
     cosine, sine = rope_tables(query_pos, head_size)
     wide_rows = rows_in.astype(jnp.float32)
     inv_rms = lax.rsqrt(jnp.mean(wide_rows * wide_rows, axis=1, keepdims=True) + eps_norm)
-    normed = (wide_rows * inv_rms * gain_full.astype(jnp.float32)[None, :]).astype(jnp.bfloat16)
+    normed = (wide_rows * inv_rms).astype(jnp.bfloat16)
     mixed = jnp.dot(normed, weight_full, preferred_element_type=jnp.float32)
     query_rows = (
         (
@@ -253,16 +461,9 @@
     grad_mixed = jnp.concatenate(
         [query_back, unrotate(grad_keys, cosine, sine), grad_values], axis=1
     ).astype(jnp.bfloat16)
-    weight_back, gain_back = (weight_full, gain_full)
-    gain_wide = gain_back.astype(jnp.float32)[None, :]
-    grad_normed = jnp.einsum(
-        "tc,dc->td", grad_mixed, weight_back, preferred_element_type=jnp.float32
-    )
-    inner = jnp.sum(grad_normed * gain_wide * wide_rows, axis=1, keepdims=True)
-    grad_rows = (
-        gain_wide * grad_normed * inv_rms - wide_rows * inv_rms**3 / width * inner
-    ).astype(jnp.bfloat16)
-    gain_term = jnp.sum(grad_normed * wide_rows * inv_rms, axis=0)
+    scaled_grad = jnp.einsum("tc,dc->td", grad_mixed, weight_full, preferred_element_type=jnp.float32)
+    inner = jnp.sum(scaled_grad * wide_rows, axis=1, keepdims=True)
+    grad_rows = (scaled_grad * inv_rms - wide_rows * inv_rms**3 / width * inner).astype(jnp.bfloat16)
     normed_cols = lax.all_to_all(normed, "intra", split_axis=1, concat_axis=0, tiled=True)
     group_term = lax.dot_general(
         normed_cols,
@@ -271,13 +472,11 @@
         preferred_element_type=jnp.float32,
     )
     term_low = lax.optimization_barrier(group_term.astype(jnp.bfloat16))
-    gain_sums = summed_on_arrival(gain_term, "intra", 0)
-    weight_grad, gain_grad = side_by_side(
-        (term_low.astype(jnp.float32).astype(jnp.bfloat16), gain_sums.astype(jnp.bfloat16)),
-        "inter",
-        0,
-        1,
-    )
+    plain_grad = summed_on_arrival_2(term_low, "inter", 0)
+    start = lax.axis_index("intra") * 512 + lax.axis_index("inter") * 8
+    weight_here = lax.dynamic_slice_in_dim(weight_full, start, 8, 0).astype(jnp.float32)
+    weight_grad = plain_grad * gain_here[:, None]
+    gain_grad = jnp.sum(plain_grad * weight_here, axis=1) / gain_here
     return (attn_flat.reshape(tokens_here, qcols)[None], grad_rows[None], weight_grad, gain_grad)
 
 

time: 336 us -> 260 us (0.77)
  waiting for transfers between devices: 139 us -> 27.7 us
  Pallas kernels: 0 us -> 56.3 us
  blocking collectives: 101 us -> 70.8 us
  local copies, waits for them, and re-layouts: 11.2 us -> 17.7 us
    all_gather x1 -> x0, waiting for transfers between devices: 103 us -> none  [sent_together(): filled = lax.all_gather(both, axis, axis=dim, tiled=True)]
    pallas_call x0 -> x1, Pallas kernels: none -> 56.3 us  [gather_weights(): pl.pallas_call(gather_kernel, out_shape=jax.ShapeDtypeStruct((TILES, 8, 4...]
    all_gather x1 -> x0, blocking collectives: 25.4 us -> none  [sent_together(): filled = lax.all_gather(both, axis, axis=dim, tiled=True)]
    all_gather x1, blocking collectives: 27.3 us -> 48.4 us  [in_one_piece(): lax.all_gather(both, axis, axis=dim, tiled=True)]
    all_gather x1, blocking collectives: 41.1 us -> 22.4 us  [gather_turned(): filled, at, outs = (lax.all_gather(both, axis, axis=0, tiled=True), 0, [])]
    all_to_all x1, starting transfers between devices: 21 us -> 8.16 us  [summed_on_arrival_2(): tiles = lax.all_to_all(split_up(x, dim, size), axis, 0, 0, tiled=True)]
    all_to_all x1, waiting for transfers between devices: 12.8 us -> 0.01 us  [from_everyone(): return lax.all_to_all(copies, axis, split_axis=0, concat_axis=0, tiled=True)]
    ppermute x0 -> x1, starting transfers between devices: none -> 12.6 us  [gain_of_outputs(): lax.ppermute(norm_gain, ('inter', 'intra'), pairs).astype(jnp.float32)]
  transfers between devices with their start and end apart: 5 -> 5, of which waited for: 3 -> 2; matrix products, arithmetic and copies ran while one was open for 11% -> 13% of each run, Pallas kernels for 0% -> 0%
where the time goes in v1:
time: 260 us; the launch traced here: 259 us
  blocking collectives  70.8 us (27%)
  Pallas kernels  56.3 us (22%)
  starting transfers between devices  29.6 us (11%)
  waiting for transfers between devices  27.7 us (11%)
  matrix products  27.3 us (10%)
  local copies, waits for them, and re-layouts  17.7 us (7%)
  other arithmetic  14.9 us (6%)
  between operations  14.4 us (6%)
    pallas_call x1, Pallas kernels, gather_weights(): pl.pallas_call(gather_kernel, out_shape=jax.ShapeDtypeStruct((TILES, 8, 4...  56.3 us
    all_gather x1, blocking collectives, in_one_piece(): lax.all_gather(both, axis, axis=dim, tiled=True)  48.4 us
    all_gather x1, blocking collectives, gather_turned(): filled, at, outs = (lax.all_gather(both, axis, axis=0, tiled=True), 0, [])  22.4 us
    all_to_all x1, waiting for transfers between devices, summed_on_arrival_2(): tiles = lax.all_to_all(split_up(x, dim, size), axis, 0, 0, tiled=True)  18.7 us
    ppermute x1, starting transfers between devices, gain_of_outputs(): lax.ppermute(norm_gain, ('inter', 'intra'), pairs).astype(jnp.float32)  12.6 us
    ppermute x1, waiting for transfers between devices, gain_of_outputs(): lax.ppermute(norm_gain, ('inter', 'intra'), pairs).astype(jnp.float32)  9.01 us
    reshape x1, local copies, waits for them, and re-layouts, local(): weight_tiles = gather_weights(tiles).reshape(TILES, width, HD)  8.86 us
    all_to_all x1, starting transfers between devices, summed_on_arrival_2(): tiles = lax.all_to_all(split_up(x, dim, size), axis, 0, 0, tiled=True)  8.16 us
  transfers between devices with their start and end apart: 5, of which 2 were waited for; matrix products, arithmetic and copies ran while one was open for 13% of the time, Pallas kernels for 0%

profile of v1, /device:TPU:1, one launch (start us, length us, event | category | flops | bytes accessed | tf_op | source)
XLA Modules:
  0.0 258.8 jit_solution(9388906936335085492)
XLA Ops:
  7.2 0.0 all-gather.2.cloned.1.call-start
  7.2 1.5 fusion.6
  8.8 0.5 multiply_multiply_fusion
  9.3 0.7 convert_element_type.87
  9.9 0.8 fusion.67.mine_ref
  10.7 56.3 %gather_weights.1 = bf16[6,8,4,2,4,2,8,128]{7,6,5,4,3,2,1,0:T(8,128)(2,1)} custom-call(bf16[6,8,128]{2,1,0:T(8,128)(2,1)S(1)} %fusion.67.mine_ref), custom_call_target="tpu_custom_call" | custom-call | tf_op jit(solution)/shard_map/gather_weights/pallas_call | solution.py:201
  67.1 0.0 copy-start
  67.1 8.9 %copy.23 = bf16[6,4096,128]{1,2,0:T(8,128)(2,1)} copy(bf16[6,4096,128]{2,1,0:T(8,128)(2,1)} %bitcast.62) | data formatting | bytes 12582912 | tf_op jit(solution)/shard_map/reshape | solution.py:402
  75.9 0.0 copy-start.10
  75.9 5.0 %fusion.19 = f32[128,768]{1,0:T(8,128)S(1)} fusion(bf16[4096,768]{0,1:T(8,128)(2,1)} %bitcast.59, bf16[1,128,4096]{2,1,0:T(8,128)(2,1)S(1)} %copy-done, f32[128]{0:T(128)S(1)} %get-tuple-element.23), kind=kOutput, calls=%fused_computation.32 | convolution fusion | flops 806879232 | bytes 7733760 | tf_op jit(solution)/shard_map/dot_general | solution.py:413
  81.0 0.1 reshape.181
  81.1 0.1 reshape_squeeze.3
  81.2 0.0 copy-start.4
  81.2 1.0 fusion.54
  82.2 0.3 multiply_subtract_fusion.1
  82.5 0.1 fusion.38
  82.7 0.6 copy-done.3
  83.3 0.8 pad_maximum_fusion
  84.1 0.0 all-gather.2.cloned.1.call-update
  84.1 0.5 copy.34
  84.6 1.2 multiply_convert_fusion
  85.8 4.4 %all-to-all-start = ((bf16[128,8,512]{0,2,1:T(8,128)(2,1)}), bf16[128,8,512]{0,2,1:T(8,128)(2,1)}, u32[]{:S(2)}, u32[]{:S(2)}) async-start(bf16[128,8,512]{0,2,1:T(8,128)(2,1)} %multiply_convert_fusion), calls=%async_computation | async-start | bytes 2097152 | tf_op jit(solution)/shard_map/all_to_all | solution.py:467
  90.2 0.8 copy.25
  91.0 0.1 broadcast_in_dim.26
  91.0 0.1 le.15
  91.2 0.1 pad_maximum_fusion.2
  91.3 0.3 copy-done.18
  91.5 48.4 %all_gather.9 = bf16[1024,256]{1,0:T(8,128)(2,1)S(1)} all-gather(bf16[128,256]{1,0:T(8,128)(2,1)S(1)} %pad_maximum_fusion.2), channel_id=1, replica_groups=mesh['inter'=64,'intra'=8] {'intra'}, dimensions={0}, use_global_device_ids=true | all-gather | bytes 589824 | tf_op jit(solution)/shard_map/all_gather | solution.py:230
  139.9 1.6 fusion.73
  141.6 0.7 fusion.12
  142.3 2.4 multiply_reduce_fusion
  144.7 2.6 %fusion.15 = f32[512,128]{1,0:T(8,128)} fusion(f32[512,1024]{1,0:T(8,128)S(1)} %get-tuple-element.25, bf16[512,128]{1,0:T(8,128)(2,1)} %copy-done.4, f32[512]{0:T(512)S(1)} %get-tuple-element.26, f32[512]{0:T(512)S(1)} %log_add_fusion, s32[512]{0:T(512)S(1)} %le.15, bf16[1024,256]{1,0:T(8,128)(2,1)} %copy-done.2), kind=kOutput, calls=%fused_computation.27 | convolution fusion | flops 271581184 | bytes 3020800 | tf_op jit(solution)/shard_map/dot_general | solution.py:348
  147.3 1.2 multiply_add_fusion
  148.5 0.2 fusion.39
  148.8 0.7 copy.38
  149.4 22.4 %all_gather.11 = f32[4096,2]{0,1:T(2,128)S(1)} all-gather(f32[512,2]{0,1:T(2,128)S(1)} %pad_maximum_fusion.3), channel_id=1, replica_groups=mesh['inter'=64,'intra'=8] {'intra'}, dimensions={0}, use_global_device_ids=true | all-gather | bytes 36864 | tf_op jit(solution)/shard_map/all_gather | solution.py:236
  171.8 0.6 add_select_fusion
  172.4 0.6 fusion.72
  173.1 3.4 %fusion.2 = f32[4096,128]{1,0:T(8,128)S(1)} fusion(f32[4096]{0:T(1024)} %bitcast.70, s32[128]{0:T(128)} %copy-done.18, s32[4096]{0:T(1024)} %add_select_fusion, bf16[4096,256]{1,0:T(8,128)(2,1)} %all-gather.2.cloned.1.call-done, bf16[128,64]{1,0:T(8,128)(2,1)} %get-tuple-element.9, bf16[128,64]{1,0:T(8,128)(2,1)} %get-tuple-element.8), kind=kOutput, calls=%fused_computation.3 | convolution fusion | flops 136380416 | bytes 3244544 | tf_op jit(solution)/shard_map/qd,kd->qk/dot_general | solution.py:358
  176.4 1.1 convolution_convert_fusion
  177.6 1.5 copy.29
  179.0 3.6 %fusion.14 = f32[128,128]{1,0:T(8,128)} fusion(f32[4096,128]{1,0:T(8,128)S(1)} %fusion.2, f32[4096]{0:T(1024)S(1)} %bitcast.69, bf16[4096,256]{1,0:T(8,128)(2,1)} %all-gather.2.cloned.1.call-done, f32[128,768]{1,0:T(8,128)S(1)} %fusion.19), kind=kOutput, calls=%fused_computation.26 | convolution fusion | flops 270008320 | bytes 4308992 | tf_op jit(solution)/shard_map/qk,qd->kd/dot_general | solution.py:374
  182.7 1.2 fusion.58
  183.9 1.0 pad_maximum_fusion.1
  184.9 0.0 copy-start.19
  184.9 0.0 all-to-all-done
  184.9 1.3 broadcast_in_dim.59
  186.3 4.4 %all-to-all-start.1 = ((bf16[8,128,768]{2,1,0:T(8,128)(2,1)}), bf16[8,128,768]{2,1,0:T(8,128)(2,1)}, u32[]{:S(2)}, u32[]{:S(2)}) async-start(bf16[8,128,768]{2,1,0:T(8,128)(2,1)} %broadcast_in_dim.59), calls=%async_computation.1 | async-start | bytes 3145728 | tf_op jit(solution)/shard_map/all_to_all | solution.py:252
  190.7 12.6 %collective-permute-start = (bf16[8]{0:T(256)(128)(2,1)S(1)}, bf16[8]{0:T(256)(128)(2,1)S(1)}, u32[]{:S(2)}, u32[]{:S(2)}) collective-permute-start(bf16[8]{0:T(256)(128)(2,1)S(1)} %copy-done.19), channel_id=1, source_target_pairs={{0,0},{64,1},{128,2},{192,3},{256,4},{320,5},{384,6},{448,7},{1,8}... | collective-permute-start | bytes 56 | tf_op jit(solution)/shard_map/ppermute | solution.py:388
  203.4 1.0 constant_dynamic-slice_fusion
  204.5 0.1 copy.35
  204.5 0.1 copy.24
  204.7 0.7 broadcast_in_dim_reshape.2
  205.4 9.0 %collective-permute-done = bf16[8]{0:T(256)(128)(2,1)S(1)} collective-permute-done((bf16[8]{0:T(256)(128)(2,1)S(1)}, bf16[8]{0:T(256)(128)(2,1)S(1)}, u32[]{:S(2)}, u32[]{:S(2)}) %collective-permute-start) | collective-permute-done | bytes 48 | tf_op jit(solution)/shard_map/ppermute | solution.py:388
  214.5 0.0 all-to-all-done.1
  214.5 3.7 %bitcast_convert_fusion = bf16[512,768]{1,0:T(8,128)(2,1)} fusion(bf16[8,128,768]{2,1,0:T(8,128)(2,1)} %all-to-all-done.1, bf16[128,8,512]{0,2,1:T(8,128)(2,1)} %all-to-all-done), kind=kOutput, calls=%fused_computation.24 | convolution fusion | flops 805699584 | bytes 3407872 | tf_op jit(solution)/shard_map/dot_general | solution.py:468
  218.1 8.2 %all-to-all-start.2 = ((bf16[64,8,768]{2,1,0:T(8,128)(2,1)}), bf16[64,8,768]{2,1,0:T(8,128)(2,1)S(1)}, u32[]{:S(2)}, u32[]{:S(2)}) async-start(bf16[64,8,768]{2,1,0:T(8,128)(2,1)} %bitcast.20), calls=%async_computation.2 | async-start | bytes 1572864 | tf_op jit(solution)/shard_map/all_to_all | solution.py:273
  226.3 0.0 copy-start.17
  226.3 3.9 %fusion.10 = (f32[128]{0:T(128)S(1)}, f32[128,4096]{1,0:T(8,128)S(1)}) fusion(bf16[1,128,4096]{2,1,0:T(8,128)(2,1)S(1)} %copy-done, bf16[128,768]{1,0:T(8,128)(2,1)S(1)} %pad_maximum_fusion.1, bf16[4096,768]{0,1:T(8,128)(2,1)} %bitcast.61), kind=kOutput, calls=%fused_computation.16 | convolution fusion | flops 806879104 | bytes 9634304 | tf_op jit(solution)/shard_map/tc,dc->td/dot_general | solution.py:464
  230.2 1.6 fusion.21
  231.8 18.7 %all-to-all-done.2 = bf16[64,8,768]{2,1,0:T(8,128)(2,1)S(1)} async-done(((bf16[64,8,768]{2,1,0:T(8,128)(2,1)}), bf16[64,8,768]{2,1,0:T(8,128)(2,1)S(1)}, u32[]{:S(2)}, u32[]{:S(2)}) %all-to-all-start.2) | async-done | bytes 786464 | tf_op jit(solution)/shard_map/all_to_all | solution.py:273
  250.5 0.1 convert_reduce_fusion
  250.6 0.8 multiply_reduce_fusion.1
  251.4 0.5 convert_divide_fusion
  (44 shorter events, 0.1 us)
Async XLA Ops:
  7.2 165.9 %all-gather.2.cloned.1.call-start = ((), (), s32[]{:S(2)}) async-start(), calls=%async_computation.3 | async-start | bytes 2359296 | tf_op jit(solution)/shard_map/all_gather | solution.py:230
  7.2 74.0 %copy-start.15 = (f32[64]{0:T(128)}, f32[64]{0:T(128)S(1)}, u32[]{:S(2)}) copy-start(f32[64]{0:T(128)S(1)} %multiply_power_fusion) | copy-start | bytes 772
  9.3 75.3 %copy-start.13 = (f32[128]{0:T(128)}, f32[128]{0:T(128)S(1)}, u32[]{:S(2)}) copy-start(f32[128]{0:T(128)S(1)} %get-tuple-element.23) | copy-start | bytes 1540
  67.1 8.9 %copy-start = (bf16[1,128,4096]{2,1,0:T(8,128)(2,1)S(1)}, bf16[1,128,4096]{2,1,0:T(8,128)(2,1)}, u32[]{:S(2)}) copy-start(bf16[1,128,4096]{2,1,0:T(8,128)(2,1)} %param.4) | copy-start | bytes 3145732
  75.9 5.3 %copy-start.16 = (f32[128]{0:T(128)}, f32[128]{0:T(128)S(1)}, u32[]{:S(2)}) copy-start(f32[128]{0:T(128)S(1)} %fusion.71) | copy-start | bytes 1540
  75.9 5.2 %copy-start.10 = (bf16[1,128,512]{2,1,0:T(8,128)(2,1)S(1)}, bf16[1,128,512]{2,1,0:T(8,128)(2,1)}, u32[]{:S(2)}) copy-start(bf16[1,128,512]{2,1,0:T(8,128)(2,1)} %param.7) | copy-start | bytes 393220
  81.2 2.8 %copy-start.4 = (bf16[512,128]{1,0:T(8,128)(2,1)}, bf16[512,128]{1,0:T(8,128)(2,1)S(1)}, u32[]{:S(2)}) copy-start(bf16[512,128]{1,0:T(8,128)(2,1)S(1)} %reshape_squeeze.3) | copy-start | bytes 393220
  82.2 1.9 copy-start.6
  82.2 1.9 copy-start.7
  82.6 0.7 copy-start.3
  85.8 4.4 %copy-start.5 = (bf16[512,128]{1,0:T(8,128)(2,1)S(1)}, bf16[512,128]{1,0:T(8,128)(2,1)}, u32[]{:S(2)}) copy-start(bf16[512,128]{1,0:T(8,128)(2,1)} %copy-done.4) | copy-start | bytes 393220
  85.8 5.4 %copy-start.8 = (bf16[128,64]{1,0:T(8,128)(2,1)S(1)}, bf16[128,64]{1,0:T(8,128)(2,1)}, u32[]{:S(2)}) copy-start(bf16[128,64]{1,0:T(8,128)(2,1)} %get-tuple-element.8) | copy-start | bytes 49156
  85.8 5.4 %copy-start.9 = (bf16[128,64]{1,0:T(8,128)(2,1)S(1)}, bf16[128,64]{1,0:T(8,128)(2,1)}, u32[]{:S(2)}) copy-start(bf16[128,64]{1,0:T(8,128)(2,1)} %get-tuple-element.9) | copy-start | bytes 49156
  85.8 99.1 %all-to-all-start = ((bf16[128,8,512]{0,2,1:T(8,128)(2,1)}), bf16[128,8,512]{0,2,1:T(8,128)(2,1)}, u32[]{:S(2)}, u32[]{:S(2)}) async-start(bf16[128,8,512]{0,2,1:T(8,128)(2,1)} %multiply_convert_fusion), calls=%async_computation | async-start | bytes 2097152 | tf_op jit(solution)/shard_map/all_to_all | solution.py:467
  91.0 0.6 copy-start.18
  139.9 2.3 copy-start.2
  139.9 2.3 copy-start.12
  173.0 3.4 %copy-start.1 = (bf16[4096,256]{1,0:T(8,128)(2,1)S(1)}, bf16[4096,256]{1,0:T(8,128)(2,1)}, u32[]{:S(2)}) copy-start(bf16[4096,256]{1,0:T(8,128)(2,1)} %all-gather.2.cloned.1.call-done) | copy-start | bytes 6291460
  184.9 5.8 %copy-start.19 = (bf16[8]{0:T(256)(128)(2,1)S(1)}, bf16[8]{0:T(256)(128)(2,1)}, u32[]{:S(2)}) copy-start(bf16[8]{0:T(256)(128)(2,1)} %param.5) | copy-start | bytes 52
  186.3 18.3 %copy-start.11 = (bf16[512,128]{0,1:T(8,128)(2,1)S(1)}, bf16[512,128]{0,1:T(8,128)(2,1)}, u32[]{:S(2)}) copy-start(bf16[512,128]{0,1:T(8,128)(2,1)} %get-tuple-element.27) | copy-start | bytes 393220
  186.3 28.2 %all-to-all-start.1 = ((bf16[8,128,768]{2,1,0:T(8,128)(2,1)}), bf16[8,128,768]{2,1,0:T(8,128)(2,1)}, u32[]{:S(2)}, u32[]{:S(2)}) async-start(bf16[8,128,768]{2,1,0:T(8,128)(2,1)} %broadcast_in_dim.59), calls=%async_computation.1 | async-start | bytes 3145728 | tf_op jit(solution)/shard_map/all_to_all | solution.py:252
  190.7 23.7 %collective-permute-start = (bf16[8]{0:T(256)(128)(2,1)S(1)}, bf16[8]{0:T(256)(128)(2,1)S(1)}, u32[]{:S(2)}, u32[]{:S(2)}) collective-permute-start(bf16[8]{0:T(256)(128)(2,1)S(1)} %copy-done.19), channel_id=1, source_target_pairs={{0,0},{64,1},{128,2},{192,3},{256,4},{320,5},{384,6},{448,7},{1,8}... | collective-permute-start | bytes 56 | tf_op jit(solution)/shard_map/ppermute | solution.py:388
  218.1 32.4 %all-to-all-start.2 = ((bf16[64,8,768]{2,1,0:T(8,128)(2,1)}), bf16[64,8,768]{2,1,0:T(8,128)(2,1)S(1)}, u32[]{:S(2)}, u32[]{:S(2)}) async-start(bf16[64,8,768]{2,1,0:T(8,128)(2,1)} %bitcast.20), calls=%async_computation.2 | async-start | bytes 1572864 | tf_op jit(solution)/shard_map/all_to_all | solution.py:273
  226.3 3.9 %copy-start.14 = (f32[128]{0:T(128)S(1)}, f32[128]{0:T(128)}, u32[]{:S(2)}) copy-start(f32[128]{0:T(128)} %copy-done.13) | copy-start | bytes 1540
  226.3 3.9 %copy-start.17 = (f32[128]{0:T(128)S(1)}, f32[128]{0:T(128)}, u32[]{:S(2)}) copy-start(f32[128]{0:T(128)} %get-tuple-element.22) | copy-start | bytes 1540
Sparse Core Ops, SparseCore 0:
  84.2 70.9 all-gather.1

commit v2 on v1

v2 whole, which is shorter than its diff:
```python
import functools
import math

import jax
import jax.numpy as jnp
from jax import lax
from jax.experimental import pallas as pl
from jax.experimental.pallas import tpu as pltpu
from jax.sharding import PartitionSpec as P

HD = 128
HEADS = 4
TILES = HEADS + 2
MESH = pl.DeviceIdType.MESH
SIZES = {"x": 4, "y": 8, "z": 8}
ORDERS = (("z", "y", "x"), ("x", "z", "y"), ("y", "x", "z"))
HALVES = 2
GAIN_ORDER = ("z", "y", "x")

eps_norm = 1e-05
rope_base = 500000.0


def place():
    i, j = lax.axis_index("inter"), lax.axis_index("intra")
    return {"x": j // 2, "y": i // 8, "z": ((i // 2) % 4) * 2 + j % 2}, i % 2


def device(at, core):
    return ((at["y"] * 4 + at["z"] // 2) * 2 + core, at["x"] * 2 + at["z"] % 2)


def moved(at, dim, step):
    size = SIZES[dim]
    return {**at, dim: (at[dim] + step + size) % size}


def slab(ref, tile, at, cores=slice(None)):
    every = slice(None)
    y, x = at.get("y", every), at.get("x", every)
    high, low = (at["z"] // 2, at["z"] % 2) if "z" in at else (every, every)
    return ref.at[tile, y, high, cores, x, low]


def enter(at, core, barrier):
    peers = [device(at, 1 - core)]
    for dim, size in SIZES.items():
        peers += [device(moved(at, dim, step), core) for step in range(1, size)]
    for peer in peers:
        pl.semaphore_signal(barrier, inc=1, device_id=peer, device_id_type=MESH)
    pl.semaphore_wait(barrier, len(peers))


def gain_slab(ref, at, cores):
    every = slice(None)
    y, x = at.get("y", every), at.get("x", every)
    high, low = (at["z"] // 2, at["z"] % 2) if "z" in at else (every, every)
    return ref.at[y, high, cores, x, low]


def gather_kernel(
    mine_ref, gain_ref, full_ref, gain_full, swap_send, swap_recv, send_1, recv_1, send_2, recv_2, ring_send, ring_recv, pass_send, pass_recv, own_sem,
    gain_send, gain_recv,
):
    at, core = place()
    partner = device(at, 1 - core)
    enter(at, core, pltpu.get_barrier_semaphore())

    def remote(src, dst, send, recv, peer):
        return pltpu.make_async_remote_copy(
            src_ref=src, dst_ref=dst, send_sem=send, recv_sem=recv, device_id=peer, device_id_type=MESH
        )

    mine = [3 * core + p for p in range(3)]
    theirs = [3 * (1 - core) + p for p in range(3)]
    swaps, owns = [], []
    for p in range(3):
        swaps.append(
            remote(
                mine_ref.at[theirs[p]],
                slab(full_ref, theirs[p], at, core),
                swap_send.at[p],
                swap_recv.at[p],
                partner,
            )
        )
        swaps[-1].start()
        owns.append(
            pltpu.make_async_copy(mine_ref.at[mine[p]], slab(full_ref, mine[p], at, core), own_sem.at[p])
        )
        owns[-1].start()
    owns.append(pltpu.make_async_copy(gain_ref, gain_slab(gain_full, at, core), own_sem.at[3]))
    owns[-1].start()
    for own in owns:
        own.wait()

    def gain_out(phase):
        dim = GAIN_ORDER[phase]
        src = gain_slab(gain_full, {d: at[d] for d in GAIN_ORDER[phase:]}, core)
        for step in range(1, SIZES[dim]):
            k = step - 1
            peer = device(moved(at, dim, step), core)
            sent.append(remote(src, src, gain_send.at[phase, k], gain_recv.at[phase, k], peer))
            sent[-1].start()

    def gain_in(phase):
        dim = GAIN_ORDER[phase]
        for step in range(1, SIZES[dim]):
            k = step - 1
            known = {d: at[d] for d in GAIN_ORDER[phase:]}
            there = gain_slab(gain_full, moved(known, dim, -step), core)
            remote(there, there, gain_send.at[phase, k], gain_recv.at[phase, k], partner).wait_recv()

    swap_in = [
        remote(
            mine_ref.at[mine[p]],
            slab(full_ref, mine[p], at, 1 - core),
            swap_send.at[p],
            swap_recv.at[p],
            partner,
        )
        for p in range(3)
    ]

    def direct(p, dim, known, send, recv):
        src = slab(full_ref, mine[p], known)
        copies = []
        for step in range(1, SIZES[dim]):
            k = step - 1
            copies.append(remote(src, src, send.at[p, k], recv.at[p, k], device(moved(at, dim, step), core)))
            copies[-1].start()
        return copies

    def arrived(p, dim, known, send, recv):
        for step in range(1, SIZES[dim]):
            k = step - 1
            there = slab(full_ref, mine[p], moved(known, dim, -step))
            remote(there, there, send.at[p, k], recv.at[p, k], partner).wait_recv()

    sent = []
    gain_out(0)
    for p in range(3):
        swap_in[p].wait_recv()
        sent += direct(p, ORDERS[p][0], at, send_1, recv_1)
    for p in range(3):
        a, b, c = ORDERS[p]
        arrived(p, a, at, send_1, recv_1)
        known = {b: at[b], c: at[c]}
        sent += direct(p, b, known, send_2, recv_2)
    gain_in(0)
    gain_out(1)

    sign = 1 - 2 * core
    ways = ((0, sign), (1, -sign))

    def piece(p, where, h):
        return slab(full_ref, mine[p], {ORDERS[p][2]: where}, h)

    def hop(p, way, step, h):
        dim = ORDERS[p][2]
        direction = ways[way][1]
        return remote(
            piece(p, moved(at, dim, -direction * step)[dim], h),
            piece(p, moved(at, dim, -direction * step)[dim], h),
            ring_send.at[p, way, step, h],
            ring_recv.at[p, way, step, h],
            device(moved(at, dim, direction), core),
        )

    def arriving(p, way, step, h):
        dim = ORDERS[p][2]
        where = moved(at, dim, -ways[way][1] * (step + 1))[dim]
        return remote(
            piece(p, where, h), piece(p, where, h), ring_send.at[p, way, step, h], ring_recv.at[p, way, step, h], partner
        )

    def pass_on(p, where, slot):
        copy = remote(
            slab(full_ref, mine[p], {ORDERS[p][2]: where}),
            slab(full_ref, mine[p], {ORDERS[p][2]: where}),
            pass_send.at[p, slot],
            pass_recv.at[p, slot],
            partner,
        )
        copy.start()
        return copy

    def steps_of(p, way):
        return SIZES[ORDERS[p][2]] // 2 - way

    for p in range(3):
        a, b, c = ORDERS[p]
        arrived(p, b, {b: at[b], c: at[c]}, send_2, recv_2)
        for h in range(HALVES):
            for way in range(2):
                copy = hop(p, way, 0, h)
                copy.start()
                sent.append(copy)
        sent.append(pass_on(p, at[c], 0))
    gain_in(1)
    gain_out(2)
    for step in range(4):
        if step == 1:
            gain_in(2)
            mine_gain = gain_slab(gain_full, {}, core)
            sent.append(remote(mine_gain, mine_gain, gain_send.at[3, 0], gain_recv.at[3, 0], partner))
            sent[-1].start()
        for h in range(HALVES):
            for p in range(3):
                for way in range(2):
                    if step >= steps_of(p, way):
                        continue
                    arriving(p, way, step, h).wait_recv()
                    if step + 1 < steps_of(p, way):
                        copy = hop(p, way, step + 1, h)
                        copy.start()
                        sent.append(copy)
                    if h == HALVES - 1:
                        dim = ORDERS[p][2]
                        where = moved(at, dim, -ways[way][1] * (step + 1))[dim]
                        sent.append(pass_on(p, where, (1 + step if way == 0 else -1 - step) % 8))
    for p in range(3):
        dim = ORDERS[p][2]
        size = SIZES[dim]
        for step in range(size // 2 + 1):
            for way in range(2):
                if (step == 0 and way == 1) or step > steps_of(p, way):
                    continue
                slot = 0 if step == 0 else (step if way == 0 else -step)
                where = moved(at, dim, (ways[way][1]) * step)[dim]
                there = slab(full_ref, theirs[p], {dim: where})
                remote(there, there, pass_send.at[p, slot % 8], pass_recv.at[p, slot % 8], partner).wait_recv()
    their_gain = gain_slab(gain_full, {}, 1 - core)
    remote(their_gain, their_gain, gain_send.at[3, 0], gain_recv.at[3, 0], partner).wait_recv()
    for copy in swaps + sent:
        copy.wait_send()


def gather_weights(tiles, gain_row):
    dma = pltpu.SemaphoreType.DMA
    return pl.pallas_call(
        gather_kernel,
        out_shape=(
            jax.ShapeDtypeStruct((TILES, 8, 4, 2, 4, 2, 8, HD), jnp.bfloat16),
            jax.ShapeDtypeStruct((8, 4, 2, 4, 2, 1, 128), jnp.float32),
        ),
        in_specs=[pl.BlockSpec(memory_space=pltpu.VMEM)] * 2,
        out_specs=(pl.BlockSpec(memory_space=pltpu.VMEM),) * 2,
        scratch_shapes=[
            dma((3,)),
            dma((3,)),
            dma((3, 7)),
            dma((3, 7)),
            dma((3, 7)),
            dma((3, 7)),
            dma((3, 2, 4, HALVES)),
            dma((3, 2, 4, HALVES)),
            dma((3, 8)),
            dma((3, 8)),
            dma((4,)),
            dma((4, 7)),
            dma((4, 7)),
        ],
        compiler_params=pltpu.CompilerParams(collective_id=0, has_side_effects=True, vmem_limit_bytes=48 * 2**20),
        name="gather_weights",
    )(tiles, gain_row)


def remote(src, dst, send, recv, peer):
    return pltpu.make_async_remote_copy(
        src_ref=src, dst_ref=dst, send_sem=send, recv_sem=recv, device_id=peer, device_id_type=MESH
    )


def across(left, right, left_dim, right_dim):
    return lax.dot_general(
        left, right, (((left_dim,), (right_dim,)), ((), ())), preferred_element_type=jnp.float32
    )


CHUNK = 256
CHUNKS = 1024 // CHUNK
BLOCKS = CHUNK // 128


def attention_kernel(
    mixed_ref, cos_ref, sin_ref, cot_ref, attn_ref, back_ref,
    kv, probs, part_out, part_in, kv_send, kv_recv, part_send, part_recv,
):
    i, j = lax.axis_index("inter"), lax.axis_index("intra")
    for block in range(8):
        kv[block] = jnp.zeros((2, 128, HD), jnp.bfloat16)
    barrier = pltpu.get_barrier_semaphore()
    for step in range(1, 8):
        pl.semaphore_signal(barrier, inc=1, device_id=(i, (j + step) % 8), device_id_type=MESH)
    cosine, sine = cos_ref[...], sin_ref[...]

    def turned(x, sign):
        return x * cosine + sign * (pltpu.roll(x, 64, 1) * sine)

    kv[j, 0] = turned(mixed_ref[4], 1.0).astype(jnp.bfloat16)
    kv[j, 1] = mixed_ref[5].astype(jnp.bfloat16)
    scale = HD ** (-0.5)
    queries = [(turned(mixed_ref[h], 1.0) * scale).astype(jnp.bfloat16) for h in range(HEADS)]
    cots = [cot_ref[:, h * HD : (h + 1) * HD] for h in range(HEADS)]
    query = jnp.concatenate(queries, axis=0)
    query_t = jnp.concatenate([q.T for q in queries], axis=1)
    cot = jnp.concatenate(cots, axis=0)
    cot_t = jnp.concatenate([c.T for c in cots], axis=1)
    pl.semaphore_wait(barrier, 7)

    def kv_copy(owner, peer):
        return remote(kv.at[owner], kv.at[owner], kv_send.at[peer], kv_recv.at[owner], (i, peer))

    for peer in range(1, 8):
        @pl.when(j < peer)
        def _():
            kv_copy(j, peer).start()

    flat = HEADS * 128
    row_pos = j * 128 + lax.broadcasted_iota(jnp.int32, (CHUNK, flat), 1) % 128
    key_pos = lax.broadcasted_iota(jnp.int32, (CHUNK, flat), 0)

    def allowed(chunk):
        return key_pos + chunk * CHUNK <= row_pos

    def rows(chunk, which):
        return jnp.concatenate([kv[chunk * BLOCKS + b, which] for b in range(BLOCKS)], axis=0)

    top = jnp.full((1, flat), -1e30, jnp.float32)
    for chunk in range(CHUNKS):
        for b in range(BLOCKS):
            owner = chunk * BLOCKS + b

            @pl.when(owner < j)
            def _():
                kv_copy(owner, j).wait_recv()

        scores = jnp.where(allowed(chunk), across(rows(chunk, 0), query_t, 1, 0), -1e30)
        probs[chunk] = scores
        top = jnp.maximum(top, jnp.max(scores, axis=0, keepdims=True))
    total = jnp.zeros((1, flat), jnp.float32)
    out_t = jnp.zeros((HD, flat), jnp.float32)
    for chunk in range(CHUNKS):
        numbers = jnp.where(allowed(chunk), jnp.exp(probs[chunk] - top), 0.0)
        probs[chunk] = numbers
        total = total + jnp.sum(numbers, axis=0, keepdims=True)
        out_t = out_t + across(rows(chunk, 1), numbers.astype(jnp.bfloat16), 0, 0)
    share = 1.0 / total
    attn_t = (out_t * share).astype(jnp.bfloat16)
    for h in range(HEADS):
        attn_ref[:, h * HD : (h + 1) * HD] = attn_t[:, h * 128 : (h + 1) * 128].T
    delta = jnp.sum(cot_t.astype(jnp.float32) * attn_t.astype(jnp.float32), axis=0, keepdims=True)
    query_grad_t = jnp.zeros((HD, flat), jnp.float32)

    def part_copy(owner, maker):
        return remote(part_out.at[owner], part_in.at[maker], part_send.at[owner], part_recv.at[maker], (i, owner))

    def send_parts(chunk):
        for b in range(BLOCKS):
            owner = chunk * BLOCKS + b

            @pl.when(owner < j)
            def _():
                part_copy(owner, j).start()

    for chunk in range(CHUNKS):
        probs_t = probs[chunk] * share
        probs_grad = across(rows(chunk, 1), cot_t, 1, 0)
        scores_grad = (probs_t * (probs_grad - delta)).astype(jnp.bfloat16)
        query_grad_t = query_grad_t + across(rows(chunk, 0), scores_grad, 0, 0)
        keys_part = across(scores_grad, query, 1, 0).astype(jnp.bfloat16)
        values_part = across(probs_t.astype(jnp.bfloat16), cot, 1, 0).astype(jnp.bfloat16)
        for b in range(BLOCKS):
            part_out[chunk * BLOCKS + b, 0] = keys_part[b * 128 : (b + 1) * 128]
            part_out[chunk * BLOCKS + b, 1] = values_part[b * 128 : (b + 1) * 128]
        if chunk:
            send_parts(chunk - 1)
    send_parts(CHUNKS - 1)
    for h in range(HEADS):
        grad = query_grad_t[:, h * 128 : (h + 1) * 128].T
        back_ref[h] = (turned(grad, -1.0) * scale).astype(jnp.bfloat16)
    part_in[j] = part_out[j]
    keys_grad = jnp.zeros((128, HD), jnp.float32)
    values_grad = jnp.zeros((128, HD), jnp.float32)
    for maker in range(8):
        @pl.when(maker > j)
        def _():
            part_copy(j, maker).wait_recv()

        @pl.when(maker < j)
        def _():
            part_in[maker] = jnp.zeros((2, 128, HD), jnp.bfloat16)

        keys_grad = keys_grad + part_in[maker, 0].astype(jnp.float32)
        values_grad = values_grad + part_in[maker, 1].astype(jnp.float32)
    back_ref[4] = turned(keys_grad, -1.0).astype(jnp.bfloat16)
    back_ref[5] = values_grad.astype(jnp.bfloat16)
    for peer in range(1, 8):
        @pl.when(j < peer)
        def _():
            kv_copy(j, peer).wait_send()

    for owner in range(7):
        @pl.when(owner < j)
        def _():
            part_copy(owner, j).wait_send()


def attention(mixed, cosine, sine, cot):
    dma = pltpu.SemaphoreType.DMA
    vmem = pl.BlockSpec(memory_space=pltpu.VMEM)
    return pl.pallas_call(
        attention_kernel,
        out_shape=(
            jax.ShapeDtypeStruct((128, HEADS * HD), jnp.bfloat16),
            jax.ShapeDtypeStruct((TILES, 128, HD), jnp.bfloat16),
        ),
        in_specs=[vmem] * 4,
        out_specs=(vmem, vmem),
        scratch_shapes=[
            pltpu.VMEM((8, 2, 128, HD), jnp.bfloat16),
            pltpu.VMEM((CHUNKS, CHUNK, HEADS * 128), jnp.float32),
            pltpu.VMEM((8, 2, 128, HD), jnp.bfloat16),
            pltpu.VMEM((8, 2, 128, HD), jnp.bfloat16),
            dma((8,)),
            dma((8,)),
            dma((8,)),
            dma((8,)),
        ],
        compiler_params=pltpu.CompilerParams(collective_id=1, has_side_effects=True, vmem_limit_bytes=32 * 2**20),
        name="attention",
    )(mixed, cosine, sine, cot)


def out_slab(ref, tile, at, cores=slice(None)):
    every = slice(None)
    y, x = at.get("y", every), at.get("x", every)
    high, low = (at["z"] // 2, at["z"] % 2) if "z" in at else (every, every)
    return ref.at[tile, x, low, y, high, cores]


RING_SHAPES = {"x": (2, 8, 4, 8, HD), "y": (4, 2, 4, 8, HD), "z": (4, 8, 8, HD)}


def line_shape(p):
    dim = ORDERS[p][0]
    return {"x": (4, 2, 8, HD), "y": (8, 2, 8, HD), "z": (2, 4, 2, 8, HD)}[dim]


def scatter_kernel(
    turned_ref, back_ref, out_ref,
    other, other_back, part, ring_0, ring_1, ring_2, line_0, line_1, line_2, dot_in, final,
    swap_send, swap_recv, ring_send, ring_recv, send_2, recv_2, send_3, recv_3, last_send, last_recv,
):
    at, core = place()
    partner = device(at, 1 - core)
    enter(at, core, pltpu.get_barrier_semaphore())
    swap = remote(turned_ref, other, swap_send.at[0], swap_recv.at[0], partner)
    swap.start()
    swap_back = remote(back_ref.at[pl.ds(3 * (1 - core), 3)], other_back, swap_send.at[1], swap_recv.at[1], partner)
    swap_back.start()
    mine = [3 * core + p for p in range(3)]
    own = jnp.concatenate([back_ref[m] for m in mine], axis=1)
    swap.wait_recv()
    swap_back.wait_recv()
    theirs = jnp.concatenate([other_back[p] for p in range(3)], axis=1)

    @pl.loop(0, 8)
    def _(k):
        rows = pl.ds(k * 512, 512)
        sums = across(turned_ref[rows, :], own, 1, 0) + across(other[rows, :], theirs, 1, 0)
        for p in range(3):
            part[p, k // 2, k % 2] = (
                sums[:, p * HD : (p + 1) * HD].reshape(8, 4, 2, 8, HD).astype(jnp.bfloat16)
            )

    rings = (ring_0, ring_1, ring_2)
    lines = (line_0, line_1, line_2)
    sign = 1 - 2 * core
    ways = (sign, -sign)
    sent = [swap, swap_back]

    def steps_of(p, way):
        return SIZES[ORDERS[p][2]] // 2 - way

    def ring_copy(p, way, step, h):
        dim = ORDERS[p][2]
        target = moved(at, dim, ways[way] * (steps_of(p, way) - step))[dim]
        return remote(
            out_slab(part, p, {dim: target}, h),
            rings[p].at[way, step, h],
            ring_send.at[p, way, step, h],
            ring_recv.at[p, way, step, h],
            device(moved(at, dim, ways[way]), core),
        )

    def add_to(slab_ref, arrived_ref):
        slab_ref[...] = (slab_ref[...].astype(jnp.float32) + arrived_ref[...].astype(jnp.float32)).astype(jnp.bfloat16)

    for h in range(HALVES):
        for p in range(3):
            for way in range(2):
                sent.append(ring_copy(p, way, 0, h))
                sent[-1].start()
    for step in range(4):
        for h in range(HALVES):
            for p in range(3):
                for way in range(2):
                    if step >= steps_of(p, way):
                        continue
                    dim = ORDERS[p][2]
                    target = moved(at, dim, ways[way] * (steps_of(p, way) - step - 1))[dim]
                    ring_copy(p, way, step, h).wait_recv()
                    add_to(out_slab(part, p, {dim: target}, h), rings[p].at[way, step, h])
                    if step + 1 < steps_of(p, way):
                        sent.append(ring_copy(p, way, step + 1, h))
                        sent[-1].start()
    for p in range(3):
        a, b, c = ORDERS[p]
        for step in range(1, SIZES[b]):
            there = moved(at, b, step)
            sent.append(
                remote(
                    out_slab(part, p, {b: there[b], c: at[c]}),
                    lines[p].at[step - 1],
                    send_2.at[p, step - 1],
                    recv_2.at[p, step - 1],
                    device(there, core),
                )
            )
            sent[-1].start()
    for p in range(3):
        a, b, c = ORDERS[p]
        here = out_slab(part, p, {b: at[b], c: at[c]})
        total = here[...].astype(jnp.float32)
        for step in range(1, SIZES[b]):
            remote(here, lines[p].at[step - 1], send_2.at[p, step - 1], recv_2.at[p, step - 1], partner).wait_recv()
            total = total + lines[p][step - 1].astype(jnp.float32)
        here[...] = total.astype(jnp.bfloat16)
        for step in range(1, SIZES[a]):
            there = moved(at, a, step)
            sent.append(
                remote(
                    out_slab(part, p, there),
                    dot_in.at[p, step - 1],
                    send_3.at[p, step - 1],
                    recv_3.at[p, step - 1],
                    device(there, core),
                )
            )
            sent[-1].start()
    for p in range(3):
        a, b, c = ORDERS[p]
        here = out_slab(part, p, at)
        total = here[...].astype(jnp.float32)
        for step in range(1, SIZES[a]):
            remote(here, dot_in.at[p, step - 1], send_3.at[p, step - 1], recv_3.at[p, step - 1], partner).wait_recv()
            total = total + dot_in[p, step - 1].astype(jnp.float32)
        final[p] = total
    lasts = [
        remote(final.at[p, 1 - core], out_ref.at[mine[p]], last_send.at[p], last_recv.at[p], partner) for p in range(3)
    ]
    for p in range(3):
        lasts[p].start()
    for p in range(3):
        out_ref[mine[p]] = final[p, core]
    for p in range(3):
        tile = 3 * (1 - core) + p
        remote(final.at[p, core], out_ref.at[tile], last_send.at[p], last_recv.at[p], partner).wait_recv()
    for copy in sent + lasts:
        copy.wait_send()


def scatter_sums(turned, back):
    dma = pltpu.SemaphoreType.DMA
    vmem = pl.BlockSpec(memory_space=pltpu.VMEM)

    def rings(p):
        dim = ORDERS[p][2]
        return pltpu.VMEM((2, SIZES[dim] // 2, HALVES, *RING_SHAPES[dim]), jnp.bfloat16)

    def lines(p):
        return pltpu.VMEM((SIZES[ORDERS[p][1]] - 1, *line_shape(p)), jnp.bfloat16)

    return pl.pallas_call(
        scatter_kernel,
        out_shape=jax.ShapeDtypeStruct((TILES, 8, HD), jnp.float32),
        in_specs=[vmem] * 2,
        out_specs=vmem,
        scratch_shapes=[
            pltpu.VMEM((4096, 128), jnp.bfloat16),
            pltpu.VMEM((3, 128, HD), jnp.bfloat16),
            pltpu.VMEM((3, 4, 2, 8, 4, 2, 8, HD), jnp.bfloat16),
            *[rings(p) for p in range(3)],
            *[lines(p) for p in range(3)],
            pltpu.VMEM((3, 7, 2, 8, HD), jnp.bfloat16),
            pltpu.VMEM((3, 2, 8, HD), jnp.float32),
            dma((2,)),
            dma((2,)),
            dma((3, 2, 4, HALVES)),
            dma((3, 2, 4, HALVES)),
            dma((3, 7)),
            dma((3, 7)),
            dma((3, 7)),
            dma((3, 7)),
            dma((3,)),
            dma((3,)),
        ],
        compiler_params=pltpu.CompilerParams(collective_id=2, has_side_effects=True, vmem_limit_bytes=32 * 2**20),
        name="scatter_sums",
    )(turned, back)


def rope_tables(first_position):
    freqs = rope_base ** (-jnp.arange(HD // 2, dtype=jnp.float32) / (HD // 2))
    positions = first_position + jnp.arange(128, dtype=jnp.int32)
    angles = positions.astype(jnp.float32)[:, None] * freqs[None, :]
    cosine, sine = jnp.cos(angles), jnp.sin(angles)
    return jnp.concatenate([cosine, cosine], axis=1), jnp.concatenate([-sine, sine], axis=1)


def local(hidden_in, norm_gain, qkv_weight, attn_cotangent):
    rows_in = hidden_in[0]
    tokens, width = rows_in.shape
    i, j = lax.axis_index("inter"), lax.axis_index("intra")
    tiles = jnp.moveaxis(qkv_weight.reshape(8, TILES, HD), 1, 0)
    lane = jnp.arange(128)
    gain_row = jnp.where(lane // 8 == (i * 8 + j) % 16, jnp.tile(norm_gain.astype(jnp.float32), 16), 0.0)[None]
    weight, gain = gather_weights(tiles, gain_row)
    weight = weight.reshape(TILES, width, HD)
    gain = gain.reshape(32, 16, 128).sum(axis=1).reshape(width)
    cosine, sine = rope_tables(j * tokens)
    wide_rows = rows_in.astype(jnp.float32)
    inv_rms = lax.rsqrt(jnp.mean(wide_rows * wide_rows, axis=1, keepdims=True) + eps_norm)
    unit = (wide_rows * inv_rms * gain[None, :]).astype(jnp.bfloat16)
    mixed = jnp.stack([jnp.dot(unit, weight[n], preferred_element_type=jnp.float32) for n in range(TILES)])
    attn, back = attention(mixed, cosine, sine, attn_cotangent[0])
    unit_t = unit.T
    plain_grad = jnp.moveaxis(scatter_sums(unit_t, back), 0, 1).reshape(8, TILES * HD)
    scaled_grad = sum(
        lax.dot_general(back[n], weight[n], (((1,), (1,)), ((), ())), preferred_element_type=jnp.float32)
        for n in range(TILES)
    )
    scaled_grad = scaled_grad * gain[None, :]
    inner = jnp.sum(scaled_grad * wide_rows, axis=1, keepdims=True)
    grad_rows = (scaled_grad * inv_rms - wide_rows * inv_rms**3 / width * inner).astype(jnp.bfloat16)
    start = j * 512 + i * 8
    weight_here = lax.dynamic_slice_in_dim(weight, start, 8, 1).astype(jnp.float32)
    weight_here = jnp.moveaxis(weight_here, 0, 1).reshape(8, TILES * HD)
    gain_here = lax.dynamic_slice_in_dim(gain, start, 8, 0)
    gain_grad = jnp.sum(plain_grad * weight_here, axis=1) / gain_here
    return (attn[None], grad_rows[None], plain_grad, gain_grad)


def solution(mesh):
    return jax.shard_map(
        local,
        mesh=mesh,
        in_specs=(
            P("inter", "intra", None),
            P(("inter", "intra")),
            P(("inter", "intra"), None),
            P("inter", "intra", None),
        ),
        out_specs=(
            P("inter", "intra", None),
            P("inter", "intra", None),
            P(("intra", "inter"), None),
            P(("intra", "inter")),
        ),
        check_vma=False,
    )
```

time: 260 us -> 146 us (0.56)
  blocking collectives: 70.8 us -> 0 us
  Pallas kernels: 56.3 us -> 123 us
  starting transfers between devices: 29.6 us -> 0 us
  waiting for transfers between devices: 27.7 us -> 0 us
  matrix products: 27.3 us -> 9.39 us
  between operations: 14.4 us -> 0.83 us
  other arithmetic: 14.9 us -> 3.36 us
  local copies, waits for them, and re-layouts: 17.7 us -> 9.35 us
    all_gather x2 -> x0, blocking collectives: 70.8 us -> none  [the longest x1 48.4 us: in_one_piece(): lax.all_gather(both, axis, axis=dim, tiled=True)]
    pallas_call x1 -> x3, Pallas kernels: 56.3 us -> 123 us  [the longest x1 56.4 us: gather_weights(): pl.pallas_call(gather_kernel, out_shape=(jax.ShapeDtypeStruct((TILES, 8,...]
    all_to_all x3 -> x0, waiting for transfers between devices: 18.7 us -> none  [the longest x1 18.7 us: summed_on_arrival_2(): tiles = lax.all_to_all(split_up(x, dim, size), axis, 0, 0, tiled=True)]
    dot_general x9 -> x12, matrix products: 27.3 us -> 9.39 us  [the longest x6 6.44 us: local(): jnp.dot(unit, weight[n], preferred_element_type=jnp.float32)]
    all_to_all x3 -> x0, starting transfers between devices: 17 us -> none  [the longest x1 8.16 us: summed_on_arrival_2(): tiles = lax.all_to_all(split_up(x, dim, size), axis, 0, 0, tiled=True)]
    ppermute x1 -> x0, starting transfers between devices: 12.6 us -> none  [gain_of_outputs(): lax.ppermute(norm_gain, ('inter', 'intra'), pairs).astype(jnp.float32)]
    ppermute x1 -> x0, waiting for transfers between devices: 9.01 us -> none  [gain_of_outputs(): lax.ppermute(norm_gain, ('inter', 'intra'), pairs).astype(jnp.float32)]
    reshape x2 -> x0, local copies, waits for them, and re-layouts: 8.95 us -> none  [the longest x1 8.86 us: local(): weight_tiles = gather_weights(tiles).reshape(TILES, width, HD)]
  transfers between devices with their start and end apart: 5 -> 0, of which waited for: 2 -> 0; matrix products, arithmetic and copies ran while one was open for 13% -> 0% of each run, Pallas kernels for 0% -> 0%
where the time goes in v2:
time: 146 us
  Pallas kernels  123 us (84%)
  matrix products  9.39 us (6%)
  local copies, waits for them, and re-layouts  9.35 us (6%)
  other arithmetic  3.36 us (2%)
    pallas_call x1, Pallas kernels, gather_weights(): pl.pallas_call(gather_kernel, out_shape=(jax.ShapeDtypeStruct((TILES, 8,...  56.4 us
    pallas_call x1, Pallas kernels, scatter_sums(): pl.pallas_call(scatter_kernel, out_shape=jax.ShapeDtypeStruct((TILES, 8,...  47.6 us
    pallas_call x1, Pallas kernels, attention(): pl.pallas_call(attention_kernel, out_shape=(jax.ShapeDtypeStruct((128, HE...  19.2 us
    dot_general x6, matrix products, local(): jnp.dot(unit, weight[n], preferred_element_type=jnp.float32)  6.44 us
    slice x1, local copies, waits for them, and re-layouts, local(): weight[n]  4.41 us
    unnamed x8, local copies, waits for them, and re-layouts  4.19 us
    dot_general x6, matrix products, local(): lax.dot_general(back[n], weight[n], (((1,), (1,)), ((), ())), preferred_e...  2.95 us

profile of v2, /device:TPU:1, one launch (start us, length us, event | category | flops | bytes accessed | tf_op | source)
XLA Modules:
  0.0 146.1 jit_solution(13402711747419977382)
XLA Ops:
  0.6 0.0 copy-start.1
  0.7 0.7 tile.4
  1.3 0.1 tile.10
  1.4 0.3 fusion.37
  1.8 0.1 pad_maximum_fusion
  1.9 1.6 %copy.16 = bf16[1,128,4096]{1,2,0:T(8,128)(2,1)S(1)} copy(bf16[1,128,4096]{2,1,0:T(8,128)(2,1)} %param.4) | data formatting | bytes 2097152 | tf_op args[0]
  3.5 0.6 fusion.5
  4.1 0.0 copy-done.1
  4.1 56.4 %gather_weights.1 = (bf16[6,8,4,2,4,2,8,128]{7,6,5,4,3,2,1,0:T(8,128)(2,1)}, f32[8,4,2,4,2,1,128]{6,5,4,3,2,1,0:T(1,128)S(1)}) custom-call(bf16[6,8,128]{2,1,0:T(8,128)(2,1)S(1)} %bitcast.120, f32[1,128]{1,0:T(1,128)S(1)} %compare_select_fusion.gain_ref), custom_call_target="tpu_custom_call" | custom-call | tf_op jit(solution)/shard_map/gather_weights/pallas_call | solution.py:241
  60.5 0.2 reduce_sum.37
  60.7 4.4 %fusion.44 = (bf16[1,8,4,2,4,2,8,128]{7,6,5,4,3,2,1,0:T(8,128)(2,1)S(1)}, bf16[1,8,4,2,4,2,8,128]{7,6,5,4,3,2,1,0:T(8,128)(2,1)S(1)}, bf16[1,8,4,2,4,2,8,128]{7,...) fusion(bf16[6,8,4,2,4,2,8,128]{7,6,5,4,3,2,1,0:T(8,128)(2,1)} %, ...), kind=kLoop, calls=%fused_computation.67 | loop fusion | bytes 12582912 | tf_op jit(solution)/shard_map/slice | solution.py:637
  65.1 1.1 fusion.19
  66.2 1.1 fusion.18
  67.3 1.1 fusion.17
  68.4 1.1 fusion.16
  69.4 0.0 copy-start
  69.4 1.1 fusion.15
  70.5 1.1 fusion.14.mixed_ref
  71.6 0.0 copy-done
  71.6 19.2 %attention.1 = (bf16[128,512]{1,0:T(8,128)(2,1)S(1)}, bf16[6,128,128]{2,1,0:T(8,128)(2,1)S(1)}) custom-call(f32[6,128,128]{2,1,0:T(8,128)S(1)} %fusion.14.mixed_ref, f32[128,128]{1,0:T(8,128)S(1)} %get-tuple-element.35.cos_ref, f32[128,128]{1,0:T(8,128)S(1)} %get-tuple-element.36.sin_ref, bf16[128,512]{1,0:T(8,128)(2,1)S(1)} %bitcast.118), custom_call_target="tpu_custom_call" | custom-call | tf_op jit(solution)/shard_map/attention/pallas_call | solution.py:413
  90.8 0.4 fusion.28
  91.3 0.4 convolution_add_fusion.4
  91.7 0.4 convolution_add_fusion.3
  92.1 0.4 convolution_add_fusion.2
  92.6 0.4 convolution_add_fusion.1
  93.0 0.8 fusion.9
  93.8 0.8 fusion.21
  94.6 47.6 %scatter_sums.1 = f32[6,8,128]{2,1,0:T(8,128)S(1)} custom-call(bf16[4096,128]{1,0:T(8,128)(2,1)S(1)} %get-tuple-element.26.turned_ref, bf16[6,128,128]{2,1,0:T(8,128)(2,1)S(1)} %get-tuple-element.11.back_ref), custom_call_target="tpu_custom_call" | custom-call | tf_op jit(solution)/shard_map/scatter_sums/pallas_call | solution.py:586
  142.1 0.8 fusion.36
  143.0 0.6 dynamic-slice_divide_fusion
  143.6 1.3 copy.23
  144.9 0.7 copy.37
  145.5 0.6 copy.38
  (5 shorter events, 0.0 us)
Async XLA Ops:
  0.6 3.4 %copy-start.1 = (bf16[8,768]{1,0:T(8,128)(2,1)S(1)}, bf16[8,768]{1,0:T(8,128)(2,1)}, u32[]{:S(2)}) copy-start(bf16[8,768]{1,0:T(8,128)(2,1)} %param.6) | copy-start | bytes 36868
  69.4 2.2 %copy-start = (bf16[1,128,512]{2,1,0:T(8,128)(2,1)S(1)}, bf16[1,128,512]{2,1,0:T(8,128)(2,1)}, u32[]{:S(2)}) copy-start(bf16[1,128,512]{2,1,0:T(8,128)(2,1)} %param.7) | copy-start | bytes 393220

commit v3 on v0

v3 whole, which is shorter than its diff:
```python
import functools

import jax
import jax.numpy as jnp
from jax import lax
from jax.experimental import pallas as pl
from jax.experimental.pallas import tpu as pltpu
from jax.sharding import PartitionSpec as P

HD = 128
HEADS = 4
TILES = HEADS + 2
WIDTH = 4096
MESH = pl.DeviceIdType.MESH
SIZES = {"x": 4, "y": 8, "z": 8}
ORDERS = (("z", "y", "x"), ("x", "z", "y"), ("y", "x", "z"))
HALVES = 2
GAIN_ORDER = ("z", "y", "x")
CHUNK = 256
CHUNKS = 1024 // CHUNK
BLOCKS = CHUNK // 128
FLAT = HEADS * 128

eps_norm = 1e-05
rope_base = 500000.0


def place():
    i, j = lax.axis_index("inter"), lax.axis_index("intra")
    return {"x": j // 2, "y": i // 8, "z": ((i // 2) % 4) * 2 + j % 2}, i % 2


def device(at, core):
    return ((at["y"] * 4 + at["z"] // 2) * 2 + core, at["x"] * 2 + at["z"] % 2)


def moved(at, dim, step):
    size = SIZES[dim]
    return {**at, dim: (at[dim] + step + size) % size}


def indices(at):
    every = slice(None)
    y, x = at.get("y", every), at.get("x", every)
    high, low = (at["z"] // 2, at["z"] % 2) if "z" in at else (every, every)
    return y, high, x, low


def slab(ref, tile, at, cores=slice(None)):
    y, high, x, low = indices(at)
    return ref.at[tile, y, high, cores, x, low]


def gain_slab(ref, at, cores):
    y, high, x, low = indices(at)
    return ref.at[y, high, cores, x, low]


def out_slab(ref, tile, at, cores=slice(None)):
    y, high, x, low = indices(at)
    return ref.at[tile, x, low, y, high, cores]


def remote(src, dst, send, recv, peer):
    return pltpu.make_async_remote_copy(
        src_ref=src, dst_ref=dst, send_sem=send, recv_sem=recv, device_id=peer, device_id_type=MESH
    )


def across(left, right, left_dim, right_dim):
    return lax.dot_general(
        left, right, (((left_dim,), (right_dim,)), ((), ())), preferred_element_type=jnp.float32
    )


def steps_of(p, way):
    return SIZES[ORDERS[p][2]] // 2 - way


def greet(at, core, barrier):
    i, j = lax.axis_index("inter"), lax.axis_index("intra")
    peers = [device(at, 1 - core)]
    for dim, size in SIZES.items():
        peers += [device(moved(at, dim, step), core) for step in range(1, size)]
    peers += [(i, (j + step) % 8) for step in range(1, 8)]
    for peer in peers:
        pl.semaphore_signal(barrier, inc=1, device_id=peer, device_id_type=MESH)
    return len(peers)


class Gather:
    def __init__(self, at, core, mine_ref, gain_ref, full, gain_full, sems, sent):
        self.at, self.core, self.partner = at, core, device(at, 1 - core)
        self.mine_ref, self.gain_ref, self.full, self.gain_full = mine_ref, gain_ref, full, gain_full
        (self.swap, self.one, self.two, self.ring, self.passing, self.gains, self.own) = sems
        self.mine = [3 * core + p for p in range(3)]
        self.theirs = [3 * (1 - core) + p for p in range(3)]
        sign = 1 - 2 * core
        self.ways = (sign, -sign)
        self.sent = sent

    def go(self, copy):
        copy.start()
        self.sent.append(copy)

    def begin(self):
        at, core, full = self.at, self.core, self.full
        owns = []
        for p in range(3):
            self.go(
                remote(
                    self.mine_ref.at[self.theirs[p]],
                    slab(full, self.theirs[p], at, core),
                    self.swap.at[0, p],
                    self.swap.at[1, p],
                    self.partner,
                )
            )
            owns.append(
                pltpu.make_async_copy(self.mine_ref.at[self.mine[p]], slab(full, self.mine[p], at, core), self.own.at[p])
            )
        owns.append(pltpu.make_async_copy(self.gain_ref, gain_slab(self.gain_full, at, core), self.own.at[3]))
        for own in owns:
            own.start()
        for own in owns:
            own.wait()
        for p in (1, 2, 0):
            there = slab(full, self.mine[p], at, 1 - core)
            remote(there, there, self.swap.at[0, p], self.swap.at[1, p], self.partner).wait_recv()
            self.direct(p, 0)
        self.gain_out(0)

    def direct(self, p, phase):
        dim = ORDERS[p][phase]
        sems = (self.one, self.two)[phase]
        src = slab(self.full, self.mine[p], {d: self.at[d] for d in ORDERS[p][phase:]})
        for step in range(1, SIZES[dim]):
            peer = device(moved(self.at, dim, step), self.core)
            self.go(remote(src, src, sems.at[0, p, step - 1], sems.at[1, p, step - 1], peer))

    def arrived(self, p, phase):
        dim = ORDERS[p][phase]
        sems = (self.one, self.two)[phase]
        known = {d: self.at[d] for d in ORDERS[p][phase:]}
        for step in range(1, SIZES[dim]):
            there = slab(self.full, self.mine[p], moved(known, dim, -step))
            remote(there, there, sems.at[0, p, step - 1], sems.at[1, p, step - 1], self.partner).wait_recv()

    def gain_out(self, phase):
        dim = GAIN_ORDER[phase]
        src = gain_slab(self.gain_full, {d: self.at[d] for d in GAIN_ORDER[phase:]}, self.core)
        for step in range(1, SIZES[dim]):
            peer = device(moved(self.at, dim, step), self.core)
            self.go(remote(src, src, self.gains.at[0, phase, step - 1], self.gains.at[1, phase, step - 1], peer))

    def gain_in(self, phase):
        dim = GAIN_ORDER[phase]
        known = {d: self.at[d] for d in GAIN_ORDER[phase:]}
        for step in range(1, SIZES[dim]):
            there = gain_slab(self.gain_full, moved(known, dim, -step), self.core)
            remote(
                there, there, self.gains.at[0, phase, step - 1], self.gains.at[1, phase, step - 1], self.partner
            ).wait_recv()

    def gain_pass(self):
        whole = gain_slab(self.gain_full, {}, self.core)
        self.go(remote(whole, whole, self.gains.at[0, 3, 0], self.gains.at[1, 3, 0], self.partner))

    def gain_passed(self):
        whole = gain_slab(self.gain_full, {}, 1 - self.core)
        remote(whole, whole, self.gains.at[0, 3, 0], self.gains.at[1, 3, 0], self.partner).wait_recv()

    def where(self, p, way, step):
        dim = ORDERS[p][2]
        return moved(self.at, dim, -self.ways[way] * step)[dim]

    def hop(self, p, way, step, h):
        dim = ORDERS[p][2]
        piece = slab(self.full, self.mine[p], {dim: self.where(p, way, step)}, h)
        peer = device(moved(self.at, dim, self.ways[way]), self.core)
        self.go(remote(piece, piece, self.ring.at[0, p, way, step, h], self.ring.at[1, p, way, step, h], peer))

    def pass_on(self, p, where, slot):
        piece = slab(self.full, self.mine[p], {ORDERS[p][2]: where})
        self.go(remote(piece, piece, self.passing.at[0, p, slot], self.passing.at[1, p, slot], self.partner))

    def ring_start(self, p):
        for h in range(HALVES):
            for way in range(2):
                self.hop(p, way, 0, h)
        self.pass_on(p, self.at[ORDERS[p][2]], 0)

    def ring_step(self, p, step):
        dim = ORDERS[p][2]
        for h in range(HALVES):
            for way in range(2):
                if step >= steps_of(p, way):
                    continue
                piece = slab(self.full, self.mine[p], {dim: self.where(p, way, step + 1)}, h)
                remote(
                    piece, piece, self.ring.at[0, p, way, step, h], self.ring.at[1, p, way, step, h], self.partner
                ).wait_recv()
                if step + 1 < steps_of(p, way):
                    self.hop(p, way, step + 1, h)
                if h == HALVES - 1:
                    self.pass_on(p, self.where(p, way, step + 1), 1 + step if way == 0 else 7 - step)

    def passed(self):
        for p in range(3):
            dim = ORDERS[p][2]
            for way in range(2):
                for step in range(way, steps_of(p, way) + 1):
                    slot = (step if way == 0 else 8 - step) % 8
                    where = moved(self.at, dim, self.ways[way] * step)[dim]
                    piece = slab(self.full, self.theirs[p], {dim: where})
                    remote(
                        piece, piece, self.passing.at[0, p, slot], self.passing.at[1, p, slot], self.partner
                    ).wait_recv()


RING_SHAPES = {"x": (2, 8, 4, 8, HD), "y": (4, 2, 4, 8, HD), "z": (4, 8, 8, HD)}
LINE_SHAPES = {"x": (4, 2, 8, HD), "y": (8, 2, 8, HD), "z": (2, 4, 2, 8, HD)}


class Scatter:
    def __init__(self, at, core, part, rings, lines, dot_in, final, total_ref, sems, sent):
        self.at, self.core, self.partner = at, core, device(at, 1 - core)
        self.part, self.rings, self.lines, self.dot_in = part, rings, lines, dot_in
        self.final, self.total_ref = final, total_ref
        self.ring, self.two, self.three, self.last = sems
        sign = 1 - 2 * core
        self.ways = (sign, -sign)
        self.sent = sent

    def go(self, copy):
        copy.start()
        self.sent.append(copy)

    def target(self, p, way, left):
        dim = ORDERS[p][2]
        return {dim: moved(self.at, dim, self.ways[way] * left)[dim]}

    def copy(self, p, way, step, h):
        dim = ORDERS[p][2]
        return remote(
            out_slab(self.part, p, self.target(p, way, steps_of(p, way) - step), h),
            self.rings[p].at[way, step, h],
            self.ring.at[0, p, way, step, h],
            self.ring.at[1, p, way, step, h],
            device(moved(self.at, dim, self.ways[way]), self.core),
        )

    def ring_start(self, p):
        for h in range(HALVES):
            for way in range(2):
                self.go(self.copy(p, way, 0, h))

    def ring_step(self, p, step):
        for h in range(HALVES):
            for way in range(2):
                if step >= steps_of(p, way):
                    continue
                self.copy(p, way, step, h).wait_recv()
                here = out_slab(self.part, p, self.target(p, way, steps_of(p, way) - step - 1), h)
                there = self.rings[p].at[way, step, h]
                here[...] = (here[...].astype(jnp.float32) + there[...].astype(jnp.float32)).astype(jnp.bfloat16)
                if step + 1 < steps_of(p, way):
                    self.go(self.copy(p, way, step + 1, h))

    def lines_out(self, p):
        a, b, c = ORDERS[p]
        for step in range(1, SIZES[b]):
            there = moved(self.at, b, step)
            self.go(
                remote(
                    out_slab(self.part, p, {b: there[b], c: self.at[c]}),
                    self.lines[p].at[step - 1],
                    self.two.at[0, p, step - 1],
                    self.two.at[1, p, step - 1],
                    device(there, self.core),
                )
            )

    def dots_out(self, p):
        a, b, c = ORDERS[p]
        here = out_slab(self.part, p, {b: self.at[b], c: self.at[c]})
        total = here[...].astype(jnp.float32)
        for step in range(1, SIZES[b]):
            remote(
                here, self.lines[p].at[step - 1], self.two.at[0, p, step - 1], self.two.at[1, p, step - 1], self.partner
            ).wait_recv()
            total = total + self.lines[p][step - 1].astype(jnp.float32)
        here[...] = total.astype(jnp.bfloat16)
        for step in range(1, SIZES[a]):
            there = moved(self.at, a, step)
            self.go(
                remote(
                    out_slab(self.part, p, there),
                    self.dot_in.at[p, step - 1],
                    self.three.at[0, p, step - 1],
                    self.three.at[1, p, step - 1],
                    device(there, self.core),
                )
            )

    def finish(self, p):
        a = ORDERS[p][0]
        here = out_slab(self.part, p, self.at)
        total = here[...].astype(jnp.float32)
        for step in range(1, SIZES[a]):
            remote(
                here, self.dot_in.at[p, step - 1], self.three.at[0, p, step - 1], self.three.at[1, p, step - 1], self.partner
            ).wait_recv()
            total = total + self.dot_in[p, step - 1].astype(jnp.float32)
        self.final[p] = total
        tile = 3 * self.core + p
        self.total_ref[tile] = self.final[p, self.core]
        self.go(
            remote(
                self.final.at[p, 1 - self.core], self.total_ref.at[tile], self.last.at[0, p], self.last.at[1, p], self.partner
            )
        )

    def finished(self, p):
        tile = 3 * (1 - self.core) + p
        remote(
            self.final.at[p, 0], self.total_ref.at[tile], self.last.at[0, p], self.last.at[1, p], self.partner
        ).wait_recv()


def whole_kernel(
    hidden_ref, mine_ref, gain_ref, cos_ref, sin_ref, cot_ref,
    attn_ref, grad_in_ref, weight_grad_ref, gain_grad_ref,
    full, gain_full, gain_row, normed, turned_own, turned_other,
    kv, probs, part_out, part_in, back, back_other, plain,
    part, ring_0, ring_1, ring_2, line_0, line_1, line_2, dot_in, final, total_ref,
    g_swap, g_one, g_two, g_ring, g_pass, g_gain, g_own,
    kv_sem, part_sem, swap_sem, s_ring, s_two, s_three, s_last,
):
    i, j = lax.axis_index("inter"), lax.axis_index("intra")
    at, core = place()
    partner = device(at, 1 - core)
    sent = []
    barrier = pltpu.get_barrier_semaphore()
    for block in range(8):
        kv[block] = jnp.zeros((2, 128, HD), jnp.bfloat16)
    count = greet(at, core, barrier)
    squares = jnp.zeros((128, 128), jnp.float32)
    for t in range(WIDTH // 128):
        tile = hidden_ref[:, t * 128 : (t + 1) * 128].astype(jnp.float32)
        squares = squares + tile * tile
    inv_rms = lax.rsqrt(jnp.sum(squares, axis=1, keepdims=True) / WIDTH + eps_norm)
    cosine, sine = cos_ref[...], sin_ref[...]
    cots = [cot_ref[:, h * HD : (h + 1) * HD] for h in range(HEADS)]
    pl.semaphore_wait(barrier, count)

    g = Gather(
        at, core, mine_ref, gain_ref, full, gain_full, (g_swap, g_one, g_two, g_ring, g_pass, g_gain, g_own), sent
    )
    g.begin()
    for p in (1, 2, 0):
        g.arrived(p, 0)
        g.direct(p, 1)
    g.gain_in(0)
    g.gain_out(1)
    for p in (2, 1):
        g.arrived(p, 1)
        g.ring_start(p)
    g.gain_in(1)
    g.gain_out(2)
    g.ring_step(2, 0)
    g.ring_step(1, 0)
    g.arrived(0, 1)
    g.ring_start(0)
    g.gain_in(2)
    g.gain_pass()
    g.ring_step(2, 1)
    g.ring_step(1, 1)
    g.gain_passed()
    for y in range(8):
        for z in range(4):
            t = y * 4 + z
            gain_row[:, t * 128 : (t + 1) * 128] = jnp.sum(gain_full[y, z], axis=(0, 1, 2))
    for t in range(WIDTH // 128):
        cols = slice(t * 128, (t + 1) * 128)
        unit = hidden_ref[:, cols].astype(jnp.float32) * inv_rms * gain_row[:, cols]
        normed[:, cols] = unit.astype(jnp.bfloat16)
    g.ring_step(0, 0)
    g.ring_step(2, 2)
    g.ring_step(1, 2)
    for t in range(WIDTH // 128):
        cols = slice(t * 128, (t + 1) * 128)
        turned_own[cols, :] = normed[:, cols].T
    g.ring_step(0, 1)
    g.ring_step(2, 3)
    g.ring_step(1, 3)
    swap = remote(turned_own, turned_other, swap_sem.at[0, 0], swap_sem.at[1, 0], partner)
    swap.start()
    g.passed()

    def weight_rows(pair, y):
        return jnp.concatenate([full[2 * pair + k, y].reshape(512, HD) for k in range(2)], axis=1)

    def mixed_pair(pair):
        total = jnp.zeros((128, 2 * HD), jnp.float32)
        for y in range(8):
            total = total + across(normed[:, y * 512 : (y + 1) * 512], weight_rows(pair, y), 1, 0)
        return total[:, :HD], total[:, HD:]

    def rotated(x, sign):
        return x * cosine + sign * (pltpu.roll(x, 64, 1) * sine)

    keys_in, values_in = mixed_pair(2)
    kv[j, 0] = rotated(keys_in, 1.0).astype(jnp.bfloat16)
    kv[j, 1] = values_in.astype(jnp.bfloat16)

    def kv_copy(owner, peer):
        return remote(kv.at[owner], kv.at[owner], kv_sem.at[0, peer], kv_sem.at[1, owner], (i, peer))

    for peer in range(1, 8):
        @pl.when(j < peer)
        def _():
            kv_copy(j, peer).start()

    scale = HD ** (-0.5)
    heads = [*mixed_pair(0), *mixed_pair(1)]
    queries = [(rotated(head, 1.0) * scale).astype(jnp.bfloat16) for head in heads]
    query = jnp.concatenate(queries, axis=0)
    query_t = jnp.concatenate([q.T for q in queries], axis=1)
    cot = jnp.concatenate(cots, axis=0)
    cot_t = jnp.concatenate([c.T for c in cots], axis=1)
    row_pos = j * 128 + lax.broadcasted_iota(jnp.int32, (CHUNK, FLAT), 1) % 128
    key_pos = lax.broadcasted_iota(jnp.int32, (CHUNK, FLAT), 0)

    def allowed(chunk):
        return key_pos + chunk * CHUNK <= row_pos

    def rows(chunk, which):
        return jnp.concatenate([kv[chunk * BLOCKS + b, which] for b in range(BLOCKS)], axis=0)

    top = jnp.full((1, FLAT), -1e30, jnp.float32)
    for chunk in range(CHUNKS):
        for b in range(BLOCKS):
            owner = chunk * BLOCKS + b

            @pl.when(owner < j)
            def _():
                kv_copy(owner, j).wait_recv()

        scores = jnp.where(allowed(chunk), across(rows(chunk, 0), query_t, 1, 0), -1e30)
        probs[chunk] = scores
        top = jnp.maximum(top, jnp.max(scores, axis=0, keepdims=True))
    total = jnp.zeros((1, FLAT), jnp.float32)
    out_t = jnp.zeros((HD, FLAT), jnp.float32)
    for chunk in range(CHUNKS):
        numbers = jnp.where(allowed(chunk), jnp.exp(probs[chunk] - top), 0.0)
        probs[chunk] = numbers
        total = total + jnp.sum(numbers, axis=0, keepdims=True)
        out_t = out_t + across(rows(chunk, 1), numbers.astype(jnp.bfloat16), 0, 0)
    share = 1.0 / total
    attn_t = (out_t * share).astype(jnp.bfloat16)
    delta = jnp.sum(cot_t.astype(jnp.float32) * attn_t.astype(jnp.float32), axis=0, keepdims=True)
    query_grad_t = jnp.zeros((HD, FLAT), jnp.float32)

    def part_copy(owner, maker):
        return remote(part_out.at[owner], part_in.at[maker], part_sem.at[0, owner], part_sem.at[1, maker], (i, owner))

    def send_parts(chunk):
        for b in range(BLOCKS):
            owner = chunk * BLOCKS + b

            @pl.when(owner < j)
            def _():
                part_copy(owner, j).start()

    for chunk in range(CHUNKS):
        probs_t = probs[chunk] * share
        probs_grad = across(rows(chunk, 1), cot_t, 1, 0)
        scores_grad = (probs_t * (probs_grad - delta)).astype(jnp.bfloat16)
        query_grad_t = query_grad_t + across(rows(chunk, 0), scores_grad, 0, 0)
        keys_part = across(scores_grad, query, 1, 0).astype(jnp.bfloat16)
        values_part = across(probs_t.astype(jnp.bfloat16), cot, 1, 0).astype(jnp.bfloat16)
        for b in range(BLOCKS):
            part_out[chunk * BLOCKS + b, 0] = keys_part[b * 128 : (b + 1) * 128]
            part_out[chunk * BLOCKS + b, 1] = values_part[b * 128 : (b + 1) * 128]
        if chunk:
            send_parts(chunk - 1)
    send_parts(CHUNKS - 1)
    for h in range(HEADS):
        attn_ref[:, h * HD : (h + 1) * HD] = attn_t[:, h * 128 : (h + 1) * 128].T
        grad = query_grad_t[:, h * 128 : (h + 1) * 128].T
        back[h] = (rotated(grad, -1.0) * scale).astype(jnp.bfloat16)
    part_in[j] = part_out[j]
    keys_grad = jnp.zeros((128, HD), jnp.float32)
    values_grad = jnp.zeros((128, HD), jnp.float32)
    for maker in range(8):
        @pl.when(maker > j)
        def _():
            part_copy(j, maker).wait_recv()

        @pl.when(maker < j)
        def _():
            part_in[maker] = jnp.zeros((2, 128, HD), jnp.bfloat16)

        keys_grad = keys_grad + part_in[maker, 0].astype(jnp.float32)
        values_grad = values_grad + part_in[maker, 1].astype(jnp.float32)
    back[4] = rotated(keys_grad, -1.0).astype(jnp.bfloat16)
    back[5] = values_grad.astype(jnp.bfloat16)

    swap_back = remote(
        back.at[pl.ds(3 * (1 - core), 3)], back_other, swap_sem.at[0, 1], swap_sem.at[1, 1], partner
    )
    swap_back.start()
    own = jnp.concatenate([back[3 * core + p] for p in range(3)], axis=1)
    swap.wait_recv()
    swap_back.wait_recv()
    theirs = jnp.concatenate([back_other[p] for p in range(3)], axis=1)

    @pl.loop(0, 8)
    def _(k):
        chosen = pl.ds(k * 512, 512)
        sums = across(turned_own[chosen, :], own, 1, 0) + across(turned_other[chosen, :], theirs, 1, 0)
        for p in range(3):
            part[p, k // 2, k % 2] = sums[:, p * HD : (p + 1) * HD].reshape(8, 4, 2, 8, HD).astype(jnp.bfloat16)

    s = Scatter(
        at, core, part, (ring_0, ring_1, ring_2), (line_0, line_1, line_2), dot_in, final, total_ref,
        (s_ring, s_two, s_three, s_last), sent,
    )
    for p in (0, 1, 2):
        s.ring_start(p)
    pairs = [jnp.concatenate([back[2 * pair], back[2 * pair + 1]], axis=1) for pair in range(3)]

    def plain_rows(y, inner):
        cols = slice(y * 512, (y + 1) * 512)
        grad = sum(across(pairs[pair], weight_rows(pair, y), 1, 1) for pair in range(3))
        grad = grad * gain_row[:, cols]
        plain[:, cols] = grad
        return inner + jnp.sum(grad * hidden_ref[:, cols].astype(jnp.float32), axis=1, keepdims=True)

    inner = jnp.zeros((128, 1), jnp.float32)
    for y in (0, 1, 2, 3):
        inner = plain_rows(y, inner)
    s.ring_step(1, 0)
    s.ring_step(2, 0)
    s.ring_step(0, 0)
    for y in (4, 5):
        inner = plain_rows(y, inner)
    s.ring_step(1, 1)
    s.ring_step(2, 1)
    for y in (6, 7):
        inner = plain_rows(y, inner)
    s.ring_step(0, 1)
    s.lines_out(0)
    s.ring_step(1, 2)
    s.ring_step(2, 2)
    fall = inv_rms * inv_rms * inv_rms * (1.0 / WIDTH) * inner
    for y in range(8):
        cols = slice(y * 512, (y + 1) * 512)
        grad_in_ref[:, cols] = (
            plain[:, cols] * inv_rms - hidden_ref[:, cols].astype(jnp.float32) * fall
        ).astype(jnp.bfloat16)
    s.ring_step(1, 3)
    s.lines_out(1)
    s.ring_step(2, 3)
    s.lines_out(2)
    for p in (0, 2, 1):
        s.dots_out(p)
    for p in (1, 0, 2):
        s.finish(p)
    for p in (1, 0, 2):
        s.finished(p)
    inside = (j, i // 16, (i // 8) % 2, (i // 2) % 4, i % 2)
    sums = jnp.zeros((8, HD), jnp.float32)
    for n in range(TILES):
        tile = total_ref[n]
        weight_grad_ref[:, n * HD : (n + 1) * HD] = tile
        sums = sums + tile * full[(n, *inside)].astype(jnp.float32)
    lane = lax.broadcasted_iota(jnp.int32, (8, 128), 1)
    row = lax.broadcasted_iota(jnp.int32, (8, 128), 0)
    gains = jnp.sum(jnp.where(lane % 8 == row, gain_full[inside], 0.0), axis=1, keepdims=True)
    answer = jnp.sum(sums, axis=1, keepdims=True) / gains
    gain_grad_ref[...] = jnp.sum(jnp.where(lane == row, answer, 0.0), axis=0, keepdims=True)

    for peer in range(1, 8):
        @pl.when(j < peer)
        def _():
            kv_copy(j, peer).wait_send()

    for owner in range(7):
        @pl.when(owner < j)
        def _():
            part_copy(owner, j).wait_send()

    for copy in sent + [swap, swap_back]:
        copy.wait_send()


def whole(hidden, tiles, gain_piece, cosine, sine, cot):
    dma = pltpu.SemaphoreType.DMA
    vmem = pl.BlockSpec(memory_space=pltpu.VMEM)
    low, wide = jnp.bfloat16, jnp.float32

    def rings(p):
        dim = ORDERS[p][2]
        return pltpu.VMEM((2, SIZES[dim] // 2, HALVES, *RING_SHAPES[dim]), low)

    def lines(p):
        return pltpu.VMEM((SIZES[ORDERS[p][1]] - 1, *LINE_SHAPES[ORDERS[p][0]]), low)

    return pl.pallas_call(
        whole_kernel,
        out_shape=(
            jax.ShapeDtypeStruct((128, FLAT), low),
            jax.ShapeDtypeStruct((128, WIDTH), low),
            jax.ShapeDtypeStruct((8, TILES * HD), wide),
            jax.ShapeDtypeStruct((1, 128), wide),
        ),
        in_specs=[vmem] * 6,
        out_specs=(vmem,) * 4,
        scratch_shapes=[
            pltpu.VMEM((TILES, 8, 4, 2, 4, 2, 8, HD), low),
            pltpu.VMEM((8, 4, 2, 4, 2, 1, 128), wide),
            pltpu.VMEM((1, WIDTH), wide),
            pltpu.VMEM((128, WIDTH), low),
            pltpu.VMEM((WIDTH, 128), low),
            pltpu.VMEM((WIDTH, 128), low),
            pltpu.VMEM((8, 2, 128, HD), low),
            pltpu.VMEM((CHUNKS, CHUNK, FLAT), wide),
            pltpu.VMEM((8, 2, 128, HD), low),
            pltpu.VMEM((8, 2, 128, HD), low),
            pltpu.VMEM((TILES, 128, HD), low),
            pltpu.VMEM((3, 128, HD), low),
            pltpu.VMEM((128, WIDTH), wide),
            pltpu.VMEM((3, 4, 2, 8, 4, 2, 8, HD), low),
            *[rings(p) for p in range(3)],
            *[lines(p) for p in range(3)],
            pltpu.VMEM((3, 7, 2, 8, HD), low),
            pltpu.VMEM((3, 2, 8, HD), wide),
            pltpu.VMEM((TILES, 8, HD), wide),
            dma((2, 3)),
            dma((2, 3, 7)),
            dma((2, 3, 7)),
            dma((2, 3, 2, 4, HALVES)),
            dma((2, 3, 8)),
            dma((2, 4, 7)),
            dma((4,)),
            dma((2, 8)),
            dma((2, 8)),
            dma((2, 2)),
            dma((2, 3, 2, 4, HALVES)),
            dma((2, 3, 7)),
            dma((2, 3, 7)),
            dma((2, 3)),
        ],
        compiler_params=pltpu.CompilerParams(collective_id=0, has_side_effects=True, vmem_limit_bytes=56 * 2**20),
        name="whole",
    )(hidden, tiles, gain_piece, cosine, sine, cot)


def rope_tables(first_position):
    freqs = rope_base ** (-jnp.arange(HD // 2, dtype=jnp.float32) / (HD // 2))
    positions = first_position + jnp.arange(128, dtype=jnp.int32)
    angles = positions.astype(jnp.float32)[:, None] * freqs[None, :]
    cosine, sine = jnp.cos(angles), jnp.sin(angles)
    return jnp.concatenate([cosine, cosine], axis=1), jnp.concatenate([-sine, sine], axis=1)


def local(hidden_in, norm_gain, qkv_weight, attn_cotangent):
    i, j = lax.axis_index("inter"), lax.axis_index("intra")
    tiles = jnp.moveaxis(qkv_weight.reshape(8, TILES, HD), 1, 0)
    lane = jnp.arange(128)
    gain_piece = jnp.where(lane // 8 == (i * 8 + j) % 16, jnp.tile(norm_gain.astype(jnp.float32), 16), 0.0)[None]
    cosine, sine = rope_tables(j * 128)
    attn, grad_in, weight_grad, gain_grad = whole(hidden_in[0], tiles, gain_piece, cosine, sine, attn_cotangent[0])
    return (attn[None], grad_in[None], weight_grad, gain_grad[0, :8])


def solution(mesh):
    return jax.shard_map(
        local,
        mesh=mesh,
        in_specs=(
            P("inter", "intra", None),
            P(("inter", "intra")),
            P(("inter", "intra"), None),
            P("inter", "intra", None),
        ),
        out_specs=(
            P("inter", "intra", None),
            P("inter", "intra", None),
            P(("intra", "inter"), None),
            P(("intra", "inter")),
        ),
        check_vma=False,
    )
```

time: 336 us -> 120 us (0.36)
  waiting for transfers between devices: 139 us -> 0 us
  Pallas kernels: 0 us -> 111 us
  blocking collectives: 101 us -> 0 us
  starting transfers between devices: 28.9 us -> 0 us
  matrix products: 25.5 us -> 0 us
  between operations: 14.5 us -> 0.7 us
  other arithmetic: 14.6 us -> 1.6 us
  local copies, waits for them, and re-layouts: 11.2 us -> 6.34 us
    pallas_call x0 -> x1, Pallas kernels: none -> 111 us  [whole(): pl.pallas_call(whole_kernel, out_shape=(jax.ShapeDtypeStruct((128, FLAT),...]
    all_gather x2 -> x0, waiting for transfers between devices: 103 us -> none  [the longest x1 103 us: sent_together(): filled = lax.all_gather(both, axis, axis=dim, tiled=True)]
    all_gather x3 -> x0, blocking collectives: 93.8 us -> none  [the longest x1 41.1 us: gather_turned(): filled, at, outs = (lax.all_gather(both, axis, axis=0, tiled=True), 0, [])]
    all_to_all x3 -> x0, waiting for transfers between devices: 35.5 us -> none  [the longest x1 22.7 us: summed_on_arrival_2(): tiles = lax.all_to_all(split_up(x, dim, size), axis, 0, 0, tiled=True)]
    all_to_all x3 -> x0, starting transfers between devices: 28.8 us -> none  [the longest x1 21 us: summed_on_arrival_2(): tiles = lax.all_to_all(split_up(x, dim, size), axis, 0, 0, tiled=True)]
    dot_general x9 -> x0, matrix products: 25.5 us -> none  [the longest x1 6.34 us: local(): jnp.einsum('tc,dc->td', grad_mixed, weight_back, preferred_element_type=j...]
    all_to_all x1 -> x0, blocking collectives: 7.46 us -> none  [summed_on_arrival(): lax.all_to_all(tiles, axis, split_axis=0, concat_axis=0, tiled=True)]
    unnamed x51 -> x9, local copies, waits for them, and re-layouts: 0.76 us -> 5.74 us
  transfers between devices with their start and end apart: 5 -> 0, of which waited for: 3 -> 0; matrix products, arithmetic and copies ran while one was open for 11% -> 0% of each run, Pallas kernels for 0% -> 0%
where the time goes in v3:
time: 120 us; the launch traced here: 119 us
  Pallas kernels  111 us (92%)
  local copies, waits for them, and re-layouts  6.34 us (5%)
  other arithmetic  1.6 us (1%)
    pallas_call x1, Pallas kernels, whole(): pl.pallas_call(whole_kernel, out_shape=(jax.ShapeDtypeStruct((128, FLAT),...  111 us
    unnamed x9, local copies, waits for them, and re-layouts  5.74 us

profile of v3, /device:TPU:1, one launch (start us, length us, event | category | flops | bytes accessed | tf_op | source)
XLA Modules:
  0.0 119.3 jit_solution(14377195679540910621)
XLA Ops:
  0.7 0.0 copy-start.1
  0.7 0.6 copy-done.1
  1.3 0.1 tile.10
  1.4 0.5 compare_select_fusion.gain_ref
  1.9 0.3 fusion
  2.2 0.8 pad_maximum_fusion
  3.0 110.7 %whole.1 = (bf16[128,512]{1,0:T(8,128)(2,1)}, bf16[128,4096]{1,0:T(8,128)(2,1)}, f32[8,768]{1,0:T(8,128)}, f32[1,128]{1,0:T(1,128)}) custom-call(bf16[128,4096]{1,0:T(8,128)(2,1)} %bitcast.9, bf16[6,8,128]{2,1,0:T(8,128)(2,1)} %bitcast.13, f32[1,128]{1,0:T(1,128)} %compare_select_fusion.gain_ref, f32[128,128]{1,0:T(8,128)} %get-tuple-element.15.cos_ref, ...), custom_call_target="tpu_custom_call" | custom-call | tf_op jit(solution)/shard_map/whole/pallas_call | solution.py:611
  113.7 0.0 copy-start.2
  113.7 0.6 copy-done.2
  114.4 0.5 slice_bitcast_fusion
  114.9 1.6 %copy.11 = bf16[1,128,512]{2,1,0:T(8,128)(2,1)} copy(bf16[1,128,512]{2,1,0:T(8,128)(2,1)} %bitcast.12) | data formatting | bytes 262144
  116.4 0.0 copy-start
  116.4 2.3 %copy.12 = bf16[1,128,4096]{2,1,0:T(8,128)(2,1)} copy(bf16[1,128,4096]{2,1,0:T(8,128)(2,1)} %bitcast.10) | data formatting | bytes 2097152
  118.7 0.0 copy-done
  118.7 0.6 copy.13
  (3 shorter events, 0.0 us)
Async XLA Ops:
  0.7 0.7 copy-start.1
  113.7 0.6 copy-start.2
  116.4 2.3 %copy-start = (f32[8,768]{1,0:T(8,128)S(1)}, f32[8,768]{1,0:T(8,128)}, u32[]{:S(2)}) copy-start(f32[8,768]{1,0:T(8,128)} %get-tuple-element.23) | copy-start | bytes 73732

commit v4 on v3

v4 whole, which is shorter than its diff:
```python
import functools

import jax
import jax.numpy as jnp
from jax import lax
from jax.experimental import pallas as pl
from jax.experimental.pallas import tpu as pltpu
from jax.sharding import PartitionSpec as P

HD = 128
HEADS = 4
TILES = HEADS + 2
WIDTH = 4096
MESH = pl.DeviceIdType.MESH
SIZES = {"x": 4, "y": 8, "z": 8}
ORDERS = (
    (("z", "y", "x"), ("y", "z", "x")),
    (("z", "x", "y"), ("z", "x", "y")),
    (("y", "x", "z"), ("y", "x", "z")),
)
RINGS = ("x", "y", "z")
HALVES = 2
GAIN_ORDER = ("z", "y", "x")
CHUNK = 256
CHUNKS = 1024 // CHUNK
BLOCKS = CHUNK // 128
FLAT = HEADS * 128

eps_norm = 1e-05
rope_base = 500000.0


def place():
    i, j = lax.axis_index("inter"), lax.axis_index("intra")
    return {"x": j // 2, "y": i // 8, "z": ((i // 2) % 4) * 2 + j % 2}, i % 2


def device(at, core):
    return ((at["y"] * 4 + at["z"] // 2) * 2 + core, at["x"] * 2 + at["z"] % 2)


def moved(at, dim, step):
    size = SIZES[dim]
    return {**at, dim: (at[dim] + step + size) % size}


def indices(at):
    every = slice(None)
    y, x = at.get("y", every), at.get("x", every)
    high, low = (at["z"] // 2, at["z"] % 2) if "z" in at else (every, every)
    return y, high, x, low


def slab(ref, tile, at, cores=slice(None)):
    y, high, x, low = indices(at)
    return ref.at[tile, y, high, cores, x, low]


def gain_slab(ref, at, cores):
    y, high, x, low = indices(at)
    return ref.at[y, high, cores, x, low]


def out_slab(ref, tile, at, cores=slice(None)):
    y, high, x, low = indices(at)
    return ref.at[tile, x, low, y, high, cores]


def remote(src, dst, send, recv, peer):
    return pltpu.make_async_remote_copy(
        src_ref=src, dst_ref=dst, send_sem=send, recv_sem=recv, device_id=peer, device_id_type=MESH
    )


def across(left, right, left_dim, right_dim):
    return lax.dot_general(
        left, right, (((left_dim,), (right_dim,)), ((), ())), preferred_element_type=jnp.float32
    )


def steps_of(p, way):
    return SIZES[RINGS[p]] // 2 - way


def tiles_of(core):
    return [4 + core, 2 * core, 2 * core + 1]


def settle(spare, count, sem):
    pltpu.make_async_copy(spare.at[pl.ds(0, count)], spare.at[pl.ds(0, count)], sem).wait()


def greet(at, core, barrier):
    i, j = lax.axis_index("inter"), lax.axis_index("intra")
    peers = [device(at, 1 - core)]
    for dim, size in SIZES.items():
        peers += [device(moved(at, dim, step), core) for step in range(1, size)]
    peers += [(i, (j + step) % 8) for step in range(1, 8)]
    for peer in peers:
        pl.semaphore_signal(barrier, inc=1, device_id=peer, device_id_type=MESH)
    return len(peers)


class Gather:
    def __init__(self, at, core, mine_ref, gain_ref, full, gain_full, spare, sems):
        self.at, self.core, self.partner = at, core, device(at, 1 - core)
        self.mine_ref, self.gain_ref, self.full, self.gain_full = mine_ref, gain_ref, full, gain_full
        (self.swap, self.one, self.two, self.ring_out, self.ring, self.passing, self.gains, self.own) = sems
        self.mine, self.theirs = tiles_of(core), tiles_of(1 - core)
        sign = 1 - 2 * core
        self.ways = (sign, -sign)
        self.spare = spare

    def go(self, copy):
        copy.start()

    def begin(self):
        at, core, full = self.at, self.core, self.full
        owns = []
        for p in range(3):
            self.go(
                remote(
                    self.mine_ref.at[self.theirs[p]],
                    slab(full, self.theirs[p], at, core),
                    self.swap.at[0],
                    self.swap.at[1],
                    self.partner,
                )
            )
            owns.append(
                pltpu.make_async_copy(self.mine_ref.at[self.mine[p]], slab(full, self.mine[p], at, core), self.own.at[p])
            )
        owns.append(pltpu.make_async_copy(self.gain_ref, gain_slab(self.gain_full, at, core), self.own.at[3]))
        for own in owns:
            own.start()
        for own in owns:
            own.wait()
        self.gain_out(0)
        settle(self.spare, 3, self.swap.at[1])
        for p in (1, 2, 0):
            for h in range(HALVES):
                self.direct(p, h, 0)

    def direct(self, p, h, phase):
        order = ORDERS[p][h]
        sems = (self.one, self.two)[phase]
        src = slab(self.full, self.mine[p], {d: self.at[d] for d in order[phase:]}, h)
        for step in range(1, SIZES[order[phase]]):
            peer = device(moved(self.at, order[phase], step), self.core)
            self.go(remote(src, src, sems.at[6], sems.at[2 * p + h], peer))

    def arrived(self, p, h, phase):
        order = ORDERS[p][h]
        sems = (self.one, self.two)[phase]
        each = 1 if phase == 0 else SIZES[order[0]]
        settle(self.spare, (SIZES[order[phase]] - 1) * each, sems.at[2 * p + h])

    def gain_out(self, phase):
        dim = GAIN_ORDER[phase]
        src = gain_slab(self.gain_full, {d: self.at[d] for d in GAIN_ORDER[phase:]}, self.core)
        for step in range(1, SIZES[dim]):
            peer = device(moved(self.at, dim, step), self.core)
            self.go(remote(src, src, self.gains.at[0, phase], self.gains.at[1, phase], peer))

    def gain_wait(self, phase, side):
        rows = (
            self.gain_full.at[pl.ds(0, 7), 0, 0, 0, 0],
            self.gain_full.at[pl.ds(0, 7), :, :, 0, 0],
            self.gain_full.at[pl.ds(0, 6), :, :, :, 0],
            self.gain_full.at[:, :, 0],
        )[phase]
        pltpu.make_async_copy(rows, rows, self.gains.at[side, phase]).wait()

    def gain_in(self, phase):
        self.gain_wait(phase, 1)

    def gain_pass(self):
        whole = gain_slab(self.gain_full, {}, self.core)
        self.go(remote(whole, whole, self.gains.at[0, 3], self.gains.at[1, 3], self.partner))

    def gain_passed(self):
        self.gain_wait(3, 1)

    def settled(self):
        settle(self.spare, 3, self.swap.at[0])
        settle(self.spare, 42, self.one.at[6])
        settle(self.spare, 208, self.two.at[6])
        for p in range(3):
            settle(self.spare, 384 if RINGS[p] == "x" else 448, self.ring_out.at[p])
            settle(self.spare, 512, self.passing.at[0, p])
        for phase in range(4):
            self.gain_wait(phase, 0)

    def where(self, p, way, step):
        dim = RINGS[p]
        return moved(self.at, dim, -self.ways[way] * step)[dim]

    def hop(self, p, way, step, h):
        dim = RINGS[p]
        piece = slab(self.full, self.mine[p], {dim: self.where(p, way, step)}, h)
        peer = device(moved(self.at, dim, self.ways[way]), self.core)
        self.go(remote(piece, piece, self.ring_out.at[p], self.ring.at[p, way, step, h], peer))

    def pass_on(self, p, h, where):
        piece = slab(self.full, self.mine[p], {RINGS[p]: where}, h)
        self.go(remote(piece, piece, self.passing.at[0, p], self.passing.at[1, p], self.partner))

    def ring_start(self, p, h):
        for way in range(2):
            self.hop(p, way, 0, h)
        self.pass_on(p, h, self.at[RINGS[p]])

    def ring_step(self, p, h, step):
        dim = RINGS[p]
        for way in range(2):
            if step >= steps_of(p, way):
                continue
            piece = slab(self.full, self.mine[p], {dim: self.where(p, way, step + 1)}, h)
            remote(piece, piece, self.ring_out.at[p], self.ring.at[p, way, step, h], self.partner).wait_recv()
            if step + 1 < steps_of(p, way):
                self.hop(p, way, step + 1, h)
            self.pass_on(p, h, self.where(p, way, step + 1))

    def passed(self, p):
        settle(self.spare, 512, self.passing.at[1, p])


RING_SHAPES = {"x": (2, 8, 4, 8, HD), "y": (4, 2, 4, 8, HD), "z": (4, 8, 8, HD)}
LINE_SHAPES = {"x": (4, 8, HD), "y": (8, 8, HD), "z": (2, 4, 8, HD)}


class Scatter:
    def __init__(self, at, core, part, rings, lines, dot_in, final, total_ref, spare, sems):
        self.at, self.core, self.partner = at, core, device(at, 1 - core)
        self.part, self.rings, self.lines, self.dot_in = part, rings, lines, dot_in
        self.final, self.total_ref = final, total_ref
        self.ring_out, self.ring, self.two, self.three, self.last = sems
        sign = 1 - 2 * core
        self.ways = (sign, -sign)
        self.spare = spare

    def go(self, copy):
        copy.start()

    def target(self, p, way, left):
        dim = RINGS[p]
        return {dim: moved(self.at, dim, self.ways[way] * left)[dim]}

    def copy(self, p, way, step, h):
        dim = RINGS[p]
        return remote(
            out_slab(self.part, p, self.target(p, way, steps_of(p, way) - step), h),
            self.rings[p].at[way, step, h],
            self.ring_out.at[p],
            self.ring.at[p, way, step, h],
            device(moved(self.at, dim, self.ways[way]), self.core),
        )

    def ring_start(self, p):
        for h in range(HALVES):
            for way in range(2):
                self.go(self.copy(p, way, 0, h))

    def ring_step(self, p, h, step):
        for way in range(2):
            if step >= steps_of(p, way):
                continue
            self.copy(p, way, step, h).wait_recv()
            here = out_slab(self.part, p, self.target(p, way, steps_of(p, way) - step - 1), h)
            there = self.rings[p].at[way, step, h]
            here[...] = (here[...].astype(jnp.float32) + there[...].astype(jnp.float32)).astype(jnp.bfloat16)
            if step + 1 < steps_of(p, way):
                self.go(self.copy(p, way, step + 1, h))

    def lines_out(self, p, h):
        a, b, c = ORDERS[p][h]
        for step in range(1, SIZES[b]):
            there = moved(self.at, b, step)
            self.go(
                remote(
                    out_slab(self.part, p, {b: there[b], c: self.at[c]}, h),
                    self.lines[2 * p + h].at[step - 1],
                    self.two.at[6],
                    self.two.at[2 * p + h],
                    device(there, self.core),
                )
            )

    def dots_out(self, p, h):
        a, b, c = ORDERS[p][h]
        lines = self.lines[2 * p + h]
        here = out_slab(self.part, p, {b: self.at[b], c: self.at[c]}, h)
        total = here[...].astype(jnp.float32)
        settle(self.spare, (SIZES[b] - 1) * SIZES[a], self.two.at[2 * p + h])
        for step in range(1, SIZES[b]):
            total = total + lines[step - 1].astype(jnp.float32)
        here[...] = total.astype(jnp.bfloat16)
        for step in range(1, SIZES[a]):
            there = moved(self.at, a, step)
            self.go(
                remote(
                    out_slab(self.part, p, there, h),
                    self.dot_in.at[p, h, step - 1],
                    self.three.at[6],
                    self.three.at[2 * p + h],
                    device(there, self.core),
                )
            )

    def finish(self, p):
        tile = tiles_of(self.core)[p]
        for h in range(HALVES):
            a = ORDERS[p][h][0]
            here = out_slab(self.part, p, self.at, h)
            total = here[...].astype(jnp.float32)
            settle(self.spare, SIZES[a] - 1, self.three.at[2 * p + h])
            for step in range(1, SIZES[a]):
                total = total + self.dot_in[p, h, step - 1].astype(jnp.float32)
            self.final[p, h] = total
        self.total_ref[tile] = self.final[p, self.core]
        self.go(
            remote(
                self.final.at[p, 1 - self.core], self.total_ref.at[tile], self.last.at[0], self.last.at[1], self.partner
            )
        )

    def finished(self, side):
        settle(self.spare, 6, self.last.at[side])

    def settled(self):
        for p in range(3):
            settle(self.spare, 384 if RINGS[p] == "x" else 448, self.ring_out.at[p])
        settle(self.spare, 208, self.two.at[6])
        settle(self.spare, 42, self.three.at[6])
        self.finished(0)


def whole_kernel(
    hidden_ref, mine_ref, gain_ref, cos_ref, sin_ref, cot_ref,
    attn_ref, grad_in_ref, weight_grad_ref, gain_grad_ref,
    full, gain_full, gain_row, normed, turned_own, turned_other,
    kv, probs, part_out, part_in, back, back_other, plain,
    part, ring_0, ring_1, ring_2, line_0, line_1, line_2, line_3, line_4, line_5, dot_in, final, total_ref, mixed, spare,
    g_swap, g_one, g_two, g_out, g_ring, g_pass, g_gain, g_own,
    kv_sem, part_sem, swap_sem, s_out, s_ring, s_two, s_three, s_last,
):
    i, j = lax.axis_index("inter"), lax.axis_index("intra")
    at, core = place()
    partner = device(at, 1 - core)
    barrier = pltpu.get_barrier_semaphore()
    for block in range(8):
        kv[block] = jnp.zeros((2, 128, HD), jnp.bfloat16)
    count = greet(at, core, barrier)
    squares = jnp.zeros((128, 128), jnp.float32)
    for t in range(WIDTH // 128):
        tile = hidden_ref[:, t * 128 : (t + 1) * 128].astype(jnp.float32)
        squares = squares + tile * tile
    inv_rms = lax.rsqrt(jnp.sum(squares, axis=1, keepdims=True) / WIDTH + eps_norm)
    cosine, sine = cos_ref[...], sin_ref[...]
    cots = [cot_ref[:, h * HD : (h + 1) * HD] for h in range(HEADS)]
    pl.semaphore_wait(barrier, count)

    g = Gather(
        at, core, mine_ref, gain_ref, full, gain_full, spare,
        (g_swap, g_one, g_two, g_out, g_ring, g_pass, g_gain, g_own),
    )
    g.begin()
    for p in (1, 2):
        for h in range(HALVES):
            g.arrived(p, h, 0)
            g.direct(p, h, 1)
    g.gain_in(0)
    g.gain_out(1)
    for h in range(HALVES):
        g.arrived(0, h, 0)
        g.direct(0, h, 1)
    for h in range(HALVES):
        for p in (1, 2):
            g.arrived(p, h, 1)
            g.ring_start(p, h)
    g.gain_in(1)
    g.gain_out(2)

    def far(step):
        for h in range(HALVES):
            for p in (1, 2):
                g.ring_step(p, h, step)

    for h in range(HALVES):
        g.arrived(0, h, 1)
        g.ring_start(0, h)
    far(0)
    g.gain_in(2)
    g.gain_pass()
    far(1)
    g.gain_passed()
    for y in range(8):
        for z in range(4):
            t = y * 4 + z
            gain_row[:, t * 128 : (t + 1) * 128] = jnp.sum(gain_full[y, z], axis=(0, 1, 2))
    for t in range(WIDTH // 128):
        cols = slice(t * 128, (t + 1) * 128)
        unit = hidden_ref[:, cols].astype(jnp.float32) * inv_rms * gain_row[:, cols]
        normed[:, cols] = unit.astype(jnp.bfloat16)
    for h in range(HALVES):
        g.ring_step(0, h, 0)
    far(2)
    for t in range(WIDTH // 128):
        cols = slice(t * 128, (t + 1) * 128)
        turned_own[cols, :] = normed[:, cols].T
    for h in range(HALVES):
        g.ring_step(0, h, 1)
    far(3)
    swap = remote(turned_own, turned_other, swap_sem.at[0, 0], swap_sem.at[1, 0], partner)
    swap.start()

    def weight_rows(tiles, y):
        return jnp.concatenate([full[tile, y].reshape(512, HD) for tile in tiles], axis=1)

    def mix(tiles):
        total = jnp.zeros((128, len(tiles) * HD), jnp.float32)
        for y in range(8):
            total = total + across(normed[:, y * 512 : (y + 1) * 512], weight_rows(tiles, y), 1, 0)
        for k, tile in enumerate(tiles):
            mixed[tile] = total[:, k * HD : (k + 1) * HD]

    def rotated(x, sign):
        return x * cosine + sign * (pltpu.roll(x, 64, 1) * sine)

    mix(g.mine[:1])
    g.passed(0)
    mix(g.theirs[:1])
    kv[j, 0] = rotated(mixed[4], 1.0).astype(jnp.bfloat16)
    kv[j, 1] = mixed[5].astype(jnp.bfloat16)

    def kv_copy(owner, peer):
        return remote(kv.at[owner], kv.at[owner], kv_sem.at[0, peer], kv_sem.at[1, owner], (i, peer))

    for peer in range(1, 8):
        @pl.when(j < peer)
        def _():
            kv_copy(j, peer).start()

    scale = HD ** (-0.5)
    mix(g.mine[1:])
    g.passed(1)
    g.passed(2)
    mix(g.theirs[1:])
    queries = [(rotated(mixed[h], 1.0) * scale).astype(jnp.bfloat16) for h in range(HEADS)]
    query = jnp.concatenate(queries, axis=0)
    query_t = jnp.concatenate([q.T for q in queries], axis=1)
    cot = jnp.concatenate(cots, axis=0)
    cot_t = jnp.concatenate([c.T for c in cots], axis=1)
    row_pos = j * 128 + lax.broadcasted_iota(jnp.int32, (CHUNK, FLAT), 1) % 128
    key_pos = lax.broadcasted_iota(jnp.int32, (CHUNK, FLAT), 0)

    def allowed(chunk):
        return key_pos + chunk * CHUNK <= row_pos

    def rows(chunk, which):
        return jnp.concatenate([kv[chunk * BLOCKS + b, which] for b in range(BLOCKS)], axis=0)

    for owner in range(7):
        @pl.when(owner < j)
        def _():
            kv_copy(owner, j).wait_recv()

    top = jnp.full((1, FLAT), -1e30, jnp.float32)
    for chunk in range(CHUNKS):
        scores = jnp.where(allowed(chunk), across(rows(chunk, 0), query_t, 1, 0), -1e30)
        probs[chunk] = scores
        top = jnp.maximum(top, jnp.max(scores, axis=0, keepdims=True))
    total = jnp.zeros((1, FLAT), jnp.float32)
    out_t = jnp.zeros((HD, FLAT), jnp.float32)
    for chunk in range(CHUNKS):
        numbers = jnp.exp(probs[chunk] - top)
        probs[chunk] = numbers
        total = total + jnp.sum(numbers, axis=0, keepdims=True)
        out_t = out_t + across(rows(chunk, 1), numbers.astype(jnp.bfloat16), 0, 0)
    share = 1.0 / total
    attn_t = (out_t * share).astype(jnp.bfloat16)
    delta = jnp.sum(cot_t.astype(jnp.float32) * attn_t.astype(jnp.float32), axis=0, keepdims=True)
    query_grad_t = jnp.zeros((HD, FLAT), jnp.float32)

    def part_copy(owner, maker):
        return remote(part_out.at[owner], part_in.at[maker], part_sem.at[0, owner], part_sem.at[1, maker], (i, owner))

    def send_parts(chunk):
        for b in range(BLOCKS):
            owner = chunk * BLOCKS + b

            @pl.when(owner < j)
            def _():
                part_copy(owner, j).start()

    for chunk in range(CHUNKS):
        probs_t = probs[chunk] * share
        probs_grad = across(rows(chunk, 1), cot_t, 1, 0)
        scores_grad = (probs_t * (probs_grad - delta)).astype(jnp.bfloat16)
        keys_part = across(scores_grad, query, 1, 0).astype(jnp.bfloat16)
        values_part = across(probs_t.astype(jnp.bfloat16), cot, 1, 0).astype(jnp.bfloat16)
        for b in range(BLOCKS):
            part_out[chunk * BLOCKS + b, 0] = keys_part[b * 128 : (b + 1) * 128]
            part_out[chunk * BLOCKS + b, 1] = values_part[b * 128 : (b + 1) * 128]
        query_grad_t = query_grad_t + across(rows(chunk, 0), scores_grad, 0, 0)
        send_parts(chunk)
    for h in range(HEADS):
        grad = query_grad_t[:, h * 128 : (h + 1) * 128].T
        back[h] = (rotated(grad, -1.0) * scale).astype(jnp.bfloat16)

    def swap_back(first, count, slot):
        return remote(
            back.at[pl.ds(first, count)], back_other.at[pl.ds(slot, count)], swap_sem.at[0, 1 + slot],
            swap_sem.at[1, 1 + slot], partner,
        )

    swap_heads = swap_back(2 * (1 - core), 2, 0)
    swap_heads.start()
    for h in range(HEADS):
        attn_ref[:, h * HD : (h + 1) * HD] = attn_t[:, h * 128 : (h + 1) * 128].T
    swap.wait_recv()
    swap_heads.wait_recv()

    def products(ps):
        own = jnp.concatenate([back[g.mine[p]] for p in ps], axis=1)
        other = jnp.concatenate([back_other[(p + 2) % 3] for p in ps], axis=1)
        both = jnp.concatenate([own, other], axis=0)
        for k in range(8):
            chosen = slice(k * 512, (k + 1) * 512)
            left = jnp.concatenate([turned_own[chosen, :], turned_other[chosen, :]], axis=1)
            sums = across(left, both, 1, 0)
            for n, p in enumerate(ps):
                part[p, k // 2, k % 2] = sums[:, n * HD : (n + 1) * HD].reshape(8, 4, 2, 8, HD).astype(jnp.bfloat16)

    s = Scatter(
        at, core, part, (ring_0, ring_1, ring_2), (line_0, line_1, line_2, line_3, line_4, line_5), dot_in, final,
        total_ref, spare, (s_out, s_ring, s_two, s_three, s_last),
    )
    products((1, 2))
    s.ring_start(1)
    s.ring_start(2)
    part_in[j] = part_out[j]
    keys_grad = jnp.zeros((128, HD), jnp.float32)
    values_grad = jnp.zeros((128, HD), jnp.float32)
    for maker in range(8):
        @pl.when(maker > j)
        def _():
            part_copy(j, maker).wait_recv()

        @pl.when(maker < j)
        def _():
            part_in[maker] = jnp.zeros((2, 128, HD), jnp.bfloat16)

        keys_grad = keys_grad + part_in[maker, 0].astype(jnp.float32)
        values_grad = values_grad + part_in[maker, 1].astype(jnp.float32)
    back[4] = rotated(keys_grad, -1.0).astype(jnp.bfloat16)
    back[5] = values_grad.astype(jnp.bfloat16)

    swap_last = swap_back(5 - core, 1, 2)
    swap_last.start()
    pairs = [jnp.concatenate([back[2 * pair], back[2 * pair + 1]], axis=1) for pair in range(3)]
    swap_last.wait_recv()
    products((0,))
    s.ring_start(0)
    g.settled()

    def plain_rows(y, inner):
        cols = slice(y * 512, (y + 1) * 512)
        grad = sum(across(pairs[pair], weight_rows((2 * pair, 2 * pair + 1), y), 1, 1) for pair in range(3))
        grad = grad * gain_row[:, cols]
        plain[:, cols] = grad
        return inner + jnp.sum(grad * hidden_ref[:, cols].astype(jnp.float32), axis=1, keepdims=True)

    inner = jnp.zeros((128, 1), jnp.float32)

    def both(step):
        for h in range(HALVES):
            for p in (1, 2):
                s.ring_step(p, h, step)

    both(0)
    for y in (0, 1, 2, 3):
        inner = plain_rows(y, inner)
    both(1)
    s.ring_step(0, 0, 0)
    for y in (4, 5, 6, 7):
        inner = plain_rows(y, inner)
    both(2)
    s.ring_step(0, 1, 0)
    fall = inv_rms * inv_rms * inv_rms * (1.0 / WIDTH) * inner
    for y in range(8):
        cols = slice(y * 512, (y + 1) * 512)
        grad_in_ref[:, cols] = (
            plain[:, cols] * inv_rms - hidden_ref[:, cols].astype(jnp.float32) * fall
        ).astype(jnp.bfloat16)
    s.ring_step(0, 0, 1)
    s.lines_out(0, 0)
    for h in range(HALVES):
        for p in (1, 2):
            s.ring_step(p, h, 3)
            s.lines_out(p, h)
    s.ring_step(0, 1, 1)
    s.lines_out(0, 1)
    for h in range(HALVES):
        for p in (1, 2):
            s.dots_out(p, h)
    for h in range(HALVES):
        s.dots_out(0, h)
    s.finish(1)
    s.finish(2)
    s.finish(0)
    s.finished(1)
    inside = (j, i // 16, (i // 8) % 2, (i // 2) % 4, i % 2)
    sums = jnp.zeros((8, HD), jnp.float32)
    for n in range(TILES):
        tile = total_ref[n]
        weight_grad_ref[:, n * HD : (n + 1) * HD] = tile
        sums = sums + tile * full[(n, *inside)].astype(jnp.float32)
    lane = lax.broadcasted_iota(jnp.int32, (8, 128), 1)
    row = lax.broadcasted_iota(jnp.int32, (8, 128), 0)
    gains = jnp.sum(jnp.where(lane % 8 == row, gain_full[inside], 0.0), axis=1, keepdims=True)
    answer = jnp.sum(sums, axis=1, keepdims=True) / gains
    gain_grad_ref[...] = jnp.sum(jnp.where(lane == row, answer, 0.0), axis=0, keepdims=True)

    for peer in range(1, 8):
        @pl.when(j < peer)
        def _():
            kv_copy(j, peer).wait_send()

    for owner in range(7):
        @pl.when(owner < j)
        def _():
            part_copy(owner, j).wait_send()

    for copy in (swap, swap_heads, swap_last):
        copy.wait_send()
    s.settled()


def whole(hidden, tiles, gain_piece, cosine, sine, cot):
    dma = pltpu.SemaphoreType.DMA
    vmem = pl.BlockSpec(memory_space=pltpu.VMEM)
    low, wide = jnp.bfloat16, jnp.float32

    def rings(p):
        dim = RINGS[p]
        return pltpu.VMEM((2, SIZES[dim] // 2, HALVES, *RING_SHAPES[dim]), low)

    def lines(p, h):
        return pltpu.VMEM((SIZES[ORDERS[p][h][1]] - 1, *LINE_SHAPES[ORDERS[p][h][0]]), low)

    return pl.pallas_call(
        whole_kernel,
        out_shape=(
            jax.ShapeDtypeStruct((128, FLAT), low),
            jax.ShapeDtypeStruct((128, WIDTH), low),
            jax.ShapeDtypeStruct((8, TILES * HD), wide),
            jax.ShapeDtypeStruct((1, 128), wide),
        ),
        in_specs=[vmem] * 6,
        out_specs=(vmem,) * 4,
        scratch_shapes=[
            pltpu.VMEM((TILES, 8, 4, 2, 4, 2, 8, HD), low),
            pltpu.VMEM((8, 4, 2, 4, 2, 1, 128), wide),
            pltpu.VMEM((1, WIDTH), wide),
            pltpu.VMEM((128, WIDTH), low),
            pltpu.VMEM((WIDTH, 128), low),
            pltpu.VMEM((WIDTH, 128), low),
            pltpu.VMEM((8, 2, 128, HD), low),
            pltpu.VMEM((CHUNKS, CHUNK, FLAT), wide),
            pltpu.VMEM((8, 2, 128, HD), low),
            pltpu.VMEM((8, 2, 128, HD), low),
            pltpu.VMEM((TILES, 128, HD), low),
            pltpu.VMEM((3, 128, HD), low),
            pltpu.VMEM((128, WIDTH), wide),
            pltpu.VMEM((3, 4, 2, 8, 4, 2, 8, HD), low),
            *[rings(p) for p in range(3)],
            *[lines(p, h) for p in range(3) for h in range(HALVES)],
            pltpu.VMEM((3, HALVES, 7, 8, HD), low),
            pltpu.VMEM((3, 2, 8, HD), wide),
            pltpu.VMEM((TILES, 8, HD), wide),
            pltpu.VMEM((TILES, 128, HD), wide),
            pltpu.VMEM((512, 8, HD), low),
            dma((2,)),
            dma((7,)),
            dma((7,)),
            dma((3,)),
            dma((3, 2, 4, HALVES)),
            dma((2, 3)),
            dma((2, 4)),
            dma((4,)),
            dma((2, 8)),
            dma((2, 8)),
            dma((2, 4)),
            dma((3,)),
            dma((3, 2, 4, HALVES)),
            dma((7,)),
            dma((7,)),
            dma((2,)),
        ],
        compiler_params=pltpu.CompilerParams(collective_id=0, has_side_effects=True, vmem_limit_bytes=40 * 2**20),
        name="whole",
    )(hidden, tiles, gain_piece, cosine, sine, cot)


def rope_tables(first_position):
    freqs = rope_base ** (-jnp.arange(HD // 2, dtype=jnp.float32) / (HD // 2))
    positions = first_position + jnp.arange(128, dtype=jnp.int32)
    angles = positions.astype(jnp.float32)[:, None] * freqs[None, :]
    cosine, sine = jnp.cos(angles), jnp.sin(angles)
    return jnp.concatenate([cosine, cosine], axis=1), jnp.concatenate([-sine, sine], axis=1)


def local(hidden_in, norm_gain, qkv_weight, attn_cotangent):
    i, j = lax.axis_index("inter"), lax.axis_index("intra")
    tiles = jnp.moveaxis(qkv_weight.reshape(8, TILES, HD), 1, 0)
    lane = jnp.arange(128)
    gain_piece = jnp.where(lane // 8 == (i * 8 + j) % 16, jnp.tile(norm_gain.astype(jnp.float32), 16), 0.0)[None]
    cosine, sine = rope_tables(j * 128)
    attn, grad_in, weight_grad, gain_grad = whole(hidden_in[0], tiles, gain_piece, cosine, sine, attn_cotangent[0])
    return (attn[None], grad_in[None], weight_grad, gain_grad[0, :8])


def solution(mesh):
    return jax.shard_map(
        local,
        mesh=mesh,
        in_specs=(
            P("inter", "intra", None),
            P(("inter", "intra")),
            P(("inter", "intra"), None),
            P("inter", "intra", None),
        ),
        out_specs=(
            P("inter", "intra", None),
            P("inter", "intra", None),
            P(("intra", "inter"), None),
            P(("intra", "inter")),
        ),
        check_vma=False,
    )
```

time: 120 us -> 97.2 us (0.81)
  Pallas kernels: 111 us -> 90.4 us
    pallas_call x1, Pallas kernels: 111 us -> 90.4 us  [whole(): pl.pallas_call(whole_kernel, out_shape=(jax.ShapeDtypeStruct((128, FLAT),...]
    unnamed x9 -> x11, local copies, waits for them, and re-layouts: 5.74 us -> 4.88 us
where the time goes in v4:
time: 97.2 us; the launch traced here: 97.1 us
  Pallas kernels  90.4 us (93%)
  local copies, waits for them, and re-layouts  5.48 us (6%)
    pallas_call x1, Pallas kernels, whole(): pl.pallas_call(whole_kernel, out_shape=(jax.ShapeDtypeStruct((128, FLAT),...  90.4 us
    unnamed x11, local copies, waits for them, and re-layouts  4.88 us

profile of v4, /device:TPU:1, one launch (start us, length us, event | category | flops | bytes accessed | tf_op | source)
XLA Modules:
  0.0 97.1 jit_solution(10276515219113704939)
XLA Ops:
  0.7 0.0 copy-start.3
  0.7 0.6 copy-done.3
  1.3 0.1 tile.10
  1.4 0.3 fusion
  1.7 0.0 copy-start.1
  1.8 0.0 copy-start.2
  1.8 0.1 pad_maximum_fusion
  1.9 0.8 copy-done.1
  2.6 0.0 copy-done.2
  2.6 0.0 copy-start
  2.7 1.2 %copy-done = bf16[1,128,4096]{2,1,0:T(8,128)(2,1)S(1)} copy-done((bf16[1,128,4096]{2,1,0:T(8,128)(2,1)S(1)}, bf16[1,128,4096]{2,1,0:T(8,128)(2,1)}, u32[]{:S(2)}) %copy-start) | copy-done | bytes 1048600
  3.9 90.4 %whole.1 = (bf16[128,512]{1,0:T(8,128)(2,1)S(1)}, bf16[128,4096]{1,0:T(8,128)(2,1)S(1)}, f32[8,768]{1,0:T(8,128)S(1)}, f32[1,128]{1,0:T(1,128)S(1)}) custom-call(bf16[128,4096]{1,0:T(8,128)(2,1)S(1)} %bitcast.9, bf16[6,8,128]{2,1,0:T(8,128)(2,1)S(1)} %bitcast.13, f32[1,128]{1,0:T(1,128)S(1)} %compare_select_fusion.gain_ref, ...), custom_call_target="tpu_custom_call" | custom-call | tf_op jit(solution)/shard_map/whole/pallas_call | solution.py:652
  94.3 0.5 slice_bitcast_fusion
  94.8 0.7 copy.11
  95.5 1.0 copy.12
  96.4 0.6 copy.13
  (4 shorter events, 0.0 us)
Async XLA Ops:
  0.7 0.7 copy-start.3
  1.7 0.9 copy-start.1
  1.8 0.9 copy-start.2
  2.6 1.2 %copy-start = (bf16[1,128,4096]{2,1,0:T(8,128)(2,1)S(1)}, bf16[1,128,4096]{2,1,0:T(8,128)(2,1)}, u32[]{:S(2)}) copy-start(bf16[1,128,4096]{2,1,0:T(8,128)(2,1)} %param.4) | copy-start | bytes 3145732

commit v5 on v4

--- a/solution.py
+++ b/solution.py
@@ -1,7 +1,6 @@
-import functools
-
 import jax
 import jax.numpy as jnp
+import numpy as np
 from jax import lax
 from jax.experimental import pallas as pl
 from jax.experimental.pallas import tpu as pltpu
@@ -105,7 +104,7 @@
     def __init__(self, at, core, mine_ref, gain_ref, full, gain_full, spare, sems):
         self.at, self.core, self.partner = at, core, device(at, 1 - core)
         self.mine_ref, self.gain_ref, self.full, self.gain_full = mine_ref, gain_ref, full, gain_full
-        (self.swap, self.one, self.two, self.ring_out, self.ring, self.passing, self.gains, self.own) = sems
+        (self.swap, self.one, self.two, self.item, self.side, self.ring_out, self.ring, self.passing, self.gains, self.own) = sems
         self.mine, self.theirs = tiles_of(core), tiles_of(1 - core)
         sign = 1 - 2 * core
         self.ways = (sign, -sign)
@@ -147,7 +146,23 @@
         src = slab(self.full, self.mine[p], {d: self.at[d] for d in order[phase:]}, h)
         for step in range(1, SIZES[order[phase]]):
             peer = device(moved(self.at, order[phase], step), self.core)
-            self.go(remote(src, src, sems.at[6], sems.at[2 * p + h], peer))
+            recv = self.item.at[h, step - 1] if p == 0 and phase == 1 else sems.at[2 * p + h]
+            self.go(remote(src, src, sems.at[6], recv, peer))
+
+    def along(self, h, step):
+        middle = ORDERS[0][h][1]
+        if step:
+            settle(self.spare, 8, self.item.at[h, step - 1])
+        known = moved({d: self.at[d] for d in (middle, "x")}, middle, -step)
+        src = slab(self.full, self.mine[0], known, h)
+        for k in (1, 3, 2):
+            peer = device(moved(self.at, "x", k), self.core)
+            self.go(remote(src, src, self.ring_out.at[0], self.side.at[h, k - 1], peer))
+
+    def beside(self, h):
+        for k in (1, 3, 2):
+            settle(self.spare, 64, self.side.at[h, k - 1])
+            self.pass_on(0, h, moved(self.at, "x", -k)["x"])
 
     def arrived(self, p, h, phase):
         order = ORDERS[p][h]
@@ -199,7 +214,7 @@
         dim = RINGS[p]
         piece = slab(self.full, self.mine[p], {dim: self.where(p, way, step)}, h)
         peer = device(moved(self.at, dim, self.ways[way]), self.core)
-        self.go(remote(piece, piece, self.ring_out.at[p], self.ring.at[p, way, step, h], peer))
+        self.go(remote(piece, piece, self.ring_out.at[p], self.ring.at[p - 1, way, step, h], peer))
 
     def pass_on(self, p, h, where):
         piece = slab(self.full, self.mine[p], {RINGS[p]: where}, h)
@@ -216,7 +231,7 @@
             if step >= steps_of(p, way):
                 continue
             piece = slab(self.full, self.mine[p], {dim: self.where(p, way, step + 1)}, h)
-            remote(piece, piece, self.ring_out.at[p], self.ring.at[p, way, step, h], self.partner).wait_recv()
+            remote(piece, piece, self.ring_out.at[p], self.ring.at[p - 1, way, step, h], self.partner).wait_recv()
             if step + 1 < steps_of(p, way):
                 self.hop(p, way, step + 1, h)
             self.pass_on(p, h, self.where(p, way, step + 1))
@@ -336,33 +351,42 @@
 
 
 def whole_kernel(
-    hidden_ref, mine_ref, gain_ref, cos_ref, sin_ref, cot_ref,
+    hidden_in, mine_ref, gain_ref, tables_in, cot_in,
     attn_ref, grad_in_ref, weight_grad_ref, gain_grad_ref,
     full, gain_full, gain_row, normed, turned_own, turned_other,
     kv, probs, part_out, part_in, back, back_other, plain,
-    part, ring_0, ring_1, ring_2, line_0, line_1, line_2, line_3, line_4, line_5, dot_in, final, total_ref, mixed, spare,
-    g_swap, g_one, g_two, g_out, g_ring, g_pass, g_gain, g_own,
+    part, ring_0, ring_1, ring_2, line_0, line_1, line_2, line_3, line_4, line_5, dot_in, final, total_ref, mixed, spare, hidden_ref, tables, cot_ref, load_sem,
+    g_swap, g_one, g_two, g_item, g_side, g_out, g_ring, g_pass, g_gain, g_own,
     kv_sem, part_sem, swap_sem, s_out, s_ring, s_two, s_three, s_last,
 ):
     i, j = lax.axis_index("inter"), lax.axis_index("intra")
     at, core = place()
     partner = device(at, 1 - core)
     barrier = pltpu.get_barrier_semaphore()
+    loads = [
+        pltpu.make_async_copy(hidden_in, hidden_ref, load_sem.at[0]),
+        pltpu.make_async_copy(cot_in, cot_ref, load_sem.at[1]),
+        pltpu.make_async_copy(tables_in.at[j], tables, load_sem.at[2]),
+    ]
+    for load in loads:
+        load.start()
     for block in range(8):
         kv[block] = jnp.zeros((2, 128, HD), jnp.bfloat16)
     count = greet(at, core, barrier)
+    for load in loads:
+        load.wait()
     squares = jnp.zeros((128, 128), jnp.float32)
     for t in range(WIDTH // 128):
         tile = hidden_ref[:, t * 128 : (t + 1) * 128].astype(jnp.float32)
         squares = squares + tile * tile
     inv_rms = lax.rsqrt(jnp.sum(squares, axis=1, keepdims=True) / WIDTH + eps_norm)
-    cosine, sine = cos_ref[...], sin_ref[...]
+    cosine, sine = tables[0], tables[1]
     cots = [cot_ref[:, h * HD : (h + 1) * HD] for h in range(HEADS)]
     pl.semaphore_wait(barrier, count)
 
     g = Gather(
         at, core, mine_ref, gain_ref, full, gain_full, spare,
-        (g_swap, g_one, g_two, g_out, g_ring, g_pass, g_gain, g_own),
+        (g_swap, g_one, g_two, g_item, g_side, g_out, g_ring, g_pass, g_gain, g_own),
     )
     g.begin()
     for p in (1, 2):
@@ -375,20 +399,32 @@
         g.arrived(0, h, 0)
         g.direct(0, h, 1)
     for h in range(HALVES):
+        g.along(h, 0)
+
+    def along(*steps):
+        for step in steps:
+            for h in range(HALVES):
+                g.along(h, step)
+
+    def begin_far(h):
         for p in (1, 2):
             g.arrived(p, h, 1)
             g.ring_start(p, h)
-    g.gain_in(1)
-    g.gain_out(2)
 
     def far(step):
         for h in range(HALVES):
             for p in (1, 2):
                 g.ring_step(p, h, step)
 
+    begin_far(0)
+    along(1, 7)
+    begin_far(1)
+    along(2, 6)
+    g.gain_in(1)
+    g.gain_out(2)
+    along(3, 5, 4)
     for h in range(HALVES):
-        g.arrived(0, h, 1)
-        g.ring_start(0, h)
+        g.pass_on(0, h, at["x"])
     far(0)
     g.gain_in(2)
     g.gain_pass()
@@ -402,17 +438,9 @@
         cols = slice(t * 128, (t + 1) * 128)
         unit = hidden_ref[:, cols].astype(jnp.float32) * inv_rms * gain_row[:, cols]
         normed[:, cols] = unit.astype(jnp.bfloat16)
+    far(2)
     for h in range(HALVES):
-        g.ring_step(0, h, 0)
-    far(2)
-    for t in range(WIDTH // 128):
-        cols = slice(t * 128, (t + 1) * 128)
-        turned_own[cols, :] = normed[:, cols].T
-    for h in range(HALVES):
-        g.ring_step(0, h, 1)
-    far(3)
-    swap = remote(turned_own, turned_other, swap_sem.at[0, 0], swap_sem.at[1, 0], partner)
-    swap.start()
+        g.beside(h)
 
     def weight_rows(tiles, y):
         return jnp.concatenate([full[tile, y].reshape(512, HD) for tile in tiles], axis=1)
@@ -442,6 +470,12 @@
             kv_copy(j, peer).start()
 
     scale = HD ** (-0.5)
+    far(3)
+    for t in range(WIDTH // 128):
+        cols = slice(t * 128, (t + 1) * 128)
+        turned_own[cols, :] = normed[:, cols].T
+    swap = remote(turned_own, turned_other, swap_sem.at[0, 0], swap_sem.at[1, 0], partner)
+    swap.start()
     mix(g.mine[1:])
     g.passed(1)
     g.passed(2)
@@ -556,9 +590,15 @@
     back[4] = rotated(keys_grad, -1.0).astype(jnp.bfloat16)
     back[5] = values_grad.astype(jnp.bfloat16)
 
+    def both(step):
+        for h in range(HALVES):
+            for p in (1, 2):
+                s.ring_step(p, h, step)
+
     swap_last = swap_back(5 - core, 1, 2)
     swap_last.start()
     pairs = [jnp.concatenate([back[2 * pair], back[2 * pair + 1]], axis=1) for pair in range(3)]
+    both(0)
     swap_last.wait_recv()
     products((0,))
     s.ring_start(0)
@@ -573,12 +613,6 @@
 
     inner = jnp.zeros((128, 1), jnp.float32)
 
-    def both(step):
-        for h in range(HALVES):
-            for p in (1, 2):
-                s.ring_step(p, h, step)
-
-    both(0)
     for y in (0, 1, 2, 3):
         inner = plain_rows(y, inner)
     both(1)
@@ -637,9 +671,10 @@
     s.settled()
 
 
-def whole(hidden, tiles, gain_piece, cosine, sine, cot):
+def whole(hidden, tiles, gain_piece, tables, cot):
     dma = pltpu.SemaphoreType.DMA
     vmem = pl.BlockSpec(memory_space=pltpu.VMEM)
+    hbm = pl.BlockSpec(memory_space=pltpu.HBM)
     low, wide = jnp.bfloat16, jnp.float32
 
     def rings(p):
@@ -657,7 +692,7 @@
             jax.ShapeDtypeStruct((8, TILES * HD), wide),
             jax.ShapeDtypeStruct((1, 128), wide),
         ),
-        in_specs=[vmem] * 6,
+        in_specs=[hbm, vmem, vmem, hbm, hbm],
         out_specs=(vmem,) * 4,
         scratch_shapes=[
             pltpu.VMEM((TILES, 8, 4, 2, 4, 2, 8, HD), low),
@@ -681,11 +716,17 @@
             pltpu.VMEM((TILES, 8, HD), wide),
             pltpu.VMEM((TILES, 128, HD), wide),
             pltpu.VMEM((512, 8, HD), low),
+            pltpu.VMEM((128, WIDTH), low),
+            pltpu.VMEM((2, 128, HD), wide),
+            pltpu.VMEM((128, FLAT), low),
+            dma((3,)),
             dma((2,)),
             dma((7,)),
             dma((7,)),
+            dma((HALVES, 7)),
+            dma((HALVES, 3)),
             dma((3,)),
-            dma((3, 2, 4, HALVES)),
+            dma((2, 2, 4, HALVES)),
             dma((2, 3)),
             dma((2, 4)),
             dma((4,)),
@@ -700,15 +741,36 @@
         ],
         compiler_params=pltpu.CompilerParams(collective_id=0, has_side_effects=True, vmem_limit_bytes=40 * 2**20),
         name="whole",
-    )(hidden, tiles, gain_piece, cosine, sine, cot)
-
-
-def rope_tables(first_position):
-    freqs = rope_base ** (-jnp.arange(HD // 2, dtype=jnp.float32) / (HD // 2))
-    positions = first_position + jnp.arange(128, dtype=jnp.int32)
-    angles = positions.astype(jnp.float32)[:, None] * freqs[None, :]
-    cosine, sine = jnp.cos(angles), jnp.sin(angles)
-    return jnp.concatenate([cosine, cosine], axis=1), jnp.concatenate([-sine, sine], axis=1)
+    )(hidden, tiles, gain_piece, tables, cot)
+
+
+def rope_tables():
+    freqs = np.float32(rope_base) ** (-np.arange(HD // 2, dtype=np.float32) / np.float32(HD // 2))
+    angles = (np.arange(1024, dtype=np.float32)[:, None] * freqs.astype(np.float32)[None, :]).astype(np.float64)
+    cosine, sine = np.cos(angles), np.sin(angles)
+    both = np.stack([np.concatenate([cosine, cosine], axis=1), np.concatenate([-sine, sine], axis=1)])
+    return np.moveaxis(both.reshape(2, 8, 128, HD), 1, 0).astype(np.float32)
+
+
+def write_kernel(*refs):
+    sems = refs[-1]
+    copies = [pltpu.make_async_copy(refs[k], refs[3 + k], sems.at[k]) for k in range(3)]
+    for copy in copies:
+        copy.start()
+    for copy in copies:
+        copy.wait()
+
+
+def written(*arrays):
+    return pl.pallas_call(
+        write_kernel,
+        out_shape=tuple(jax.ShapeDtypeStruct(a.shape, a.dtype) for a in arrays),
+        in_specs=[pl.BlockSpec(memory_space=pltpu.VMEM)] * 3,
+        out_specs=(pl.BlockSpec(memory_space=pltpu.HBM),) * 3,
+        scratch_shapes=[pltpu.SemaphoreType.DMA((3,))],
+        compiler_params=pltpu.CompilerParams(vmem_limit_bytes=16 * 2**20),
+        name="written",
+    )(*arrays)
 
 
 def local(hidden_in, norm_gain, qkv_weight, attn_cotangent):
@@ -716,8 +778,10 @@
     tiles = jnp.moveaxis(qkv_weight.reshape(8, TILES, HD), 1, 0)
     lane = jnp.arange(128)
     gain_piece = jnp.where(lane // 8 == (i * 8 + j) % 16, jnp.tile(norm_gain.astype(jnp.float32), 16), 0.0)[None]
-    cosine, sine = rope_tables(j * 128)
-    attn, grad_in, weight_grad, gain_grad = whole(hidden_in[0], tiles, gain_piece, cosine, sine, attn_cotangent[0])
+    tables = jnp.asarray(rope_tables())
+    kept = [pltpu.with_memory_space_constraint(v, pltpu.HBM) for v in (hidden_in[0], attn_cotangent[0], tables)]
+    attn, grad_in, weight_grad, gain_grad = whole(kept[0], tiles, gain_piece, kept[2], kept[1])
+    attn, grad_in, weight_grad = written(attn, grad_in, weight_grad)
     return (attn[None], grad_in[None], weight_grad, gain_grad[0, :8])
 
 

time: 97.2 us -> 92.7 us (0.954)
  local copies, waits for them, and re-layouts: 5.48 us -> 1.24 us
    unnamed x11 -> x4, local copies, waits for them, and re-layouts: 4.88 us -> 0.64 us
    pallas_call x0 -> x1, Pallas kernels: none -> 1.04 us  [written(): pl.pallas_call(write_kernel, out_shape=tuple((jax.ShapeDtypeStruct(a.shap...]
where the time goes in v5:
time: 92.7 us; the launch traced here: 92.5 us
  Pallas kernels  90.6 us (98%)
  local copies, waits for them, and re-layouts  1.24 us (1%)
    pallas_call x1, Pallas kernels, whole(): pl.pallas_call(whole_kernel, out_shape=(jax.ShapeDtypeStruct((128, FLAT),...  89.5 us

profile of v5, /device:TPU:1, one launch (start us, length us, event | category | flops | bytes accessed | tf_op | source)
XLA Modules:
  0.0 92.5 jit_solution(4079587437588478398)
XLA Ops:
  0.6 0.0 copy-start.1
  0.7 0.0 copy-start
  0.7 0.6 copy-done.1
  1.3 0.1 tile.10
  1.4 0.0 copy-done
  1.4 89.5 %whole.1 = (bf16[128,512]{1,0:T(8,128)(2,1)S(1)}, bf16[128,4096]{1,0:T(8,128)(2,1)S(1)}, f32[8,768]{1,0:T(8,128)S(1)}, f32[1,128]{1,0:T(1,128)S(1)}) custom-call(bf16[128,4096]{1,0:T(8,128)(2,1)} %bitcast.10, bf16[6,8,128]{2,1,0:T(8,128)(2,1)S(1)} %bitcast.9, f32[1,128]{1,0:T(1,128)S(1)} %compare_select_fusion.gain_ref, ...), custom_call_target="tpu_custom_call" | custom-call | tf_op jit(solution)/shard_map/whole/pallas_call | solution.py:687
  90.9 1.0 %written.1 = (bf16[128,512]{1,0:T(8,128)(2,1)}, bf16[128,4096]{1,0:T(8,128)(2,1)}, f32[8,768]{1,0:T(8,128)}) custom-call(bf16[128,512]{1,0:T(8,128)(2,1)S(1)} %get-tuple-element.11.refs_0_, bf16[128,4096]{1,0:T(8,128)(2,1)S(1)} %get-tuple-element.12.refs_1_, f32[8,768]{1,0:T(8,128)S(1)} %get-tuple-element.13.refs_2_), custom_call_target="tpu_custom_call" | custom-call | tf_op jit(solution)/shard_map/written/pallas_call | solution.py:765
  92.0 0.5 slice_bitcast_fusion
  (2 shorter events, 0.0 us)
Async XLA Ops:
  0.6 0.7 copy-start.1
  0.7 0.8 copy-start

commit v6 on v5

--- a/solution.py
+++ b/solution.py
@@ -19,7 +19,6 @@
 )
 RINGS = ("x", "y", "z")
 HALVES = 2
-GAIN_ORDER = ("z", "y", "x")
 CHUNK = 256
 CHUNKS = 1024 // CHUNK
 BLOCKS = CHUNK // 128
@@ -53,11 +52,6 @@
 def slab(ref, tile, at, cores=slice(None)):
     y, high, x, low = indices(at)
     return ref.at[tile, y, high, cores, x, low]
-
-
-def gain_slab(ref, at, cores):
-    y, high, x, low = indices(at)
-    return ref.at[y, high, cores, x, low]
 
 
 def out_slab(ref, tile, at, cores=slice(None)):
@@ -101,9 +95,10 @@
 
 
 class Gather:
-    def __init__(self, at, core, mine_ref, gain_ref, full, gain_full, spare, sems):
+    def __init__(self, at, core, mine_ref, gain_ref, full, gain_pair, gain_near, gain_far, spare, sems):
         self.at, self.core, self.partner = at, core, device(at, 1 - core)
-        self.mine_ref, self.gain_ref, self.full, self.gain_full = mine_ref, gain_ref, full, gain_full
+        self.mine_ref, self.gain_ref, self.full = mine_ref, gain_ref, full
+        self.pair, self.near, self.far = gain_pair, gain_near, gain_far
         (self.swap, self.one, self.two, self.item, self.side, self.ring_out, self.ring, self.passing, self.gains, self.own) = sems
         self.mine, self.theirs = tiles_of(core), tiles_of(1 - core)
         sign = 1 - 2 * core
@@ -129,16 +124,17 @@
             owns.append(
                 pltpu.make_async_copy(self.mine_ref.at[self.mine[p]], slab(full, self.mine[p], at, core), self.own.at[p])
             )
-        owns.append(pltpu.make_async_copy(self.gain_ref, gain_slab(self.gain_full, at, core), self.own.at[3]))
+        self.go(remote(self.gain_ref, self.pair, self.gains.at[0, 0], self.gains.at[1, 0], self.partner))
         for own in owns:
             own.start()
         for own in owns:
             own.wait()
-        self.gain_out(0)
         settle(self.spare, 3, self.swap.at[1])
         for p in (1, 2, 0):
             for h in range(HALVES):
                 self.direct(p, h, 0)
+        self.gain_wait(0, 1)
+        self.near[0] = self.gain_ref[...] + self.pair[...]
 
     def direct(self, p, h, phase):
         order = ORDERS[p][h]
@@ -170,31 +166,34 @@
         each = 1 if phase == 0 else SIZES[order[0]]
         settle(self.spare, (SIZES[order[phase]] - 1) * each, sems.at[2 * p + h])
 
-    def gain_out(self, phase):
-        dim = GAIN_ORDER[phase]
-        src = gain_slab(self.gain_full, {d: self.at[d] for d in GAIN_ORDER[phase:]}, self.core)
-        for step in range(1, SIZES[dim]):
-            peer = device(moved(self.at, dim, step), self.core)
-            self.go(remote(src, src, self.gains.at[0, phase], self.gains.at[1, phase], peer))
-
     def gain_wait(self, phase, side):
-        rows = (
-            self.gain_full.at[pl.ds(0, 7), 0, 0, 0, 0],
-            self.gain_full.at[pl.ds(0, 7), :, :, 0, 0],
-            self.gain_full.at[pl.ds(0, 6), :, :, :, 0],
-            self.gain_full.at[:, :, 0],
-        )[phase]
+        rows = (self.pair, self.near.at[pl.ds(0, 7)], self.far.at[0, pl.ds(0, 3)], self.far.at[pl.ds(0, 7)])[phase]
         pltpu.make_async_copy(rows, rows, self.gains.at[side, phase]).wait()
 
-    def gain_in(self, phase):
-        self.gain_wait(phase, 1)
-
-    def gain_pass(self):
-        whole = gain_slab(self.gain_full, {}, self.core)
-        self.go(remote(whole, whole, self.gains.at[0, 3], self.gains.at[1, 3], self.partner))
-
-    def gain_passed(self):
-        self.gain_wait(3, 1)
+    def gain_group(self):
+        i, j = lax.axis_index("inter"), lax.axis_index("intra")
+        for step in range(1, 8):
+            self.go(
+                remote(
+                    self.near.at[0], self.near.at[step], self.gains.at[0, 1], self.gains.at[1, 1], (i, (j + step) % 8)
+                )
+            )
+
+    def gain_high(self):
+        at = self.at
+        self.gain_wait(1, 1)
+        self.far[at["y"], at["z"] // 2] = sum(self.near[k] for k in range(8))
+        here = self.far.at[at["y"], at["z"] // 2]
+        for step in (1, 3, 2):
+            peer = device(moved(at, "z", 2 * step), self.core)
+            self.go(remote(here, here, self.gains.at[0, 2], self.gains.at[1, 2], peer))
+
+    def gain_all(self):
+        self.gain_wait(2, 1)
+        here = self.far.at[self.at["y"]]
+        for step in range(1, 8):
+            peer = device(moved(self.at, "y", step), self.core)
+            self.go(remote(here, here, self.gains.at[0, 3], self.gains.at[1, 3], peer))
 
     def settled(self):
         settle(self.spare, 3, self.swap.at[0])
@@ -353,7 +352,7 @@
 def whole_kernel(
     hidden_in, mine_ref, gain_ref, tables_in, cot_in,
     attn_ref, grad_in_ref, weight_grad_ref, gain_grad_ref,
-    full, gain_full, gain_row, normed, turned_own, turned_other,
+    full, gain_pair, gain_near, gain_far, gain_row, normed, turned_own, turned_other,
     kv, probs, part_out, part_in, back, back_other, plain,
     part, ring_0, ring_1, ring_2, line_0, line_1, line_2, line_3, line_4, line_5, dot_in, final, total_ref, mixed, spare, hidden_ref, tables, cot_ref, load_sem,
     g_swap, g_one, g_two, g_item, g_side, g_out, g_ring, g_pass, g_gain, g_own,
@@ -385,21 +384,21 @@
     pl.semaphore_wait(barrier, count)
 
     g = Gather(
-        at, core, mine_ref, gain_ref, full, gain_full, spare,
+        at, core, mine_ref, gain_ref, full, gain_pair, gain_near, gain_far, spare,
         (g_swap, g_one, g_two, g_item, g_side, g_out, g_ring, g_pass, g_gain, g_own),
     )
     g.begin()
+    g.gain_group()
     for p in (1, 2):
         for h in range(HALVES):
             g.arrived(p, h, 0)
             g.direct(p, h, 1)
-    g.gain_in(0)
-    g.gain_out(1)
     for h in range(HALVES):
         g.arrived(0, h, 0)
         g.direct(0, h, 1)
     for h in range(HALVES):
         g.along(h, 0)
+    g.gain_high()
 
     def along(*steps):
         for step in steps:
@@ -420,27 +419,24 @@
     along(1, 7)
     begin_far(1)
     along(2, 6)
-    g.gain_in(1)
-    g.gain_out(2)
+    g.gain_all()
     along(3, 5, 4)
     for h in range(HALVES):
         g.pass_on(0, h, at["x"])
     far(0)
-    g.gain_in(2)
-    g.gain_pass()
     far(1)
-    g.gain_passed()
+    g.gain_wait(3, 1)
     for y in range(8):
         for z in range(4):
             t = y * 4 + z
-            gain_row[:, t * 128 : (t + 1) * 128] = jnp.sum(gain_full[y, z], axis=(0, 1, 2))
+            gain_row[:, t * 128 : (t + 1) * 128] = gain_far[y, z]
     for t in range(WIDTH // 128):
         cols = slice(t * 128, (t + 1) * 128)
         unit = hidden_ref[:, cols].astype(jnp.float32) * inv_rms * gain_row[:, cols]
         normed[:, cols] = unit.astype(jnp.bfloat16)
+    g.beside(0)
     far(2)
-    for h in range(HALVES):
-        g.beside(h)
+    g.beside(1)
 
     def weight_rows(tiles, y):
         return jnp.concatenate([full[tile, y].reshape(512, HD) for tile in tiles], axis=1)
@@ -573,6 +569,11 @@
     products((1, 2))
     s.ring_start(1)
     s.ring_start(2)
+    pairs = [jnp.concatenate([back[2 * pair], back[2 * pair + 1]], axis=1) for pair in range(2)]
+    for y in range(8):
+        plain[:, y * 512 : (y + 1) * 512] = sum(
+            across(pairs[pair], weight_rows((2 * pair, 2 * pair + 1), y), 1, 1) for pair in range(2)
+        )
     part_in[j] = part_out[j]
     keys_grad = jnp.zeros((128, HD), jnp.float32)
     values_grad = jnp.zeros((128, HD), jnp.float32)
@@ -597,7 +598,7 @@
 
     swap_last = swap_back(5 - core, 1, 2)
     swap_last.start()
-    pairs = [jnp.concatenate([back[2 * pair], back[2 * pair + 1]], axis=1) for pair in range(3)]
+    last_pair = jnp.concatenate([back[4], back[5]], axis=1)
     both(0)
     swap_last.wait_recv()
     products((0,))
@@ -606,27 +607,25 @@
 
     def plain_rows(y, inner):
         cols = slice(y * 512, (y + 1) * 512)
-        grad = sum(across(pairs[pair], weight_rows((2 * pair, 2 * pair + 1), y), 1, 1) for pair in range(3))
+        grad = plain[:, cols] + across(last_pair, weight_rows((4, 5), y), 1, 1)
         grad = grad * gain_row[:, cols]
         plain[:, cols] = grad
         return inner + jnp.sum(grad * hidden_ref[:, cols].astype(jnp.float32), axis=1, keepdims=True)
 
     inner = jnp.zeros((128, 1), jnp.float32)
 
-    for y in (0, 1, 2, 3):
+    for y in range(8):
         inner = plain_rows(y, inner)
     both(1)
-    s.ring_step(0, 0, 0)
-    for y in (4, 5, 6, 7):
-        inner = plain_rows(y, inner)
-    both(2)
-    s.ring_step(0, 1, 0)
     fall = inv_rms * inv_rms * inv_rms * (1.0 / WIDTH) * inner
     for y in range(8):
         cols = slice(y * 512, (y + 1) * 512)
         grad_in_ref[:, cols] = (
             plain[:, cols] * inv_rms - hidden_ref[:, cols].astype(jnp.float32) * fall
         ).astype(jnp.bfloat16)
+    s.ring_step(0, 0, 0)
+    both(2)
+    s.ring_step(0, 1, 0)
     s.ring_step(0, 0, 1)
     s.lines_out(0, 0)
     for h in range(HALVES):
@@ -652,7 +651,7 @@
         sums = sums + tile * full[(n, *inside)].astype(jnp.float32)
     lane = lax.broadcasted_iota(jnp.int32, (8, 128), 1)
     row = lax.broadcasted_iota(jnp.int32, (8, 128), 0)
-    gains = jnp.sum(jnp.where(lane % 8 == row, gain_full[inside], 0.0), axis=1, keepdims=True)
+    gains = jnp.sum(jnp.where(lane == (i % 16) * 8 + row, gain_far[j, i // 16], 0.0), axis=1, keepdims=True)
     answer = jnp.sum(sums, axis=1, keepdims=True) / gains
     gain_grad_ref[...] = jnp.sum(jnp.where(lane == row, answer, 0.0), axis=0, keepdims=True)
 
@@ -696,7 +695,9 @@
         out_specs=(vmem,) * 4,
         scratch_shapes=[
             pltpu.VMEM((TILES, 8, 4, 2, 4, 2, 8, HD), low),
-            pltpu.VMEM((8, 4, 2, 4, 2, 1, 128), wide),
+            pltpu.VMEM((1, 128), wide),
+            pltpu.VMEM((8, 1, 128), wide),
+            pltpu.VMEM((8, 4, 1, 128), wide),
             pltpu.VMEM((1, WIDTH), wide),
             pltpu.VMEM((128, WIDTH), low),
             pltpu.VMEM((WIDTH, 128), low),

time: 92.7 us -> 91.3 us (0.985)
  Pallas kernels: 90.6 us -> 89.2 us
    pallas_call x1, Pallas kernels: 89.5 us -> 88.1 us  [whole(): pl.pallas_call(whole_kernel, out_shape=(jax.ShapeDtypeStruct((128, FLAT),...]
where the time goes in v6:
time: 91.3 us; the launch traced here: 91.1 us
  Pallas kernels  89.2 us (98%)
  local copies, waits for them, and re-layouts  1.24 us (1%)
    pallas_call x1, Pallas kernels, whole(): pl.pallas_call(whole_kernel, out_shape=(jax.ShapeDtypeStruct((128, FLAT),...  88.1 us

profile of v6, /device:TPU:1, one launch (start us, length us, event | category | flops | bytes accessed | tf_op | source)
XLA Modules:
  0.0 91.1 jit_solution(9175674792351647102)
XLA Ops:
  0.6 0.0 copy-start.1
  0.7 0.0 copy-start
  0.7 0.6 copy-done.1
  1.3 0.1 tile.10
  1.4 0.0 copy-done
  1.4 88.1 %whole.1 = (bf16[128,512]{1,0:T(8,128)(2,1)S(1)}, bf16[128,4096]{1,0:T(8,128)(2,1)S(1)}, f32[8,768]{1,0:T(8,128)S(1)}, f32[1,128]{1,0:T(1,128)S(1)}) custom-call(bf16[128,4096]{1,0:T(8,128)(2,1)} %bitcast.10, bf16[6,8,128]{2,1,0:T(8,128)(2,1)S(1)} %bitcast.9, f32[1,128]{1,0:T(1,128)S(1)} %compare_select_fusion.gain_ref, ...), custom_call_target="tpu_custom_call" | custom-call | tf_op jit(solution)/shard_map/whole/pallas_call | solution.py:686
  89.6 1.0 %written.1 = (bf16[128,512]{1,0:T(8,128)(2,1)}, bf16[128,4096]{1,0:T(8,128)(2,1)}, f32[8,768]{1,0:T(8,128)}) custom-call(bf16[128,512]{1,0:T(8,128)(2,1)S(1)} %get-tuple-element.11.refs_0_, bf16[128,4096]{1,0:T(8,128)(2,1)S(1)} %get-tuple-element.12.refs_1_, f32[8,768]{1,0:T(8,128)S(1)} %get-tuple-element.13.refs_2_), custom_call_target="tpu_custom_call" | custom-call | tf_op jit(solution)/shard_map/written/pallas_call | solution.py:766
  90.6 0.5 slice_bitcast_fusion
  (2 shorter events, 0.0 us)
Async XLA Ops:
  0.6 0.7 copy-start.1
  0.7 0.8 copy-start

commit v7 on v6

--- a/solution.py
+++ b/solution.py
@@ -19,6 +19,7 @@
 )
 RINGS = ("x", "y", "z")
 HALVES = 2
+QUARTERS = 2
 CHUNK = 256
 CHUNKS = 1024 // CHUNK
 BLOCKS = CHUNK // 128
@@ -59,6 +60,26 @@
     return ref.at[tile, x, low, y, high, cores]
 
 
+def shares(dim, q):
+    if dim == "y":
+        return slice(None), slice(q * 2, q * 2 + 2)
+    return slice(q * 4, q * 4 + 4), slice(None)
+
+
+def ring_slab(ref, tile, dim, where, h, q):
+    y, high, x, low = indices({dim: where})
+    cut_y, cut_high = shares(dim, q)
+    y, high = (y, cut_high) if dim == "y" else (cut_y, high)
+    return ref.at[tile, y, high, h, x, low]
+
+
+def ring_out_slab(ref, tile, dim, where, h, q):
+    y, high, x, low = indices({dim: where})
+    cut_y, cut_high = shares(dim, q)
+    y, high = (y, cut_high) if dim == "y" else (cut_y, high)
+    return ref.at[tile, x, low, y, high, h]
+
+
 def remote(src, dst, send, recv, peer):
     return pltpu.make_async_remote_copy(
         src_ref=src, dst_ref=dst, send_sem=send, recv_sem=recv, device_id=peer, device_id_type=MESH
@@ -73,6 +94,10 @@
 
 def steps_of(p, way):
     return SIZES[RINGS[p]] // 2 - way
+
+
+def ring_sem(sems, p, way, step, h, q):
+    return sems.at[7 * p - 4 * (p > 0) + way * (2 if p == 0 else 4) + step, h, q]
 
 
 def tiles_of(core):
@@ -88,6 +113,8 @@
     peers = [device(at, 1 - core)]
     for dim, size in SIZES.items():
         peers += [device(moved(at, dim, step), core) for step in range(1, size)]
+        if dim != "x":
+            peers += [device(moved(at, dim, step), 1 - core) for step in range(1, size)]
     peers += [(i, (j + step) % 8) for step in range(1, 8)]
     for peer in peers:
         pl.semaphore_signal(barrier, inc=1, device_id=peer, device_id_type=MESH)
@@ -151,7 +178,7 @@
             settle(self.spare, 8, self.item.at[h, step - 1])
         known = moved({d: self.at[d] for d in (middle, "x")}, middle, -step)
         src = slab(self.full, self.mine[0], known, h)
-        for k in (1, 3, 2):
+        for k in (2, 1, 3):
             peer = device(moved(self.at, "x", k), self.core)
             self.go(remote(src, src, self.ring_out.at[0], self.side.at[h, k - 1], peer))
 
@@ -209,45 +236,47 @@
         dim = RINGS[p]
         return moved(self.at, dim, -self.ways[way] * step)[dim]
 
-    def hop(self, p, way, step, h):
+    def hop(self, p, way, step, h, q):
         dim = RINGS[p]
-        piece = slab(self.full, self.mine[p], {dim: self.where(p, way, step)}, h)
+        piece = ring_slab(self.full, self.mine[p], dim, self.where(p, way, step), h, q)
         peer = device(moved(self.at, dim, self.ways[way]), self.core)
-        self.go(remote(piece, piece, self.ring_out.at[p], self.ring.at[p - 1, way, step, h], peer))
+        self.go(remote(piece, piece, self.ring_out.at[p], self.ring.at[7 * (p - 1) + 4 * way + step, h, q], peer))
 
     def pass_on(self, p, h, where):
         piece = slab(self.full, self.mine[p], {RINGS[p]: where}, h)
         self.go(remote(piece, piece, self.passing.at[0, p], self.passing.at[1, p], self.partner))
 
     def ring_start(self, p, h):
-        for way in range(2):
-            self.hop(p, way, 0, h)
+        for q in range(QUARTERS):
+            for way in range(2):
+                self.hop(p, way, 0, h, q)
         self.pass_on(p, h, self.at[RINGS[p]])
 
-    def ring_step(self, p, h, step):
+    def ring_step(self, p, h, step, q):
         dim = RINGS[p]
         for way in range(2):
             if step >= steps_of(p, way):
                 continue
-            piece = slab(self.full, self.mine[p], {dim: self.where(p, way, step + 1)}, h)
-            remote(piece, piece, self.ring_out.at[p], self.ring.at[p - 1, way, step, h], self.partner).wait_recv()
+            piece = ring_slab(self.full, self.mine[p], dim, self.where(p, way, step + 1), h, q)
+            remote(piece, piece, self.ring_out.at[p], self.ring.at[7 * (p - 1) + 4 * way + step, h, q], self.partner).wait_recv()
             if step + 1 < steps_of(p, way):
-                self.hop(p, way, step + 1, h)
-            self.pass_on(p, h, self.where(p, way, step + 1))
+                self.hop(p, way, step + 1, h, q)
+            if q == QUARTERS - 1:
+                self.pass_on(p, h, self.where(p, way, step + 1))
 
     def passed(self, p):
         settle(self.spare, 512, self.passing.at[1, p])
 
 
-RING_SHAPES = {"x": (2, 8, 4, 8, HD), "y": (4, 2, 4, 8, HD), "z": (4, 8, 8, HD)}
+RING_SHAPES = {"x": (2, 4, 4, 8, HD), "y": (4, 2, 2, 8, HD), "z": (4, 4, 8, HD)}
 LINE_SHAPES = {"x": (4, 8, HD), "y": (8, 8, HD), "z": (2, 4, 8, HD)}
 
 
 class Scatter:
-    def __init__(self, at, core, part, rings, lines, dot_in, final, total_ref, spare, sems):
+    def __init__(self, at, core, part, rings, lines, dot_in, total_ref, spare, sems):
         self.at, self.core, self.partner = at, core, device(at, 1 - core)
         self.part, self.rings, self.lines, self.dot_in = part, rings, lines, dot_in
-        self.final, self.total_ref = final, total_ref
+        self.total_ref = total_ref
         self.ring_out, self.ring, self.two, self.three, self.last = sems
         sign = 1 - 2 * core
         self.ways = (sign, -sign)
@@ -258,33 +287,35 @@
 
     def target(self, p, way, left):
         dim = RINGS[p]
-        return {dim: moved(self.at, dim, self.ways[way] * left)[dim]}
-
-    def copy(self, p, way, step, h):
+        return moved(self.at, dim, self.ways[way] * left)[dim]
+
+    def copy(self, p, way, step, h, q):
         dim = RINGS[p]
         return remote(
-            out_slab(self.part, p, self.target(p, way, steps_of(p, way) - step), h),
-            self.rings[p].at[way, step, h],
+            ring_out_slab(self.part, p, dim, self.target(p, way, steps_of(p, way) - step), h, q),
+            self.rings[p].at[way, step, h, q],
             self.ring_out.at[p],
-            self.ring.at[p, way, step, h],
+            ring_sem(self.ring, p, way, step, h, q),
             device(moved(self.at, dim, self.ways[way]), self.core),
         )
 
     def ring_start(self, p):
         for h in range(HALVES):
-            for way in range(2):
-                self.go(self.copy(p, way, 0, h))
-
-    def ring_step(self, p, h, step):
+            for q in range(QUARTERS):
+                for way in range(2):
+                    self.go(self.copy(p, way, 0, h, q))
+
+    def ring_step(self, p, h, step, q):
         for way in range(2):
             if step >= steps_of(p, way):
                 continue
-            self.copy(p, way, step, h).wait_recv()
-            here = out_slab(self.part, p, self.target(p, way, steps_of(p, way) - step - 1), h)
-            there = self.rings[p].at[way, step, h]
+            self.copy(p, way, step, h, q).wait_recv()
+            dim = RINGS[p]
+            here = ring_out_slab(self.part, p, dim, self.target(p, way, steps_of(p, way) - step - 1), h, q)
+            there = self.rings[p].at[way, step, h, q]
             here[...] = (here[...].astype(jnp.float32) + there[...].astype(jnp.float32)).astype(jnp.bfloat16)
             if step + 1 < steps_of(p, way):
-                self.go(self.copy(p, way, step + 1, h))
+                self.go(self.copy(p, way, step + 1, h, q))
 
     def lines_out(self, p, h):
         a, b, c = ORDERS[p][h]
@@ -309,44 +340,40 @@
         for step in range(1, SIZES[b]):
             total = total + lines[step - 1].astype(jnp.float32)
         here[...] = total.astype(jnp.bfloat16)
+        tile = tiles_of(self.core)[p]
         for step in range(1, SIZES[a]):
             there = moved(self.at, a, step)
             self.go(
                 remote(
                     out_slab(self.part, p, there, h),
-                    self.dot_in.at[p, h, step - 1],
+                    self.dot_in.at[tile, step - 1],
                     self.three.at[6],
-                    self.three.at[2 * p + h],
-                    device(there, self.core),
+                    self.three.at[tile],
+                    device(there, h),
                 )
             )
-
-    def finish(self, p):
-        tile = tiles_of(self.core)[p]
-        for h in range(HALVES):
-            a = ORDERS[p][h][0]
-            here = out_slab(self.part, p, self.at, h)
-            total = here[...].astype(jnp.float32)
-            settle(self.spare, SIZES[a] - 1, self.three.at[2 * p + h])
-            for step in range(1, SIZES[a]):
-                total = total + self.dot_in[p, h, step - 1].astype(jnp.float32)
-            self.final[p, h] = total
-        self.total_ref[tile] = self.final[p, self.core]
-        self.go(
-            remote(
-                self.final.at[p, 1 - self.core], self.total_ref.at[tile], self.last.at[0], self.last.at[1], self.partner
-            )
-        )
-
-    def finished(self, side):
-        settle(self.spare, 6, self.last.at[side])
+        own = out_slab(self.part, p, self.at, h)
+
+        @pl.when(self.core == h)
+        def _():
+            self.dot_in[tile, 7] = own[...]
+
+        @pl.when(self.core != h)
+        def _():
+            self.go(remote(own, self.dot_in.at[tile, 7], self.three.at[6], self.last.at[p], self.partner))
+
+    def finish(self, p, mine):
+        tile = tiles_of(self.core if mine else 1 - self.core)[p]
+        settle(self.spare, 7, self.three.at[tile])
+        if not mine:
+            settle(self.spare, 1, self.last.at[p])
+        self.total_ref[tile] = sum(self.dot_in[tile, k].astype(jnp.float32) for k in range(8))
 
     def settled(self):
         for p in range(3):
             settle(self.spare, 384 if RINGS[p] == "x" else 448, self.ring_out.at[p])
         settle(self.spare, 208, self.two.at[6])
-        settle(self.spare, 42, self.three.at[6])
-        self.finished(0)
+        settle(self.spare, 45, self.three.at[6])
 
 
 def whole_kernel(
@@ -354,7 +381,7 @@
     attn_ref, grad_in_ref, weight_grad_ref, gain_grad_ref,
     full, gain_pair, gain_near, gain_far, gain_row, normed, turned_own, turned_other,
     kv, probs, part_out, part_in, back, back_other, plain,
-    part, ring_0, ring_1, ring_2, line_0, line_1, line_2, line_3, line_4, line_5, dot_in, final, total_ref, mixed, spare, hidden_ref, tables, cot_ref, load_sem,
+    part, ring_0, ring_1, ring_2, line_0, line_1, line_2, line_3, line_4, line_5, dot_in, total_ref, mixed, spare, hidden_ref, tables, cot_ref, load_sem,
     g_swap, g_one, g_two, g_item, g_side, g_out, g_ring, g_pass, g_gain, g_own,
     kv_sem, part_sem, swap_sem, s_out, s_ring, s_two, s_three, s_last,
 ):
@@ -412,8 +439,9 @@
 
     def far(step):
         for h in range(HALVES):
-            for p in (1, 2):
-                g.ring_step(p, h, step)
+            for q in range(QUARTERS):
+                for p in (1, 2):
+                    g.ring_step(p, h, step, q)
 
     begin_far(0)
     along(1, 7)
@@ -435,8 +463,8 @@
         unit = hidden_ref[:, cols].astype(jnp.float32) * inv_rms * gain_row[:, cols]
         normed[:, cols] = unit.astype(jnp.bfloat16)
     g.beside(0)
+    g.beside(1)
     far(2)
-    g.beside(1)
 
     def weight_rows(tiles, y):
         return jnp.concatenate([full[tile, y].reshape(512, HD) for tile in tiles], axis=1)
@@ -563,8 +591,7 @@
                 part[p, k // 2, k % 2] = sums[:, n * HD : (n + 1) * HD].reshape(8, 4, 2, 8, HD).astype(jnp.bfloat16)
 
     s = Scatter(
-        at, core, part, (ring_0, ring_1, ring_2), (line_0, line_1, line_2, line_3, line_4, line_5), dot_in, final,
-        total_ref, spare, (s_out, s_ring, s_two, s_three, s_last),
+        at, core, part, (ring_0, ring_1, ring_2), (line_0, line_1, line_2, line_3, line_4, line_5), dot_in, total_ref, spare, (s_out, s_ring, s_two, s_three, s_last),
     )
     products((1, 2))
     s.ring_start(1)
@@ -593,8 +620,9 @@
 
     def both(step):
         for h in range(HALVES):
-            for p in (1, 2):
-                s.ring_step(p, h, step)
+            for q in range(QUARTERS):
+                for p in (1, 2):
+                    s.ring_step(p, h, step, q)
 
     swap_last = swap_back(5 - core, 1, 2)
     swap_last.start()
@@ -623,26 +651,31 @@
         grad_in_ref[:, cols] = (
             plain[:, cols] * inv_rms - hidden_ref[:, cols].astype(jnp.float32) * fall
         ).astype(jnp.bfloat16)
-    s.ring_step(0, 0, 0)
+    def late(h, step):
+        for q in range(QUARTERS):
+            s.ring_step(0, h, step, q)
+
+    late(0, 0)
     both(2)
-    s.ring_step(0, 1, 0)
-    s.ring_step(0, 0, 1)
+    late(1, 0)
+    late(0, 1)
     s.lines_out(0, 0)
     for h in range(HALVES):
-        for p in (1, 2):
-            s.ring_step(p, h, 3)
-            s.lines_out(p, h)
-    s.ring_step(0, 1, 1)
+        for q in range(QUARTERS):
+            for p in (1, 2):
+                s.ring_step(p, h, 3, q)
+                if q == QUARTERS - 1:
+                    s.lines_out(p, h)
+    late(1, 1)
     s.lines_out(0, 1)
     for h in range(HALVES):
         for p in (1, 2):
             s.dots_out(p, h)
     for h in range(HALVES):
         s.dots_out(0, h)
-    s.finish(1)
-    s.finish(2)
-    s.finish(0)
-    s.finished(1)
+    for p in (1, 2, 0):
+        s.finish(p, True)
+        s.finish(p, False)
     inside = (j, i // 16, (i // 8) % 2, (i // 2) % 4, i % 2)
     sums = jnp.zeros((8, HD), jnp.float32)
     for n in range(TILES):
@@ -678,7 +711,7 @@
 
     def rings(p):
         dim = RINGS[p]
-        return pltpu.VMEM((2, SIZES[dim] // 2, HALVES, *RING_SHAPES[dim]), low)
+        return pltpu.VMEM((2, SIZES[dim] // 2, HALVES, QUARTERS, *RING_SHAPES[dim]), low)
 
     def lines(p, h):
         return pltpu.VMEM((SIZES[ORDERS[p][h][1]] - 1, *LINE_SHAPES[ORDERS[p][h][0]]), low)
@@ -712,8 +745,7 @@
             pltpu.VMEM((3, 4, 2, 8, 4, 2, 8, HD), low),
             *[rings(p) for p in range(3)],
             *[lines(p, h) for p in range(3) for h in range(HALVES)],
-            pltpu.VMEM((3, HALVES, 7, 8, HD), low),
-            pltpu.VMEM((3, 2, 8, HD), wide),
+            pltpu.VMEM((TILES, 8, 8, HD), low),
             pltpu.VMEM((TILES, 8, HD), wide),
             pltpu.VMEM((TILES, 128, HD), wide),
             pltpu.VMEM((512, 8, HD), low),
@@ -727,7 +759,7 @@
             dma((HALVES, 7)),
             dma((HALVES, 3)),
             dma((3,)),
-            dma((2, 2, 4, HALVES)),
+            dma((14, HALVES, QUARTERS)),
             dma((2, 3)),
             dma((2, 4)),
             dma((4,)),
@@ -735,10 +767,10 @@
             dma((2, 8)),
             dma((2, 4)),
             dma((3,)),
-            dma((3, 2, 4, HALVES)),
+            dma((17, HALVES, QUARTERS)),
             dma((7,)),
             dma((7,)),
-            dma((2,)),
+            dma((3,)),
         ],
         compiler_params=pltpu.CompilerParams(collective_id=0, has_side_effects=True, vmem_limit_bytes=40 * 2**20),
         name="whole",

time: 91.3 us -> 88.5 us (0.969)
  Pallas kernels: 89.2 us -> 86.4 us
    pallas_call x1, Pallas kernels: 88.1 us -> 85.3 us  [whole(): pl.pallas_call(whole_kernel, out_shape=(jax.ShapeDtypeStruct((128, FLAT),...]
where the time goes in v7:
time: 88.5 us; the launch traced here: 88.3 us
  Pallas kernels  86.4 us (98%)
  local copies, waits for them, and re-layouts  1.24 us (1%)
    pallas_call x1, Pallas kernels, whole(): pl.pallas_call(whole_kernel, out_shape=(jax.ShapeDtypeStruct((128, FLAT),...  85.3 us

profile of v7, /device:TPU:1, one launch (start us, length us, event | category | flops | bytes accessed | tf_op | source)
XLA Modules:
  0.0 88.3 jit_solution(6253344959637229011)
XLA Ops:
  0.6 0.0 copy-start.1
  0.7 0.0 copy-start
  0.7 0.6 copy-done.1
  1.3 0.1 tile.10
  1.4 0.0 copy-done
  1.4 85.3 %whole.1 = (bf16[128,512]{1,0:T(8,128)(2,1)S(1)}, bf16[128,4096]{1,0:T(8,128)(2,1)S(1)}, f32[8,768]{1,0:T(8,128)S(1)}, f32[1,128]{1,0:T(1,128)S(1)}) custom-call(bf16[128,4096]{1,0:T(8,128)(2,1)} %bitcast.10, bf16[6,8,128]{2,1,0:T(8,128)(2,1)S(1)} %bitcast.9, f32[1,128]{1,0:T(1,128)S(1)} %compare_select_fusion.gain_ref, ...), custom_call_target="tpu_custom_call" | custom-call | tf_op jit(solution)/shard_map/whole/pallas_call | solution.py:719
  86.8 1.0 %written.1 = (bf16[128,512]{1,0:T(8,128)(2,1)}, bf16[128,4096]{1,0:T(8,128)(2,1)}, f32[8,768]{1,0:T(8,128)}) custom-call(bf16[128,512]{1,0:T(8,128)(2,1)S(1)} %get-tuple-element.11.refs_0_, bf16[128,4096]{1,0:T(8,128)(2,1)S(1)} %get-tuple-element.12.refs_1_, f32[8,768]{1,0:T(8,128)S(1)} %get-tuple-element.13.refs_2_), custom_call_target="tpu_custom_call" | custom-call | tf_op jit(solution)/shard_map/written/pallas_call | solution.py:798
  87.8 0.5 slice_bitcast_fusion
  (2 shorter events, 0.0 us)
Async XLA Ops:
  0.6 0.7 copy-start.1
  0.7 0.8 copy-start

commit v8 on v7

--- a/solution.py
+++ b/solution.py
@@ -464,7 +464,6 @@
         normed[:, cols] = unit.astype(jnp.bfloat16)
     g.beside(0)
     g.beside(1)
-    far(2)
 
     def weight_rows(tiles, y):
         return jnp.concatenate([full[tile, y].reshape(512, HD) for tile in tiles], axis=1)
@@ -480,6 +479,11 @@
         return x * cosine + sign * (pltpu.roll(x, 64, 1) * sine)
 
     mix(g.mine[:1])
+
+    @pl.when(core == 1)
+    def _():
+        far(2)
+
     g.passed(0)
     mix(g.theirs[:1])
     kv[j, 0] = rotated(mixed[4], 1.0).astype(jnp.bfloat16)
@@ -488,12 +492,17 @@
     def kv_copy(owner, peer):
         return remote(kv.at[owner], kv.at[owner], kv_sem.at[0, peer], kv_sem.at[1, owner], (i, peer))
 
-    for peer in range(1, 8):
+    for peer in range(7, 0, -1):
         @pl.when(j < peer)
         def _():
             kv_copy(j, peer).start()
 
     scale = HD ** (-0.5)
+
+    @pl.when(core == 0)
+    def _():
+        far(2)
+
     far(3)
     for t in range(WIDTH // 128):
         cols = slice(t * 128, (t + 1) * 128)
@@ -618,8 +627,8 @@
     back[4] = rotated(keys_grad, -1.0).astype(jnp.bfloat16)
     back[5] = values_grad.astype(jnp.bfloat16)
 
-    def both(step):
-        for h in range(HALVES):
+    def both(step, halves=(0, 1)):
+        for h in halves:
             for q in range(QUARTERS):
                 for p in (1, 2):
                     s.ring_step(p, h, step, q)
@@ -627,10 +636,11 @@
     swap_last = swap_back(5 - core, 1, 2)
     swap_last.start()
     last_pair = jnp.concatenate([back[4], back[5]], axis=1)
-    both(0)
+    both(0, (0,))
     swap_last.wait_recv()
     products((0,))
     s.ring_start(0)
+    both(0, (1,))
     g.settled()
 
     def plain_rows(y, inner):

time: 88.5 us -> 88.5 us (level)
  no operation moved by 1% of the time
where the time goes in v8:
time: 88.5 us; the launch traced here: 88.3 us
  Pallas kernels  86.4 us (98%)
  local copies, waits for them, and re-layouts  1.24 us (1%)
    pallas_call x1, Pallas kernels, whole(): pl.pallas_call(whole_kernel, out_shape=(jax.ShapeDtypeStruct((128, FLAT),...  85.3 us

profile of v8, /device:TPU:1, one launch (start us, length us, event | category | flops | bytes accessed | tf_op | source)
XLA Modules:
  0.0 88.3 jit_solution(1828251041858617368)
XLA Ops:
  0.6 0.0 copy-start.1
  0.7 0.0 copy-start
  0.7 0.6 copy-done.1
  1.3 0.1 tile.10
  1.4 0.0 copy-done
  1.4 85.3 %whole.1 = (bf16[128,512]{1,0:T(8,128)(2,1)S(1)}, bf16[128,4096]{1,0:T(8,128)(2,1)S(1)}, f32[8,768]{1,0:T(8,128)S(1)}, f32[1,128]{1,0:T(1,128)S(1)}) custom-call(bf16[128,4096]{1,0:T(8,128)(2,1)} %bitcast.10, bf16[6,8,128]{2,1,0:T(8,128)(2,1)S(1)} %bitcast.9, f32[1,128]{1,0:T(1,128)S(1)} %compare_select_fusion.gain_ref, ...), custom_call_target="tpu_custom_call" | custom-call | tf_op jit(solution)/shard_map/whole/pallas_call | solution.py:729
  86.7 1.0 %written.1 = (bf16[128,512]{1,0:T(8,128)(2,1)}, bf16[128,4096]{1,0:T(8,128)(2,1)}, f32[8,768]{1,0:T(8,128)}) custom-call(bf16[128,512]{1,0:T(8,128)(2,1)S(1)} %get-tuple-element.11.refs_0_, bf16[128,4096]{1,0:T(8,128)(2,1)S(1)} %get-tuple-element.12.refs_1_, f32[8,768]{1,0:T(8,128)S(1)} %get-tuple-element.13.refs_2_), custom_call_target="tpu_custom_call" | custom-call | tf_op jit(solution)/shard_map/written/pallas_call | solution.py:808
  87.8 0.5 slice_bitcast_fusion
  (2 shorter events, 0.0 us)
Async XLA Ops:
  0.6 0.7 copy-start.1
  0.7 0.8 copy-start
